TPU v7x, 32 devices: a whole 2x2x4 slice. The times are simulated.
32 devices in a mesh: stream: 8 (over y, x, core), leaf: 4 (over z).
Axes of the slice: x: 2, y: 2, z: 4, core: 2. Of those that a mesh axis runs over, the one named last changes fastest.
Arguments:
- points_rhs: bfloat16 [2048, 32, 128], P(('stream', 'leaf')), may hold values from -6 to 6
- leaf_basis: bfloat16 [2048, 64, 128], P(('stream', 'leaf')), may hold values from -0.5 to 0.5
- transfer: bfloat16 [1024, 64, 128], P(('stream', 'leaf')), may hold values from -0.5 to 0.5
- leaf_coupling: bfloat16 [2048, 64, 256], P(('stream', 'leaf')), may hold values from -0.375 to 0.375
- parent_coupling: bfloat16 [1024, 64, 512], P(('stream', 'leaf')), may hold values from -0.25 to 0.25
- near_blocks: bfloat16 [2048, 3, 128, 128], P(('stream', 'leaf')), may hold values from -0.3125 to 0.3125
- near_offsets: int32 [2048, 3], P(('stream', 'leaf')), may hold values from -2 to 2, as said below
- coupling_offsets: int32 [2048, 4], P(('stream', 'leaf')), may hold values from -5 to 5, as said below
- parent_owner: int32 [1024, 8], P(('stream', 'leaf')), may hold values from 0 to 31, all different within a row; in each aligned block of 32 rows (0 to 31, 32 to 63, ...) at most 16 rows name the same one
- parent_local: int32 [1024, 8], P(('stream', 'leaf')), may hold values from 0 to 31
Outputs:
- product: bfloat16 [2048, 32, 128], P(('stream', 'leaf'))
Inputs may be any that keep to these rules, and one draw needn't show every extreme that they name: `near_offsets`: each row holds 3 different offsets; the first is 0. `coupling_offsets`: each row holds 4 different nonzero offsets, none of which stands in the same row of near_offsets. `parent_owner`: each row names 8 different blocks; the rows of one device name no block more than 16 times, and in every draw some block is named exactly 16 times by the rows of some device.
All inputs are finite; a program needn't handle non-finite values.
Results may differ from a plain program's by a relative error of at most 0.0053.
Values may be sent and summed in bfloat16 or wider, within the bound.
No kernel may reach another device: no remote copies, remote signals or barrier semaphores. Data moves between devices by JAX's collectives and lax.ppermute only.
A program may use at most 128 MiB of HBM per device.

v0:
```python
import functools

import jax
import jax.numpy as jnp
from jax import lax
from jax.experimental import pallas as pl
from jax.experimental.pallas import tpu as pltpu
from jax.sharding import PartitionSpec as P

AXES = ("stream", "leaf")
FAR = 5
NEAR = 2
F32 = jnp.float32
BF16 = jnp.bfloat16

LIMIT = 16 * 1024 * 1024


def dot_t(a, b):
    return lax.dot_general(a, b, (((1,), (1,)), ((), ())), preferred_element_type=F32)


def dot_n(a, b):
    return lax.dot_general(a, b, (((1,), (0,)), ((), ())), preferred_element_type=F32)


def in_hbm(x):
    return pltpu.with_memory_space_constraint(x, pltpu.HBM)


def left_half(rows, lanes):
    return lax.broadcasted_iota(jnp.int32, (rows, lanes), 1) < lanes // 2


def swap_halves(tile):
    half = tile.shape[1] // 2
    return jnp.concatenate([tile[:, half:], tile[:, :half]], axis=1)


def beside(tiles, mask):
    tops, bots = [], []
    for a, b in zip(tiles[::2], tiles[1::2]):
        tops.append(jnp.where(mask, a, swap_halves(b)))
        bots.append(jnp.where(mask, swap_halves(a), b))
    return jnp.concatenate([jnp.concatenate(tops, axis=1), jnp.concatenate(bots, axis=1)], axis=0)


def dense(doubled, mask):
    half = doubled.shape[0] // 2
    return jnp.where(mask, doubled[:half], doubled[half:]).astype(BF16)


def upward_kernel(par_ref, pts_ref, basis_ref, trans_ref, coeff_ref, pay_ref, side_ref, *, steps, parents):
    step = pl.program_id(0)
    pairs = trans_ref.shape[0]
    n = pts_ref.shape[1]
    wide = left_half(n, 128)
    mask = left_half(n // 2, 128)
    batch = 4
    for first in range(0, pairs, batch):
        own = range(first, first + batch)
        sums = []
        for leaf in range(2 * first, 2 * (first + batch)):
            b = basis_ref[leaf]
            sums.append(dot_t(pts_ref[leaf], jnp.concatenate([b, b], axis=0)))
        paired = [jnp.where(wide, sums[2 * q], sums[2 * q + 1]).astype(BF16) for q in range(batch)]
        ups = []
        for q, p in enumerate(own):
            t = trans_ref[p]
            ups.append(dot_t(paired[q], jnp.concatenate([t, t], axis=0)))
        for q, c in enumerate(sums):
            coeff_ref[2 * first + q] = dense(c, mask)
        for q, p in enumerate(own):
            pay_ref[step * pairs + p] = dense(ups[q], mask)

    def edge(ref, at, first):
        leaves = pts_ref.shape[0]
        lo = 0 if first else leaves - FAR
        for q in range(FAR):
            ref[at + q] = coeff_ref[lo + q]
        lo = 0 if first else leaves - NEAR
        for q in range(NEAR):
            x = pts_ref[lo + q]
            ref[at + FAR + 2 * q] = x[: n // 2]
            ref[at + FAR + 2 * q + 1] = x[n // 2 :]

    odd = par_ref[0] == 1

    @pl.when(step == 0)
    def _():
        @pl.when(odd)
        def _():
            edge(pay_ref, parents, True)

        @pl.when(jnp.logical_not(odd))
        def _():
            edge(side_ref, 0, True)

    @pl.when(step == steps - 1)
    def _():
        @pl.when(odd)
        def _():
            edge(side_ref, 0, False)

        @pl.when(jnp.logical_not(odd))
        def _():
            edge(pay_ref, parents, False)


def upward(par, points, basis, transfer):
    leaves, n, size = points.shape
    parents, rank, _ = transfer.shape
    steps = 4
    lc, pc = leaves // steps, parents // steps
    halo = FAR + 2 * NEAR
    tile = (n // 2, 2 * rank)
    return pl.pallas_call(
        functools.partial(upward_kernel, steps=steps, parents=parents),
        out_shape=(
            jax.ShapeDtypeStruct((leaves,) + tile, BF16),
            jax.ShapeDtypeStruct((parents + halo,) + tile, BF16),
            jax.ShapeDtypeStruct((halo,) + tile, BF16),
        ),
        grid_spec=pltpu.PrefetchScalarGridSpec(
            num_scalar_prefetch=1,
            grid=(steps,),
            in_specs=[
                pl.BlockSpec((lc, n, size), lambda i, s: (i, 0, 0)),
                pl.BlockSpec((lc, rank, size), lambda i, s: (i, 0, 0)),
                pl.BlockSpec((pc, rank, 2 * rank), lambda i, s: (i, 0, 0)),
            ],
            out_specs=[
                pl.BlockSpec((lc,) + tile, lambda i, s: (i, 0, 0)),
                pl.BlockSpec((parents + halo,) + tile, lambda i, s: (0, 0, 0)),
                pl.BlockSpec((halo,) + tile, lambda i, s: (0, 0, 0)),
            ],
        ),
        compiler_params=pltpu.CompilerParams(vmem_limit_bytes=LIMIT),
        name="upward",
    )(par, *[in_hbm(x) for x in (points, basis, transfer)])


def local_kernel(
    par_ref, noff_ref, coff_ref, pts_ref, coeff_ref, pay_ref, side_ref, near_ref, coup_ref,
    near_out, field_out, pts_pad, coeff_pad, *, parents
):
    step = pl.program_id(0)
    leaves = pts_ref.shape[0]
    n = pts_ref.shape[1]
    chunk = near_ref.shape[0]
    mask = left_half(n // 2, 128)
    wide = left_half(n, 128)

    @pl.when(step == 0)
    def _():
        pts_pad[NEAR : NEAR + leaves] = pts_ref[...]
        coeff_pad[FAR : FAR + leaves] = coeff_ref[...]

        def put(ref, at, low):
            co = 0 if low else leaves + FAR
            po = 0 if low else leaves + NEAR
            for q in range(FAR):
                coeff_pad[co + q] = ref[at + q]
            for q in range(NEAR):
                pts_pad[po + q, : n // 2] = ref[at + FAR + 2 * q]
                pts_pad[po + q, n // 2 :] = ref[at + FAR + 2 * q + 1]

        odd = par_ref[0] == 1

        @pl.when(odd)
        def _():
            put(pay_ref, parents, True)
            put(side_ref, 0, False)

        @pl.when(jnp.logical_not(odd))
        def _():
            put(side_ref, 0, True)
            put(pay_ref, parents, False)

    slots = near_ref.shape[1]
    far_slots = coff_ref.shape[0]
    batch = 4
    for first in range(0, chunk, batch):
        nears, fields = [], []
        for j in range(first, first + batch):
            c = step * chunk + j
            xs = [pts_pad[c + NEAR + noff_ref[k, c]] for k in range(slots)]
            ws = [near_ref[j, k] for k in range(slots)]
            nears.append(dot_t(jnp.concatenate(xs, axis=1), jnp.concatenate(ws, axis=1)))
            w = coup_ref[j]
            lhs = beside([coeff_pad[c + FAR + coff_ref[k, c]] for k in range(far_slots)], mask)
            fields.append(dot_t(lhs, jnp.concatenate([w, w], axis=0)))
        for q, j in enumerate(range(first, first + batch)):
            near_out[j] = nears[q]
        for q in range(0, batch, 2):
            field_out[(first + q) // 2] = jnp.where(wide, fields[q], fields[q + 1])


def local_terms(par, near_offsets, coupling_offsets, points, coeffs, payload, side, near_blocks, leaf_coupling):
    leaves, n, size = points.shape
    rank = leaf_coupling.shape[1]
    slots = near_blocks.shape[1]
    chunk = 8
    halo = side.shape[0]
    parents = payload.shape[0] - halo
    tile = side.shape[1:]
    whole = lambda i, *s: (0, 0, 0)
    return pl.pallas_call(
        functools.partial(local_kernel, parents=parents),
        out_shape=(
            jax.ShapeDtypeStruct((leaves, n, size), F32),
            jax.ShapeDtypeStruct((leaves // 2, n, 2 * rank), F32),
        ),
        grid_spec=pltpu.PrefetchScalarGridSpec(
            num_scalar_prefetch=3,
            grid=(leaves // chunk,),
            in_specs=[
                pl.BlockSpec(points.shape, whole),
                pl.BlockSpec(coeffs.shape, whole),
                pl.BlockSpec(payload.shape, whole),
                pl.BlockSpec(side.shape, whole),
                pl.BlockSpec((chunk, slots, size, size), lambda i, *s: (i, 0, 0, 0)),
                pl.BlockSpec((chunk,) + leaf_coupling.shape[1:], lambda i, *s: (i, 0, 0)),
            ],
            out_specs=[
                pl.BlockSpec((chunk, n, size), lambda i, *s: (i, 0, 0)),
                pl.BlockSpec((chunk // 2, n, 2 * rank), lambda i, *s: (i, 0, 0)),
            ],
            scratch_shapes=[
                pltpu.VMEM((leaves + 2 * NEAR, n, size), BF16),
                pltpu.VMEM((leaves + 2 * FAR,) + tile, BF16),
            ],
        ),
        compiler_params=pltpu.CompilerParams(vmem_limit_bytes=LIMIT),
        name="local_terms",
    )(
        par, near_offsets, coupling_offsets, points, coeffs, payload, side, in_hbm(near_blocks), in_hbm(leaf_coupling)
    )


def downward_kernel(
    me_ref, owner_ref, local_ref, table, coup_ref, trans_ref, basis_ref, near_ref, field_ref, out_ref
):
    parents = trans_ref.shape[0]
    n = near_ref.shape[1]
    size = near_ref.shape[2]
    slots = owner_ref.shape[0]
    mask = left_half(n // 2, 128)
    zero = jnp.zeros(basis_ref.shape[1:], BF16)
    me = me_ref[0]
    batch = 4

    def rows(step, carry):
        own = [step * batch + q for q in range(batch)]
        halves = []
        for p in own:
            tiles = [table[(owner_ref[k, p] ^ me) * parents + local_ref[k, p]] for k in range(slots)]
            halves.append(dot_t(beside(tiles, mask), coup_ref[p]).astype(BF16))
        totals = [
            (field_ref[p] + dot_n(half, trans_ref[p])).astype(BF16) for p, half in zip(own, halves)
        ]
        fars = []
        for p, total in zip(own, totals):
            spread = jnp.concatenate(
                [
                    jnp.concatenate([basis_ref[2 * p], zero], axis=1),
                    jnp.concatenate([zero, basis_ref[2 * p + 1]], axis=1),
                ],
                axis=0,
            )
            fars.append(dot_n(total, spread))
        outs = []
        for p, far in zip(own, fars):
            outs.append((far[:, :size] + near_ref[2 * p]).astype(BF16))
            outs.append((far[:, size:] + near_ref[2 * p + 1]).astype(BF16))
        for q, out in enumerate(outs):
            out_ref[2 * batch * step + q] = out
        return carry

    lax.fori_loop(0, parents // batch, rows, 0)


def downward(me, owner, local, table, coupling, transfer, basis, near, field):
    leaves, n, size = near.shape
    smem = pl.BlockSpec(memory_space=pltpu.SMEM)
    vmem = pl.BlockSpec(memory_space=pltpu.VMEM)
    big = [pltpu.with_memory_space_constraint(x, pltpu.VMEM) for x in (table, coupling, transfer, basis, near, field)]
    return pl.pallas_call(
        downward_kernel,
        out_shape=jax.ShapeDtypeStruct((leaves, n, size), BF16),
        in_specs=[smem] * 3 + [vmem] * 6,
        out_specs=vmem,
        compiler_params=pltpu.CompilerParams(vmem_limit_bytes=LIMIT),
        name="downward",
    )(me, owner, local, *big)


def on_device(
    points_rhs,
    leaf_basis,
    transfer,
    leaf_coupling,
    parent_coupling,
    near_blocks,
    near_offsets,
    coupling_offsets,
    parent_owner,
    parent_local,
):
    streams, leafs = lax.axis_size("stream"), lax.axis_size("leaf")
    devices = streams * leafs
    parents = transfer.shape[0]
    me = lax.axis_index(AXES).astype(jnp.int32)
    par = (me % 2).reshape(1)

    def swap(x, bits):
        return lax.ppermute(x, AXES, [(i, i ^ bits) for i in range(devices)])

    coeffs, payload, side = upward(par, points_rhs, leaf_basis, transfer)
    odd_pairs = [(i, i + 1) for i in range(1, devices - 1, 2)]
    side_in = lax.ppermute(side, AXES, odd_pairs + [(b, a) for a, b in odd_pairs])

    got = swap(payload, 1)
    groups = []
    group = jnp.concatenate([payload[:parents], got[:parents]], axis=0)
    groups.append((0, group))
    bit = 2
    while bit < leafs:
        whole = jnp.concatenate([g for _, g in groups], axis=0)
        groups.append((bit, swap(whole, bit)))
        bit *= 2

    pieces = {}
    for base, group in groups:
        have = {0: group}
        for s in range(2, streams, 2):
            low = s & -s
            high = 1 << (s.bit_length() - 1)
            if low == high:
                have[s] = swap(have[s ^ low], s * leafs)
            else:
                rows = group.shape[0] // 2
                have[s] = jnp.concatenate(
                    [swap(have[s ^ low][:rows], low * leafs), swap(have[s ^ high][rows:], high * leafs)],
                    axis=0,
                )
        for s in list(have):
            have[s ^ 1] = swap(have[s], leafs)
        for s, g in have.items():
            pieces[s * leafs + base] = g
    table = jnp.concatenate([pieces[k] for k in sorted(pieces)], axis=0)

    near, field = local_terms(
        par, near_offsets.T, coupling_offsets.T, points_rhs, coeffs, got, side_in, near_blocks, leaf_coupling
    )
    return downward(
        me.reshape(1), parent_owner.T, parent_local.T, table, parent_coupling, transfer, leaf_basis, near, field
    )


def solution(mesh):
    three = P(AXES, None, None)
    two = P(AXES, None)
    return jax.shard_map(
        on_device,
        mesh=mesh,
        in_specs=(three,) * 5 + (P(AXES, None, None, None),) + (two,) * 4,
        out_specs=three,
        check_vma=False,
    )
```

profile of v0, /device:TPU:17, one launch (start us, length us, event | category | flops | bytes accessed | tf_op | source)
XLA Modules:
  0.0 64.0 jit_solution(2337998005789425832)
XLA Ops:
  0.0 4.0 %upward.1 = (bf16[64,16,128]{2,1,0:T(8,128)(2,1)S(1)}, bf16[41,16,128]{2,1,0:T(8,128)(2,1)S(1)}, bf16[9,16,128]{2,1,0:T(8,128)(2,1)S(1)}) custom-call(s32[1]{0:T(128)} %bitcast.3.par_ref, bf16[64,32,128]{2,1,0:T(8,128)(2,1)} %pts_ref.3, bf16[64,64,128]{2,1,0:T(8,128)(2,1)} %basis_ref.3, bf16[32,64,128]{2,1,0:T(8,128)(2,1)} %trans_ref.3), custom_call_target="tpu_custom_call" | custom-call | tf_op jit(solution)/shard_map/upward/pallas_call | solution.py:117
  4.0 1.4 %collective-permute-start = (bf16[41,16,128]{2,1,0:T(8,128)(2,1)S(1)}, bf16[41,16,128]{2,1,0:T(8,128)(2,1)S(1)}, u32[]{:S(2)}, u32[]{:S(2)}) collective-permute-start(bf16[41,16,128]{2,1,0:T(8,128)(2,1)S(1)} %get-tuple-element.10), channel_id=1, source_target_pairs={{0,1},{1,0},{2,3},{3,2},{4,5},{5,4},{6,7},{7,6},{8,9},{9,8},{10,11... | collective-permute-start | bytes 503816 | tf_op jit(solution)/shard_map/ppermute | solution.py:317
  5.4 3.8 %collective-permute-done.pay_ref = bf16[41,16,128]{2,1,0:T(8,128)(2,1)S(1)} collective-permute-done((bf16[41,16,128]{2,1,0:T(8,128)(2,1)S(1)}, bf16[41,16,128]{2,1,0:T(8,128)(2,1)S(1)}, u32[]{:S(2)}, u32[]{:S(2)}) %collective-permute-start) | collective-permute-done | bytes 167968 | tf_op jit(solution)/shard_map/ppermute | solution.py:317
  9.3 1.3 %collective-permute-start.8 = (bf16[64,16,128]{2,1,0:T(8,128)(2,1)S(1)}, bf16[64,16,128]{2,1,0:T(8,128)(2,1)S(1)}, u32[]{:S(2)}, u32[]{:S(2)}) collective-permute-start(bf16[64,16,128]{2,1,0:T(8,128)(2,1)S(1)} %pad_maximum_fusion), channel_id=1, source_target_pairs={{0,16},{1,17},{2,18},{3,19},{4,20},{5,21},{6,22},{7,23},{8,24},{9,... | collective-permute-start | bytes 786440 | tf_op jit(solution)/shard_map/ppermute | solution.py:317
  10.6 1.2 %collective-permute-start.4 = (bf16[64,16,128]{2,1,0:T(8,128)(2,1)S(1)}, bf16[64,16,128]{2,1,0:T(8,128)(2,1)S(1)}, u32[]{:S(2)}, u32[]{:S(2)}) collective-permute-start(bf16[64,16,128]{2,1,0:T(8,128)(2,1)S(1)} %pad_maximum_fusion), channel_id=1, source_target_pairs={{0,8},{1,9},{2,10},{3,11},{4,12},{5,13},{6,14},{7,15},{8,0},{9,1},... | collective-permute-start | bytes 786440 | tf_op jit(solution)/shard_map/ppermute | solution.py:317
  11.8 0.1 collective-permute-start.1
  11.9 2.4 %collective-permute-start.2 = (bf16[64,16,128]{2,1,0:T(8,128)(2,1)S(1)}, bf16[64,16,128]{2,1,0:T(8,128)(2,1)S(1)}, u32[]{:S(2)}, u32[]{:S(2)}) collective-permute-start(bf16[64,16,128]{2,1,0:T(8,128)(2,1)S(1)} %pad_maximum_fusion), channel_id=1, source_target_pairs={{0,4},{1,5},{2,6},{3,7},{4,0},{5,1},{6,2},{7,3},{8,12},{9,13},{10,... | collective-permute-start | bytes 786440 | tf_op jit(solution)/shard_map/ppermute | solution.py:317
  14.3 4.3 %collective-permute-start.18 = (bf16[9,16,128]{2,1,0:T(8,128)(2,1)S(1)}, bf16[9,16,128]{2,1,0:T(8,128)(2,1)S(1)}, u32[]{:S(2)}, u32[]{:S(2)}) collective-permute-start(bf16[9,16,128]{2,1,0:T(8,128)(2,1)S(1)} %get-tuple-element.12), channel_id=1, source_target_pairs={{1,2},{3,4},{5,6},{7,8},{9,10},{11,12},{13,14},{15,16},{17,18},{19... | collective-permute-start | bytes 110600 | tf_op jit(solution)/shard_map/ppermute | solution.py:321
  18.6 9.2 %collective-permute-done.18.side_ref = bf16[9,16,128]{2,1,0:T(8,128)(2,1)S(1)} collective-permute-done((bf16[9,16,128]{2,1,0:T(8,128)(2,1)S(1)}, bf16[9,16,128]{2,1,0:T(8,128)(2,1)S(1)}, u32[]{:S(2)}, u32[]{:S(2)}) %collective-permute-start.18) | collective-permute-done | bytes 36896 | tf_op jit(solution)/shard_map/ppermute | solution.py:321
  27.8 0.0 copy-start.1
  27.8 1.0 %copy-done.1 = bf16[64,32,128]{2,1,0:T(8,128)(2,1)S(1)} copy-done((bf16[64,32,128]{2,1,0:T(8,128)(2,1)S(1)}, bf16[64,32,128]{2,1,0:T(8,128)(2,1)}, u32[]{:S(2)}) %copy-start.1) | copy-done | bytes 524312
  28.8 0.0 copy-start.6
  28.8 0.7 %copy-done.6 = s32[64,3]{0,1:T(4,128)S(1)} copy-done((s32[64,3]{0,1:T(4,128)S(1)}, s32[64,3]{0,1:T(4,128)}, u32[]{:S(2)}) %copy-start.6) | copy-done | bytes 792
  29.5 0.0 copy-start.7
  29.5 0.7 %copy-done.7 = s32[64,4]{0,1:T(4,128)S(1)} copy-done((s32[64,4]{0,1:T(4,128)S(1)}, s32[64,4]{0,1:T(4,128)}, u32[]{:S(2)}) %copy-start.7) | copy-done | bytes 1048
  30.2 8.4 %local_terms.1 = (f32[64,32,128]{2,1,0:T(8,128)S(1)}, f32[32,32,128]{2,1,0:T(8,128)S(1)}) custom-call(s32[1]{0:T(128)} %bitcast.3.par_ref, s32[3,64]{1,0:T(4,128)S(1)} %bitcast.8, s32[4,64]{1,0:T(4,128)S(1)} %bitcast.9, bf16[64,32,128]{2,1,0:T(8,128)(2,1)S(1)} %copy-done.1, bf16[64,16,128]{2,1,0:T(8,128)(2,1)S(1)} %get-tuple-element.11.coeff_ref, ...), custom_call_target="tpu_custom_call" | custom-call | tf_op jit(solution)/shard_map/local_terms/pallas_call | solution.py:208
  38.5 0.0 collective-permute-done.8
  38.6 0.7 %collective-permute-start.12 = (bf16[32,16,128]{2,1,0:T(8,128)(2,1)S(1)}, bf16[32,16,128]{2,1,0:T(8,128)(2,1)S(1)}, u32[]{:S(2)}, u32[]{:S(2)}) collective-permute-start(bf16[32,16,128]{2,1,0:T(8,128)(2,1)S(1)} %slice.25), channel_id=1, source_target_pairs={{0,8},{1,9},{2,10},{3,11},{4,12},{5,13},{6,14},{7,15},{8,0},{9,1},... | collective-permute-start | bytes 393224 | tf_op jit(solution)/shard_map/ppermute | solution.py:317
  39.3 0.0 collective-permute-done.4
  39.3 0.3 collective-permute-start.13
  39.6 0.0 collective-permute-done.1
  39.6 1.1 %collective-permute-start.3 = (bf16[64,16,128]{2,1,0:T(8,128)(2,1)S(1)}, bf16[64,16,128]{2,1,0:T(8,128)(2,1)S(1)}, u32[]{:S(2)}, u32[]{:S(2)}) collective-permute-start(bf16[64,16,128]{2,1,0:T(8,128)(2,1)S(1)} %collective-permute-done.1), channel_id=1, source_target_pairs={{0,4},{1,5},{2,6},{3,7},{4,0},{5,1},{6,2},{7,3},{8,12},{9,13},{10,... | collective-permute-start | bytes 786440 | tf_op jit(solution)/shard_map/ppermute | solution.py:317
  40.6 1.2 %collective-permute-start.5 = (bf16[64,16,128]{2,1,0:T(8,128)(2,1)S(1)}, bf16[64,16,128]{2,1,0:T(8,128)(2,1)S(1)}, u32[]{:S(2)}, u32[]{:S(2)}) collective-permute-start(bf16[64,16,128]{2,1,0:T(8,128)(2,1)S(1)} %collective-permute-done.1), channel_id=1, source_target_pairs={{0,8},{1,9},{2,10},{3,11},{4,12},{5,13},{6,14},{7,15},{8,0},{9,1},... | collective-permute-start | bytes 786440 | tf_op jit(solution)/shard_map/ppermute | solution.py:317
  41.8 0.0 collective-permute-done.2
  41.9 0.8 %collective-permute-start.9 = (bf16[64,16,128]{2,1,0:T(8,128)(2,1)S(1)}, bf16[64,16,128]{2,1,0:T(8,128)(2,1)S(1)}, u32[]{:S(2)}, u32[]{:S(2)}) collective-permute-start(bf16[64,16,128]{2,1,0:T(8,128)(2,1)S(1)} %collective-permute-done.1), channel_id=1, source_target_pairs={{0,16},{1,17},{2,18},{3,19},{4,20},{5,21},{6,22},{7,23},{8,24},{9,... | collective-permute-start | bytes 786440 | tf_op jit(solution)/shard_map/ppermute | solution.py:317
  42.8 0.0 copy-start
  42.8 0.0 copy-start.2
  42.8 0.0 copy-start.3
  42.8 0.0 copy-start.4
  42.8 0.0 copy-start.5
  42.8 0.4 collective-permute-done.12
  43.2 2.1 %collective-permute-start.6 = (bf16[64,16,128]{2,1,0:T(8,128)(2,1)S(1)}, bf16[64,16,128]{2,1,0:T(8,128)(2,1)S(1)}, u32[]{:S(2)}, u32[]{:S(2)}) collective-permute-start(bf16[64,16,128]{2,1,0:T(8,128)(2,1)S(1)} %collective-permute-done.4), channel_id=1, source_target_pairs={{0,4},{1,5},{2,6},{3,7},{4,0},{5,1},{6,2},{7,3},{8,12},{9,13},{10,... | collective-permute-start | bytes 786440 | tf_op jit(solution)/shard_map/ppermute | solution.py:317
  45.3 0.0 collective-permute-done.13
  45.3 0.2 collective-permute-start.10
  45.6 4.5 %collective-permute-done.9 = bf16[64,16,128]{2,1,0:T(8,128)(2,1)S(1)} collective-permute-done((bf16[64,16,128]{2,1,0:T(8,128)(2,1)S(1)}, bf16[64,16,128]{2,1,0:T(8,128)(2,1)S(1)}, u32[]{:S(2)}, u32[]{:S(2)}) %collective-permute-start.9) | collective-permute-done | bytes 262176 | tf_op jit(solution)/shard_map/ppermute | solution.py:317
  50.1 0.4 collective-permute-start.14
  50.5 0.0 collective-permute-done.5
  50.5 1.1 %collective-permute-start.15 = (bf16[32,16,128]{2,1,0:T(8,128)(2,1)S(1)}, bf16[32,16,128]{2,1,0:T(8,128)(2,1)S(1)}, u32[]{:S(2)}, u32[]{:S(2)}) collective-permute-start(bf16[32,16,128]{2,1,0:T(8,128)(2,1)S(1)} %slice.28), channel_id=1, source_target_pairs={{0,16},{1,17},{2,18},{3,19},{4,20},{5,21},{6,22},{7,23},{8,24},{9,... | collective-permute-start | bytes 393224 | tf_op jit(solution)/shard_map/ppermute | solution.py:317
  51.6 0.0 collective-permute-done.3
  51.6 1.4 %collective-permute-start.7 = (bf16[64,16,128]{2,1,0:T(8,128)(2,1)S(1)}, bf16[64,16,128]{2,1,0:T(8,128)(2,1)S(1)}, u32[]{:S(2)}, u32[]{:S(2)}) collective-permute-start(bf16[64,16,128]{2,1,0:T(8,128)(2,1)S(1)} %collective-permute-done.5), channel_id=1, source_target_pairs={{0,4},{1,5},{2,6},{3,7},{4,0},{5,1},{6,2},{7,3},{8,12},{9,13},{10,... | collective-permute-start | bytes 786440 | tf_op jit(solution)/shard_map/ppermute | solution.py:317
  53.2 0.0 collective-permute-done.6
  53.2 0.1 collective-permute-start.16
  53.3 1.0 %collective-permute-done.14 = bf16[32,16,128]{2,1,0:T(8,128)(2,1)S(1)} collective-permute-done((bf16[32,16,128]{2,1,0:T(8,128)(2,1)S(1)}, bf16[32,16,128]{2,1,0:T(8,128)(2,1)S(1)}, u32[]{:S(2)}, u32[]{:S(2)}) %collective-permute-start.14) | collective-permute-done | bytes 131104 | tf_op jit(solution)/shard_map/ppermute | solution.py:317
  54.3 1.7 %collective-permute-start.11 = (bf16[64,16,128]{2,1,0:T(8,128)(2,1)S(1)}, bf16[64,16,128]{2,1,0:T(8,128)(2,1)S(1)}, u32[]{:S(2)}, u32[]{:S(2)}) collective-permute-start(bf16[64,16,128]{2,1,0:T(8,128)(2,1)S(1)} %collective-permute-done.9), channel_id=1, source_target_pairs={{0,4},{1,5},{2,6},{3,7},{4,0},{5,1},{6,2},{7,3},{8,12},{9,13},{10,... | collective-permute-start | bytes 786440 | tf_op jit(solution)/shard_map/ppermute | solution.py:317
  56.0 0.0 collective-permute-done.15
  56.1 1.1 %collective-permute-start.17 = (bf16[64,16,128]{2,1,0:T(8,128)(2,1)S(1)}, bf16[64,16,128]{2,1,0:T(8,128)(2,1)S(1)}, u32[]{:S(2)}, u32[]{:S(2)}) collective-permute-start(bf16[64,16,128]{2,1,0:T(8,128)(2,1)S(1)} %pad_maximum_fusion.2), channel_id=1, source_target_pairs={{0,4},{1,5},{2,6},{3,7},{4,0},{5,1},{6,2},{7,3},{8,12},{9,13},{10,... | collective-permute-start | bytes 786440 | tf_op jit(solution)/shard_map/ppermute | solution.py:317
  57.2 0.0 collective-permute-done.7
  57.3 0.0 collective-permute-done.10
  57.4 0.0 collective-permute-done.11
  57.6 0.0 collective-permute-done.16
  57.6 0.8 %collective-permute-done.17 = bf16[64,16,128]{2,1,0:T(8,128)(2,1)S(1)} collective-permute-done((bf16[64,16,128]{2,1,0:T(8,128)(2,1)S(1)}, bf16[64,16,128]{2,1,0:T(8,128)(2,1)S(1)}, u32[]{:S(2)}, u32[]{:S(2)}) %collective-permute-start.17) | collective-permute-done | bytes 262176 | tf_op jit(solution)/shard_map/ppermute | solution.py:317
  58.4 0.0 copy-done
  58.4 0.0 copy-done.2
  58.4 0.0 copy-done.3
  58.4 0.0 copy-done.4
  58.4 0.0 copy-done.5
  58.5 5.5 %downward.1 = bf16[64,32,128]{2,1,0:T(8,128)(2,1)} custom-call(s32[1]{0:T(128)} %bitcast.me_ref, s32[8,32]{1,0:T(8,128)S(1)} %bitcast.6, s32[8,32]{1,0:T(8,128)S(1)} %bitcast.7, bf16[1024,16,128]{2,1,0:T(8,128)(2,1)S(1)} %constant_dynamic-update-slice_fusion.table, bf16[32,64,512]{2,1,0:T(8,128)(2,1)S(1)} %copy-done.3, bf16[32,64,128]{2,1,0:T(8,128)(2,1)S(1)} %copy-done.2, ...), custom_call_target="tpu_custom_call" | custom-call | tf_op jit(solution)/shard_map/downward/pallas_call | solution.py:288
  (26 shorter events, 0.7 us)
Async XLA Ops:
  4.0 5.2 %collective-permute-start = (bf16[41,16,128]{2,1,0:T(8,128)(2,1)S(1)}, bf16[41,16,128]{2,1,0:T(8,128)(2,1)S(1)}, u32[]{:S(2)}, u32[]{:S(2)}) collective-permute-start(bf16[41,16,128]{2,1,0:T(8,128)(2,1)S(1)} %get-tuple-element.10), channel_id=1, source_target_pairs={{0,1},{1,0},{2,3},{3,2},{4,5},{5,4},{6,7},{7,6},{8,9},{9,8},{10,11... | collective-permute-start | bytes 503816 | tf_op jit(solution)/shard_map/ppermute | solution.py:317
  9.3 29.2 %collective-permute-start.8 = (bf16[64,16,128]{2,1,0:T(8,128)(2,1)S(1)}, bf16[64,16,128]{2,1,0:T(8,128)(2,1)S(1)}, u32[]{:S(2)}, u32[]{:S(2)}) collective-permute-start(bf16[64,16,128]{2,1,0:T(8,128)(2,1)S(1)} %pad_maximum_fusion), channel_id=1, source_target_pairs={{0,16},{1,17},{2,18},{3,19},{4,20},{5,21},{6,22},{7,23},{8,24},{9,... | collective-permute-start | bytes 786440 | tf_op jit(solution)/shard_map/ppermute | solution.py:317
  10.6 28.7 %collective-permute-start.4 = (bf16[64,16,128]{2,1,0:T(8,128)(2,1)S(1)}, bf16[64,16,128]{2,1,0:T(8,128)(2,1)S(1)}, u32[]{:S(2)}, u32[]{:S(2)}) collective-permute-start(bf16[64,16,128]{2,1,0:T(8,128)(2,1)S(1)} %pad_maximum_fusion), channel_id=1, source_target_pairs={{0,8},{1,9},{2,10},{3,11},{4,12},{5,13},{6,14},{7,15},{8,0},{9,1},... | collective-permute-start | bytes 786440 | tf_op jit(solution)/shard_map/ppermute | solution.py:317
  11.8 27.8 %collective-permute-start.1 = (bf16[64,16,128]{2,1,0:T(8,128)(2,1)S(1)}, bf16[64,16,128]{2,1,0:T(8,128)(2,1)S(1)}, u32[]{:S(2)}, u32[]{:S(2)}) collective-permute-start(bf16[64,16,128]{2,1,0:T(8,128)(2,1)S(1)} %pad_maximum_fusion), channel_id=1, source_target_pairs={{0,2},{1,3},{2,0},{3,1},{4,6},{5,7},{6,4},{7,5},{8,10},{9,11},{10,... | collective-permute-start | bytes 786440 | tf_op jit(solution)/shard_map/ppermute | solution.py:317
  11.9 30.0 %collective-permute-start.2 = (bf16[64,16,128]{2,1,0:T(8,128)(2,1)S(1)}, bf16[64,16,128]{2,1,0:T(8,128)(2,1)S(1)}, u32[]{:S(2)}, u32[]{:S(2)}) collective-permute-start(bf16[64,16,128]{2,1,0:T(8,128)(2,1)S(1)} %pad_maximum_fusion), channel_id=1, source_target_pairs={{0,4},{1,5},{2,6},{3,7},{4,0},{5,1},{6,2},{7,3},{8,12},{9,13},{10,... | collective-permute-start | bytes 786440 | tf_op jit(solution)/shard_map/ppermute | solution.py:317
  14.3 13.5 %collective-permute-start.18 = (bf16[9,16,128]{2,1,0:T(8,128)(2,1)S(1)}, bf16[9,16,128]{2,1,0:T(8,128)(2,1)S(1)}, u32[]{:S(2)}, u32[]{:S(2)}) collective-permute-start(bf16[9,16,128]{2,1,0:T(8,128)(2,1)S(1)} %get-tuple-element.12), channel_id=1, source_target_pairs={{1,2},{3,4},{5,6},{7,8},{9,10},{11,12},{13,14},{15,16},{17,18},{19... | collective-permute-start | bytes 110600 | tf_op jit(solution)/shard_map/ppermute | solution.py:321
  27.8 1.0 %copy-start.1 = (bf16[64,32,128]{2,1,0:T(8,128)(2,1)S(1)}, bf16[64,32,128]{2,1,0:T(8,128)(2,1)}, u32[]{:S(2)}) copy-start(bf16[64,32,128]{2,1,0:T(8,128)(2,1)} %pts_ref.3) | copy-start | bytes 1572868
  28.8 0.7 %copy-start.6 = (s32[64,3]{0,1:T(4,128)S(1)}, s32[64,3]{0,1:T(4,128)}, u32[]{:S(2)}) copy-start(s32[64,3]{0,1:T(4,128)} %param.16) | copy-start | bytes 2308
  29.5 0.7 %copy-start.7 = (s32[64,4]{0,1:T(4,128)S(1)}, s32[64,4]{0,1:T(4,128)}, u32[]{:S(2)}) copy-start(s32[64,4]{0,1:T(4,128)} %param.17) | copy-start | bytes 3076
  38.6 4.6 %collective-permute-start.12 = (bf16[32,16,128]{2,1,0:T(8,128)(2,1)S(1)}, bf16[32,16,128]{2,1,0:T(8,128)(2,1)S(1)}, u32[]{:S(2)}, u32[]{:S(2)}) collective-permute-start(bf16[32,16,128]{2,1,0:T(8,128)(2,1)S(1)} %slice.25), channel_id=1, source_target_pairs={{0,8},{1,9},{2,10},{3,11},{4,12},{5,13},{6,14},{7,15},{8,0},{9,1},... | collective-permute-start | bytes 393224 | tf_op jit(solution)/shard_map/ppermute | solution.py:317
  39.3 6.0 %collective-permute-start.13 = (bf16[32,16,128]{2,1,0:T(8,128)(2,1)S(1)}, bf16[32,16,128]{2,1,0:T(8,128)(2,1)S(1)}, u32[]{:S(2)}, u32[]{:S(2)}) collective-permute-start(bf16[32,16,128]{2,1,0:T(8,128)(2,1)S(1)} %slice.26), channel_id=1, source_target_pairs={{0,16},{1,17},{2,18},{3,19},{4,20},{5,21},{6,22},{7,23},{8,24},{9,... | collective-permute-start | bytes 393224 | tf_op jit(solution)/shard_map/ppermute | solution.py:317
  39.6 12.0 %collective-permute-start.3 = (bf16[64,16,128]{2,1,0:T(8,128)(2,1)S(1)}, bf16[64,16,128]{2,1,0:T(8,128)(2,1)S(1)}, u32[]{:S(2)}, u32[]{:S(2)}) collective-permute-start(bf16[64,16,128]{2,1,0:T(8,128)(2,1)S(1)} %collective-permute-done.1), channel_id=1, source_target_pairs={{0,4},{1,5},{2,6},{3,7},{4,0},{5,1},{6,2},{7,3},{8,12},{9,13},{10,... | collective-permute-start | bytes 786440 | tf_op jit(solution)/shard_map/ppermute | solution.py:317
  40.6 9.9 %collective-permute-start.5 = (bf16[64,16,128]{2,1,0:T(8,128)(2,1)S(1)}, bf16[64,16,128]{2,1,0:T(8,128)(2,1)S(1)}, u32[]{:S(2)}, u32[]{:S(2)}) collective-permute-start(bf16[64,16,128]{2,1,0:T(8,128)(2,1)S(1)} %collective-permute-done.1), channel_id=1, source_target_pairs={{0,8},{1,9},{2,10},{3,11},{4,12},{5,13},{6,14},{7,15},{8,0},{9,1},... | collective-permute-start | bytes 786440 | tf_op jit(solution)/shard_map/ppermute | solution.py:317
  41.9 8.2 %collective-permute-start.9 = (bf16[64,16,128]{2,1,0:T(8,128)(2,1)S(1)}, bf16[64,16,128]{2,1,0:T(8,128)(2,1)S(1)}, u32[]{:S(2)}, u32[]{:S(2)}) collective-permute-start(bf16[64,16,128]{2,1,0:T(8,128)(2,1)S(1)} %collective-permute-done.1), channel_id=1, source_target_pairs={{0,16},{1,17},{2,18},{3,19},{4,20},{5,21},{6,22},{7,23},{8,24},{9,... | collective-permute-start | bytes 786440 | tf_op jit(solution)/shard_map/ppermute | solution.py:317
  42.8 15.6 %copy-start = (bf16[64,64,128]{2,1,0:T(8,128)(2,1)S(1)}, bf16[64,64,128]{2,1,0:T(8,128)(2,1)}, u32[]{:S(2)}) copy-start(bf16[64,64,128]{2,1,0:T(8,128)(2,1)} %basis_ref.3) | copy-start | bytes 3145732
  42.8 15.6 %copy-start.2 = (bf16[32,64,128]{2,1,0:T(8,128)(2,1)S(1)}, bf16[32,64,128]{2,1,0:T(8,128)(2,1)}, u32[]{:S(2)}) copy-start(bf16[32,64,128]{2,1,0:T(8,128)(2,1)} %trans_ref.3) | copy-start | bytes 1572868
  42.8 15.6 %copy-start.3 = (bf16[32,64,512]{2,1,0:T(8,128)(2,1)S(1)}, bf16[32,64,512]{2,1,0:T(8,128)(2,1)}, u32[]{:S(2)}) copy-start(bf16[32,64,512]{2,1,0:T(8,128)(2,1)} %coup_ref.3) | copy-start | bytes 6291460
  42.8 15.6 %copy-start.4 = (s32[32,8]{0,1:T(8,128)S(1)}, s32[32,8]{0,1:T(8,128)}, u32[]{:S(2)}) copy-start(s32[32,8]{0,1:T(8,128)} %param.18) | copy-start | bytes 3076
  42.8 15.6 %copy-start.5 = (s32[32,8]{0,1:T(8,128)S(1)}, s32[32,8]{0,1:T(8,128)}, u32[]{:S(2)}) copy-start(s32[32,8]{0,1:T(8,128)} %param.19) | copy-start | bytes 3076
  43.2 10.0 %collective-permute-start.6 = (bf16[64,16,128]{2,1,0:T(8,128)(2,1)S(1)}, bf16[64,16,128]{2,1,0:T(8,128)(2,1)S(1)}, u32[]{:S(2)}, u32[]{:S(2)}) collective-permute-start(bf16[64,16,128]{2,1,0:T(8,128)(2,1)S(1)} %collective-permute-done.4), channel_id=1, source_target_pairs={{0,4},{1,5},{2,6},{3,7},{4,0},{5,1},{6,2},{7,3},{8,12},{9,13},{10,... | collective-permute-start | bytes 786440 | tf_op jit(solution)/shard_map/ppermute | solution.py:317
  45.3 12.0 %collective-permute-start.10 = (bf16[64,16,128]{2,1,0:T(8,128)(2,1)S(1)}, bf16[64,16,128]{2,1,0:T(8,128)(2,1)S(1)}, u32[]{:S(2)}, u32[]{:S(2)}) collective-permute-start(bf16[64,16,128]{2,1,0:T(8,128)(2,1)S(1)} %collective-permute-done.8), channel_id=1, source_target_pairs={{0,4},{1,5},{2,6},{3,7},{4,0},{5,1},{6,2},{7,3},{8,12},{9,13},{10,... | collective-permute-start | bytes 786440 | tf_op jit(solution)/shard_map/ppermute | solution.py:317
  50.1 4.3 %collective-permute-start.14 = (bf16[32,16,128]{2,1,0:T(8,128)(2,1)S(1)}, bf16[32,16,128]{2,1,0:T(8,128)(2,1)S(1)}, u32[]{:S(2)}, u32[]{:S(2)}) collective-permute-start(bf16[32,16,128]{2,1,0:T(8,128)(2,1)S(1)} %slice.27), channel_id=1, source_target_pairs={{0,8},{1,9},{2,10},{3,11},{4,12},{5,13},{6,14},{7,15},{8,0},{9,1},... | collective-permute-start | bytes 393224 | tf_op jit(solution)/shard_map/ppermute | solution.py:317
  50.5 5.5 %collective-permute-start.15 = (bf16[32,16,128]{2,1,0:T(8,128)(2,1)S(1)}, bf16[32,16,128]{2,1,0:T(8,128)(2,1)S(1)}, u32[]{:S(2)}, u32[]{:S(2)}) collective-permute-start(bf16[32,16,128]{2,1,0:T(8,128)(2,1)S(1)} %slice.28), channel_id=1, source_target_pairs={{0,16},{1,17},{2,18},{3,19},{4,20},{5,21},{6,22},{7,23},{8,24},{9,... | collective-permute-start | bytes 393224 | tf_op jit(solution)/shard_map/ppermute | solution.py:317
  51.6 5.6 %collective-permute-start.7 = (bf16[64,16,128]{2,1,0:T(8,128)(2,1)S(1)}, bf16[64,16,128]{2,1,0:T(8,128)(2,1)S(1)}, u32[]{:S(2)}, u32[]{:S(2)}) collective-permute-start(bf16[64,16,128]{2,1,0:T(8,128)(2,1)S(1)} %collective-permute-done.5), channel_id=1, source_target_pairs={{0,4},{1,5},{2,6},{3,7},{4,0},{5,1},{6,2},{7,3},{8,12},{9,13},{10,... | collective-permute-start | bytes 786440 | tf_op jit(solution)/shard_map/ppermute | solution.py:317
  53.2 4.4 %collective-permute-start.16 = (bf16[64,16,128]{2,1,0:T(8,128)(2,1)S(1)}, bf16[64,16,128]{2,1,0:T(8,128)(2,1)S(1)}, u32[]{:S(2)}, u32[]{:S(2)}) collective-permute-start(bf16[64,16,128]{2,1,0:T(8,128)(2,1)S(1)} %pad_maximum_fusion.1), channel_id=1, source_target_pairs={{0,4},{1,5},{2,6},{3,7},{4,0},{5,1},{6,2},{7,3},{8,12},{9,13},{10,... | collective-permute-start | bytes 786440 | tf_op jit(solution)/shard_map/ppermute | solution.py:317
  54.3 3.0 %collective-permute-start.11 = (bf16[64,16,128]{2,1,0:T(8,128)(2,1)S(1)}, bf16[64,16,128]{2,1,0:T(8,128)(2,1)S(1)}, u32[]{:S(2)}, u32[]{:S(2)}) collective-permute-start(bf16[64,16,128]{2,1,0:T(8,128)(2,1)S(1)} %collective-permute-done.9), channel_id=1, source_target_pairs={{0,4},{1,5},{2,6},{3,7},{4,0},{5,1},{6,2},{7,3},{8,12},{9,13},{10,... | collective-permute-start | bytes 786440 | tf_op jit(solution)/shard_map/ppermute | solution.py:317
  56.1 2.3 %collective-permute-start.17 = (bf16[64,16,128]{2,1,0:T(8,128)(2,1)S(1)}, bf16[64,16,128]{2,1,0:T(8,128)(2,1)S(1)}, u32[]{:S(2)}, u32[]{:S(2)}) collective-permute-start(bf16[64,16,128]{2,1,0:T(8,128)(2,1)S(1)} %pad_maximum_fusion.2), channel_id=1, source_target_pairs={{0,4},{1,5},{2,6},{3,7},{4,0},{5,1},{6,2},{7,3},{8,12},{9,13},{10,... | collective-permute-start | bytes 786440 | tf_op jit(solution)/shard_map/ppermute | solution.py:317
where the time goes:
time: 64.4 us; the launch traced here: 64 us
  starting transfers between devices  23 us (36%)
  waiting for transfers between devices  19.6 us (30%)
  Pallas kernels  17.9 us (28%)
  local copies, waits for them, and re-layouts  3.1 us (5%)
    ppermute x18, starting transfers between devices, swap(): return lax.ppermute(x, AXES, [(i, i ^ bits) for i in range(devices)])  18.6 us
    ppermute x18, waiting for transfers between devices, swap(): return lax.ppermute(x, AXES, [(i, i ^ bits) for i in range(devices)])  10.5 us
    ppermute x1, waiting for transfers between devices, on_device(): lax.ppermute(side, AXES, odd_pairs + [(b, a) for a, b in odd_pairs])  9.17 us
    pallas_call x1, Pallas kernels, local_terms(): pl.pallas_call(functools.partial(local_kernel, parents=parents), out_shap...  8.36 us
    pallas_call x1, Pallas kernels, downward(): pl.pallas_call(downward_kernel, out_shape=jax.ShapeDtypeStruct((leaves, n...  5.52 us
    ppermute x1, starting transfers between devices, on_device(): lax.ppermute(side, AXES, odd_pairs + [(b, a) for a, b in odd_pairs])  4.32 us
    pallas_call x1, Pallas kernels, upward(): pl.pallas_call(functools.partial(upward_kernel, steps=steps, parents=pare...  3.98 us
    unnamed x32, local copies, waits for them, and re-layouts  2.94 us
  transfers between devices with their start and end apart: 19, of which 6 were waited for; matrix products, arithmetic and copies ran while one was open for 1% of the time, Pallas kernels for 13%

commit v1 on v0

v1 whole, which is shorter than its diff:
```python
import functools

import jax
import jax.numpy as jnp
from jax import lax
from jax.experimental import pallas as pl
from jax.experimental.pallas import tpu as pltpu
from jax.sharding import PartitionSpec as P


AXES = ("stream", "leaf")
FAR = 5
NEAR = 2
F32 = jnp.float32
BF16 = jnp.bfloat16

AHEAD = 3
LIMIT = 16 * 1024 * 1024


def dot_t(a, b):
    return lax.dot_general(a, b, (((1,), (1,)), ((), ())), preferred_element_type=F32)


def dot_n(a, b):
    return lax.dot_general(a, b, (((1,), (0,)), ((), ())), preferred_element_type=F32)


def in_hbm(x):
    return pltpu.with_memory_space_constraint(x, pltpu.HBM)


def left_half(rows, lanes):
    return lax.broadcasted_iota(jnp.int32, (rows, lanes), 1) < lanes // 2


def swap_halves(tile):
    half = tile.shape[1] // 2
    return jnp.concatenate([tile[:, half:], tile[:, :half]], axis=1)


def beside(tiles, mask):
    tops, bots = [], []
    for a, b in zip(tiles[::2], tiles[1::2]):
        tops.append(jnp.where(mask, a, swap_halves(b)))
        bots.append(jnp.where(mask, swap_halves(a), b))
    return jnp.concatenate([jnp.concatenate(tops, axis=1), jnp.concatenate(bots, axis=1)], axis=0)


def dense(pair, mask):
    half = pair.shape[0] // 2
    top, bot = pair[:half], pair[half:]
    return jnp.where(mask, top, swap_halves(bot)), jnp.where(mask, swap_halves(top), bot)


def diagonal(a, b):
    zero = jnp.zeros_like(a)
    return jnp.concatenate(
        [jnp.concatenate([a, zero], axis=1), jnp.concatenate([zero, b], axis=1)], axis=0
    )


def upward_kernel(
    par_ref, pts_hbm, basis_hbm, trans_hbm, coeff_ref, pay_ref, side_ref, pts_ref, basis_ref, trans_ref, sems, *, steps
):
    leaves, n, _ = pts_ref.shape
    parents = trans_ref.shape[0]
    mask = left_half(n // 2, 128)
    pairs = parents // steps

    def copies(i):
        own = pl.ds(i * pairs, pairs)
        both = pl.ds(2 * i * pairs, 2 * pairs)
        return (
            pltpu.make_async_copy(pts_hbm.at[both], pts_ref.at[both], sems.at[0, i]),
            pltpu.make_async_copy(basis_hbm.at[both], basis_ref.at[both], sems.at[1, i]),
            pltpu.make_async_copy(trans_hbm.at[own], trans_ref.at[own], sems.at[2, i]),
        )

    for i in range(steps):
        for c in copies(i):
            c.start()

    for i in range(steps):
        for c in copies(i):
            c.wait()
        own = range(i * pairs, (i + 1) * pairs)
        paired = []
        for p in own:
            x = jnp.concatenate([pts_ref[2 * p], pts_ref[2 * p + 1]], axis=1)
            paired.append(dot_t(x, diagonal(basis_ref[2 * p], basis_ref[2 * p + 1])).astype(BF16))
        ups = []
        for q in range(0, pairs, 2):
            x = jnp.concatenate([paired[q], paired[q + 1]], axis=1)
            ups.append(dot_t(x, diagonal(trans_ref[own[q]], trans_ref[own[q + 1]])).astype(BF16))
        for q, p in enumerate(own):
            coeff_ref[2 * p], coeff_ref[2 * p + 1] = dense(paired[q], mask)
        for q, up in enumerate(ups):
            p = own[2 * q]
            pay_ref[p], pay_ref[p + 1] = dense(up, mask)

    def edge(ref, at, first):
        lo = 0 if first else leaves - FAR
        for q in range(FAR):
            ref[at + q] = coeff_ref[lo + q]
        lo = 0 if first else leaves - NEAR
        for q in range(NEAR):
            x = pts_ref[lo + q]
            ref[at + FAR + 2 * q] = x[: n // 2]
            ref[at + FAR + 2 * q + 1] = x[n // 2 :]

    odd = par_ref[0] == 1

    @pl.when(odd)
    def _():
        edge(pay_ref, parents, True)
        edge(side_ref, 0, False)

    @pl.when(jnp.logical_not(odd))
    def _():
        edge(side_ref, 0, True)
        edge(pay_ref, parents, False)


def upward(par, points, basis, transfer):
    leaves, n, _ = points.shape
    parents, rank, _ = transfer.shape
    steps = 2
    halo = FAR + 2 * NEAR
    tile = (n // 2, 2 * rank)
    smem = pl.BlockSpec(memory_space=pltpu.SMEM)
    vmem = pl.BlockSpec(memory_space=pltpu.VMEM)
    hbm = pl.BlockSpec(memory_space=pltpu.HBM)
    return pl.pallas_call(
        functools.partial(upward_kernel, steps=steps),
        out_shape=(
            jax.ShapeDtypeStruct((leaves,) + tile, BF16),
            jax.ShapeDtypeStruct((parents + halo,) + tile, BF16),
            jax.ShapeDtypeStruct((halo,) + tile, BF16),
        ),
        in_specs=[smem] + [hbm] * 3,
        out_specs=[vmem] * 3,
        scratch_shapes=[
            pltpu.VMEM(points.shape, BF16),
            pltpu.VMEM(basis.shape, BF16),
            pltpu.VMEM(transfer.shape, BF16),
            pltpu.SemaphoreType.DMA((3, steps)),
        ],
        compiler_params=pltpu.CompilerParams(vmem_limit_bytes=LIMIT),
        name="upward",
    )(par, *[in_hbm(x) for x in (points, basis, transfer)])


def local_kernel(
    par_ref, noff_ref, coff_ref, pts_hbm, near_hbm, coup_hbm, coeff_ref, pay_ref, side_ref,
    near_out, field_out, pts_pad, coeff_pad, near_ref, coup_ref, sems, pts_sem, *, steps
):
    leaves, n, _ = pts_hbm.shape
    chunk = leaves // steps
    slots = near_ref.shape[1]
    far_slots = coff_ref.shape[0]
    halo = side_ref.shape[0]
    at = pay_ref.shape[0] - halo
    mask = left_half(n // 2, 128)

    def copies(i):
        own = pl.ds(i * chunk, chunk)
        return (
            pltpu.make_async_copy(near_hbm.at[own], near_ref.at[own], sems.at[0, i]),
            pltpu.make_async_copy(coup_hbm.at[own], coup_ref.at[own], sems.at[1, i]),
        )

    points_in = pltpu.make_async_copy(pts_hbm, pts_pad.at[pl.ds(NEAR, leaves)], pts_sem)
    points_in.start()
    for i in range(AHEAD):
        for c in copies(i):
            c.start()

    coeff_pad[FAR : FAR + leaves] = coeff_ref[...]

    def put(ref, at, low):
        co = 0 if low else leaves + FAR
        po = 0 if low else leaves + NEAR
        for q in range(FAR):
            coeff_pad[co + q] = ref[at + q]
        for q in range(NEAR):
            pts_pad[po + q, : n // 2] = ref[at + FAR + 2 * q]
            pts_pad[po + q, n // 2 :] = ref[at + FAR + 2 * q + 1]

    odd = par_ref[0] == 1

    @pl.when(odd)
    def _():
        put(pay_ref, at, True)
        put(side_ref, 0, False)

    @pl.when(jnp.logical_not(odd))
    def _():
        put(side_ref, 0, True)
        put(pay_ref, at, False)

    points_in.wait()

    def body(i, carry):
        for c in copies(i):
            c.wait()

        @pl.when(i + AHEAD < steps)
        def _():
            for c in copies(i + AHEAD):
                c.start()

        nears, fields = [], []
        for j in range(chunk):
            c = i * chunk + j
            xs = [pts_pad[c + NEAR + noff_ref[k, c]] for k in range(slots)]
            ws = [near_ref[c, k] for k in range(slots)]
            nears.append(dot_t(jnp.concatenate(xs, axis=1), jnp.concatenate(ws, axis=1)))
        for j in range(chunk):
            c = i * chunk + j
            lhs = beside([coeff_pad[c + FAR + coff_ref[k, c]] for k in range(far_slots)], mask)
            fields.append(dot_t(lhs, coup_ref[c]))
        for j in range(chunk):
            near_out[i * chunk + j] = nears[j]
        for j in range(0, chunk, 2):
            field_out[(i * chunk + j) // 2] = jnp.concatenate([fields[j], fields[j + 1]], axis=1)
        return carry

    lax.fori_loop(0, steps, body, 0)


def local_terms(par, near_offsets, coupling_offsets, points, coeffs, payload, side, near_blocks, leaf_coupling):
    leaves, n, size = points.shape
    rank = leaf_coupling.shape[1]
    steps = 8
    tile = side.shape[1:]
    smem = pl.BlockSpec(memory_space=pltpu.SMEM)
    vmem = pl.BlockSpec(memory_space=pltpu.VMEM)
    hbm = pl.BlockSpec(memory_space=pltpu.HBM)
    return pl.pallas_call(
        functools.partial(local_kernel, steps=steps),
        out_shape=(
            jax.ShapeDtypeStruct((leaves, n, size), F32),
            jax.ShapeDtypeStruct((leaves // 2, n, 2 * rank), F32),
        ),
        in_specs=[smem] * 3 + [hbm] * 3 + [vmem] * 3,
        out_specs=[vmem] * 2,
        scratch_shapes=[
            pltpu.VMEM((leaves + 2 * NEAR, n, size), BF16),
            pltpu.VMEM((leaves + 2 * FAR,) + tile, BF16),
            pltpu.VMEM(near_blocks.shape, BF16),
            pltpu.VMEM(leaf_coupling.shape, BF16),
            pltpu.SemaphoreType.DMA((2, steps)),
            pltpu.SemaphoreType.DMA,
        ],
        compiler_params=pltpu.CompilerParams(vmem_limit_bytes=LIMIT),
        name="local_terms",
    )(
        par, near_offsets, coupling_offsets, in_hbm(points), in_hbm(near_blocks), in_hbm(leaf_coupling),
        coeffs, payload, side,
    )


def downward_kernel(
    me_ref, owner_ref, local_ref, table, coup_ref, trans_ref, basis_ref, near_ref, field_ref, out_hbm, out_ref, sems,
    *, batch
):
    parents = trans_ref.shape[0]
    n = near_ref.shape[1]
    size = near_ref.shape[2]
    slots = owner_ref.shape[0]
    mask = left_half(n // 2, 128)
    me = me_ref[0]

    def copy(step):
        own = pl.ds(2 * batch * step, 2 * batch)
        return pltpu.make_async_copy(out_ref.at[own], out_hbm.at[own], sems.at[step])

    def rows(step, carry):
        own = [step * batch + q for q in range(batch)]
        halves = []
        for p in own:
            tiles = [table[(owner_ref[k, p] ^ me) * parents + local_ref[k, p]] for k in range(slots)]
            halves.append(dot_t(beside(tiles, mask), coup_ref[p]).astype(BF16))
        totals = [
            (field_ref[p] + dot_n(half, trans_ref[p])).astype(BF16) for p, half in zip(own, halves)
        ]
        fars = []
        for p, total in zip(own, totals):
            spread = diagonal(basis_ref[2 * p], basis_ref[2 * p + 1])
            fars.append(dot_n(total, spread))
        outs = []
        for p, far in zip(own, fars):
            outs.append((far[:, :size] + near_ref[2 * p]).astype(BF16))
            outs.append((far[:, size:] + near_ref[2 * p + 1]).astype(BF16))
        for q, out in enumerate(outs):
            out_ref[2 * batch * step + q] = out
        copy(step).start()
        return carry

    lax.fori_loop(0, parents // batch, rows, 0)
    for step in range(parents // batch):
        copy(step).wait()


def downward(me, owner, local, table, coupling, transfer, basis, near, field):
    leaves, n, size = near.shape
    smem = pl.BlockSpec(memory_space=pltpu.SMEM)
    vmem = pl.BlockSpec(memory_space=pltpu.VMEM)
    big = [pltpu.with_memory_space_constraint(x, pltpu.VMEM) for x in (table, coupling, transfer, basis, near, field)]
    batch = 8
    return pl.pallas_call(
        functools.partial(downward_kernel, batch=batch),
        out_shape=jax.ShapeDtypeStruct((leaves, n, size), BF16),
        in_specs=[smem] * 3 + [vmem] * 6,
        out_specs=pl.BlockSpec(memory_space=pltpu.HBM),
        scratch_shapes=[
            pltpu.VMEM((leaves, n, size), BF16),
            pltpu.SemaphoreType.DMA((transfer.shape[0] // batch,)),
        ],
        compiler_params=pltpu.CompilerParams(vmem_limit_bytes=LIMIT),
        name="downward",
    )(me, owner, local, *big)


def on_device(
    points_rhs,
    leaf_basis,
    transfer,
    leaf_coupling,
    parent_coupling,
    near_blocks,
    near_offsets,
    coupling_offsets,
    parent_owner,
    parent_local,
):
    streams, leafs = lax.axis_size("stream"), lax.axis_size("leaf")
    devices = streams * leafs
    parents = transfer.shape[0]
    me = lax.axis_index(AXES).astype(jnp.int32)
    par = (me % 2).reshape(1)

    def swap(x, bits):
        return lax.ppermute(x, AXES, [(i, i ^ bits) for i in range(devices)])

    coeffs, payload, side = upward(par, points_rhs, leaf_basis, transfer)
    odd_pairs = [(i, i + 1) for i in range(1, devices - 1, 2)]
    side_in = lax.ppermute(side, AXES, odd_pairs + [(b, a) for a, b in odd_pairs])

    got = swap(payload, 1)
    line = [payload[:parents], got[:parents]]
    line += [swap(line[0], k) for k in range(2, leafs)]
    groups = [(0, jnp.concatenate(line[:2], axis=0)), (2, jnp.concatenate(line[2:], axis=0))]

    pieces = {}
    for base, group in groups:
        have = {0: group}
        for s in range(2, streams, 2):
            low = s & -s
            high = 1 << (s.bit_length() - 1)
            if low == high:
                have[s] = swap(have[s ^ low], s * leafs)
            else:
                rows = group.shape[0] // 2
                have[s] = jnp.concatenate(
                    [swap(have[s ^ low][:rows], low * leafs), swap(have[s ^ high][rows:], high * leafs)],
                    axis=0,
                )
        for s in list(have):
            have[s ^ 1] = swap(have[s], leafs)
        for s, g in have.items():
            pieces[s * leafs + base] = g
    table = jnp.concatenate([pieces[k] for k in sorted(pieces)], axis=0)

    near, field = local_terms(
        par, near_offsets.T, coupling_offsets.T, points_rhs, coeffs, got, side_in, near_blocks, leaf_coupling
    )
    return downward(
        me.reshape(1), parent_owner.T, parent_local.T, table, parent_coupling, transfer, leaf_basis, near, field
    )


def solution(mesh):
    three = P(AXES, None, None)
    two = P(AXES, None)
    return jax.shard_map(
        on_device,
        mesh=mesh,
        in_specs=(three,) * 5 + (P(AXES, None, None, None),) + (two,) * 4,
        out_specs=three,
        check_vma=False,
    )
```

time: 64.4 us -> 46.4 us (0.72)
  the two profiles are of different devices: /device:TPU:17 before, /device:TPU:0 now
where the time goes in v1:
time: 46.4 us; the launch traced here: 46.2 us
  starting transfers between devices  18.5 us (40%)
  Pallas kernels  13.5 us (29%)
  waiting for transfers between devices  13.1 us (28%)
  local copies, waits for them, and re-layouts  0.75 us (2%)
    ppermute x19, starting transfers between devices, swap(): return lax.ppermute(x, AXES, [(i, i ^ bits) for i in range(devices)])  17.9 us
    ppermute x19, waiting for transfers between devices, swap(): return lax.ppermute(x, AXES, [(i, i ^ bits) for i in range(devices)])  13.1 us
    pallas_call x1, Pallas kernels, local_terms(): pl.pallas_call(functools.partial(local_kernel, steps=steps), out_shape=(j...  6.94 us
    pallas_call x1, Pallas kernels, downward(): pl.pallas_call(functools.partial(downward_kernel, batch=batch), out_shape...  3.81 us
    pallas_call x1, Pallas kernels, upward(): pl.pallas_call(functools.partial(upward_kernel, steps=steps), out_shape=(...  2.7 us
  transfers between devices with their start and end apart: 20, of which 9 were waited for; matrix products, arithmetic and copies ran while one was open for 2% of the time, Pallas kernels for 15%

profile of v1, /device:TPU:0, one launch (start us, length us, event | category | flops | bytes accessed | tf_op | source)
XLA Modules:
  0.0 46.2 jit_solution(7334667722861192775)
XLA Ops:
  0.0 0.0 copy-start.5
  0.0 0.0 copy-start.6
  0.0 2.7 %upward.1 = (bf16[64,16,128]{2,1,0:T(8,128)(2,1)S(1)}, bf16[41,16,128]{2,1,0:T(8,128)(2,1)S(1)}, bf16[9,16,128]{2,1,0:T(8,128)(2,1)S(1)}) custom-call(s32[1]{0:T(128)} %bitcast.3.par_ref, bf16[64,32,128]{2,1,0:T(8,128)(2,1)} %pts_hbm.3, bf16[64,64,128]{2,1,0:T(8,128)(2,1)} %basis_ref.1, bf16[32,64,128]{2,1,0:T(8,128)(2,1)} %trans_ref.1), custom_call_target="tpu_custom_call" | custom-call | tf_op jit(solution)/shard_map/upward/pallas_call | solution.py:134
  2.7 3.1 %collective-permute-start = (bf16[41,16,128]{2,1,0:T(8,128)(2,1)S(1)}, bf16[41,16,128]{2,1,0:T(8,128)(2,1)S(1)}, u32[]{:S(2)}, u32[]{:S(2)}) collective-permute-start(bf16[41,16,128]{2,1,0:T(8,128)(2,1)S(1)} %get-tuple-element.10), channel_id=1, source_target_pairs={{0,1},{1,0},{2,3},{3,2},{4,5},{5,4},{6,7},{7,6},{8,9},{9,8},{10,11... | collective-permute-start | bytes 503816 | tf_op jit(solution)/shard_map/ppermute | solution.py:345
  5.9 2.7 %collective-permute-start.1 = (bf16[32,16,128]{2,1,0:T(8,128)(2,1)S(1)}, bf16[32,16,128]{2,1,0:T(8,128)(2,1)S(1)}, u32[]{:S(2)}, u32[]{:S(2)}) collective-permute-start(bf16[32,16,128]{2,1,0:T(8,128)(2,1)S(1)} %get-tuple-element.17), channel_id=1, source_target_pairs={{0,2},{1,3},{2,0},{3,1},{4,6},{5,7},{6,4},{7,5},{8,10},{9,11},{10,... | collective-permute-start | bytes 393224 | tf_op jit(solution)/shard_map/ppermute | solution.py:345
  8.5 0.0 collective-permute-start.2
  8.5 0.7 %collective-permute-start.19 = (bf16[9,16,128]{2,1,0:T(8,128)(2,1)S(1)}, bf16[9,16,128]{2,1,0:T(8,128)(2,1)S(1)}, u32[]{:S(2)}, u32[]{:S(2)}) collective-permute-start(bf16[9,16,128]{2,1,0:T(8,128)(2,1)S(1)} %get-tuple-element.12), channel_id=1, source_target_pairs={{1,2},{3,4},{5,6},{7,8},{9,10},{11,12},{13,14},{15,16},{17,18},{19... | collective-permute-start | bytes 110600 | tf_op jit(solution)/shard_map/ppermute | solution.py:349
  9.2 3.0 %collective-permute-done.pay_ref = bf16[41,16,128]{2,1,0:T(8,128)(2,1)S(1)} collective-permute-done((bf16[41,16,128]{2,1,0:T(8,128)(2,1)S(1)}, bf16[41,16,128]{2,1,0:T(8,128)(2,1)S(1)}, u32[]{:S(2)}, u32[]{:S(2)}) %collective-permute-start) | collective-permute-done | bytes 167968 | tf_op jit(solution)/shard_map/ppermute | solution.py:345
  12.2 2.2 %collective-permute-start.5 = (bf16[64,16,128]{2,1,0:T(8,128)(2,1)S(1)}, bf16[64,16,128]{2,1,0:T(8,128)(2,1)S(1)}, u32[]{:S(2)}, u32[]{:S(2)}) collective-permute-start(bf16[64,16,128]{2,1,0:T(8,128)(2,1)S(1)} %pad_maximum_fusion), channel_id=1, source_target_pairs={{0,8},{1,9},{2,10},{3,11},{4,12},{5,13},{6,14},{7,15},{8,0},{9,1},... | collective-permute-start | bytes 786440 | tf_op jit(solution)/shard_map/ppermute | solution.py:345
  14.5 1.5 %collective-permute-start.9 = (bf16[64,16,128]{2,1,0:T(8,128)(2,1)S(1)}, bf16[64,16,128]{2,1,0:T(8,128)(2,1)S(1)}, u32[]{:S(2)}, u32[]{:S(2)}) collective-permute-start(bf16[64,16,128]{2,1,0:T(8,128)(2,1)S(1)} %pad_maximum_fusion), channel_id=1, source_target_pairs={{0,16},{1,17},{2,18},{3,19},{4,20},{5,21},{6,22},{7,23},{8,24},{9,... | collective-permute-start | bytes 786440 | tf_op jit(solution)/shard_map/ppermute | solution.py:345
  16.0 3.6 %collective-permute-done.1 = bf16[32,16,128]{2,1,0:T(8,128)(2,1)S(1)} collective-permute-done((bf16[32,16,128]{2,1,0:T(8,128)(2,1)S(1)}, bf16[32,16,128]{2,1,0:T(8,128)(2,1)S(1)}, u32[]{:S(2)}, u32[]{:S(2)}) %collective-permute-start.1) | collective-permute-done | bytes 131104 | tf_op jit(solution)/shard_map/ppermute | solution.py:345
  19.6 0.0 collective-permute-done.2
  19.7 0.1 constant_dynamic-update-slice_fusion
  19.7 1.6 %collective-permute-start.10 = (bf16[64,16,128]{2,1,0:T(8,128)(2,1)S(1)}, bf16[64,16,128]{2,1,0:T(8,128)(2,1)S(1)}, u32[]{:S(2)}, u32[]{:S(2)}) collective-permute-start(bf16[64,16,128]{2,1,0:T(8,128)(2,1)S(1)} %get-tuple-element.19), channel_id=1, source_target_pairs={{0,16},{1,17},{2,18},{3,19},{4,20},{5,21},{6,22},{7,23},{8,24},{9,... | collective-permute-start | bytes 786440 | tf_op jit(solution)/shard_map/ppermute | solution.py:345
  21.3 1.1 %collective-permute-start.6 = (bf16[64,16,128]{2,1,0:T(8,128)(2,1)S(1)}, bf16[64,16,128]{2,1,0:T(8,128)(2,1)S(1)}, u32[]{:S(2)}, u32[]{:S(2)}) collective-permute-start(bf16[64,16,128]{2,1,0:T(8,128)(2,1)S(1)} %get-tuple-element.19), channel_id=1, source_target_pairs={{0,8},{1,9},{2,10},{3,11},{4,12},{5,13},{6,14},{7,15},{8,0},{9,1},... | collective-permute-start | bytes 786440 | tf_op jit(solution)/shard_map/ppermute | solution.py:345
  22.4 0.0 collective-permute-done.19.side_ref
  22.4 0.0 collective-permute-start.3
  22.4 0.9 %collective-permute-done.9 = bf16[64,16,128]{2,1,0:T(8,128)(2,1)S(1)} collective-permute-done((bf16[64,16,128]{2,1,0:T(8,128)(2,1)S(1)}, bf16[64,16,128]{2,1,0:T(8,128)(2,1)S(1)}, u32[]{:S(2)}, u32[]{:S(2)}) %collective-permute-start.9) | collective-permute-done | bytes 262176 | tf_op jit(solution)/shard_map/ppermute | solution.py:345
  23.3 0.7 %collective-permute-start.4 = (bf16[64,16,128]{2,1,0:T(8,128)(2,1)S(1)}, bf16[64,16,128]{2,1,0:T(8,128)(2,1)S(1)}, u32[]{:S(2)}, u32[]{:S(2)}) collective-permute-start(bf16[64,16,128]{2,1,0:T(8,128)(2,1)S(1)} %get-tuple-element.19), channel_id=1, source_target_pairs={{0,4},{1,5},{2,6},{3,7},{4,0},{5,1},{6,2},{7,3},{8,12},{9,13},{10,... | collective-permute-start | bytes 786440 | tf_op jit(solution)/shard_map/ppermute | solution.py:345
  24.1 0.0 copy-done.5
  24.1 0.0 copy-done.6
  24.1 6.9 %local_terms.1 = (f32[64,32,128]{2,1,0:T(8,128)S(1)}, f32[32,32,128]{2,1,0:T(8,128)S(1)}) custom-call(s32[1]{0:T(128)} %bitcast.3.par_ref, s32[3,64]{1,0:T(4,128)S(1)} %bitcast.8, s32[4,64]{1,0:T(4,128)S(1)} %bitcast.9, bf16[64,32,128]{2,1,0:T(8,128)(2,1)} %pts_hbm.3, bf16[64,3,128,128]{3,2,1,0:T(8,128)(2,1)} %near_hbm.1, bf16[64,64,256]{2,1,0:T(8,128)(2,1)} %coup_hbm.1, ...), custom_call_target="tpu_custom_call" | custom-call | tf_op jit(solution)/shard_map/local_terms/pallas_call | solution.py:240
  31.0 0.0 collective-permute-done.5
  31.0 0.6 %collective-permute-start.13 = (bf16[32,16,128]{2,1,0:T(8,128)(2,1)S(1)}, bf16[32,16,128]{2,1,0:T(8,128)(2,1)S(1)}, u32[]{:S(2)}, u32[]{:S(2)}) collective-permute-start(bf16[32,16,128]{2,1,0:T(8,128)(2,1)S(1)} %slice.25), channel_id=1, source_target_pairs={{0,8},{1,9},{2,10},{3,11},{4,12},{5,13},{6,14},{7,15},{8,0},{9,1},... | collective-permute-start | bytes 393224 | tf_op jit(solution)/shard_map/ppermute | solution.py:345
  31.7 0.0 collective-permute-done.10
  31.7 2.1 %collective-permute-start.14 = (bf16[32,16,128]{2,1,0:T(8,128)(2,1)S(1)}, bf16[32,16,128]{2,1,0:T(8,128)(2,1)S(1)}, u32[]{:S(2)}, u32[]{:S(2)}) collective-permute-start(bf16[32,16,128]{2,1,0:T(8,128)(2,1)S(1)} %slice.26), channel_id=1, source_target_pairs={{0,16},{1,17},{2,18},{3,19},{4,20},{5,21},{6,22},{7,23},{8,24},{9,... | collective-permute-start | bytes 393224 | tf_op jit(solution)/shard_map/ppermute | solution.py:345
  33.8 0.0 collective-permute-done.6
  33.8 1.2 %collective-permute-start.15 = (bf16[32,16,128]{2,1,0:T(8,128)(2,1)S(1)}, bf16[32,16,128]{2,1,0:T(8,128)(2,1)S(1)}, u32[]{:S(2)}, u32[]{:S(2)}) collective-permute-start(bf16[32,16,128]{2,1,0:T(8,128)(2,1)S(1)} %slice.27), channel_id=1, source_target_pairs={{0,8},{1,9},{2,10},{3,11},{4,12},{5,13},{6,14},{7,15},{8,0},{9,1},... | collective-permute-start | bytes 393224 | tf_op jit(solution)/shard_map/ppermute | solution.py:345
  35.0 0.0 collective-permute-done.3
  35.0 0.5 collective-permute-start.16
  35.4 0.0 copy-start
  35.4 0.0 copy-start.1
  35.4 0.0 copy-start.2
  35.4 0.0 copy-start.3
  35.4 0.0 copy-start.4
  35.5 0.0 collective-permute-done.4
  35.5 0.1 collective-permute-start.7
  35.7 1.0 %collective-permute-done.13 = bf16[32,16,128]{2,1,0:T(8,128)(2,1)S(1)} collective-permute-done((bf16[32,16,128]{2,1,0:T(8,128)(2,1)S(1)}, bf16[32,16,128]{2,1,0:T(8,128)(2,1)S(1)}, u32[]{:S(2)}, u32[]{:S(2)}) %collective-permute-start.13) | collective-permute-done | bytes 131104 | tf_op jit(solution)/shard_map/ppermute | solution.py:345
  36.7 0.0 collective-permute-start.8
  36.7 1.4 %collective-permute-done.14 = bf16[32,16,128]{2,1,0:T(8,128)(2,1)S(1)} collective-permute-done((bf16[32,16,128]{2,1,0:T(8,128)(2,1)S(1)}, bf16[32,16,128]{2,1,0:T(8,128)(2,1)S(1)}, u32[]{:S(2)}, u32[]{:S(2)}) %collective-permute-start.14) | collective-permute-done | bytes 131104 | tf_op jit(solution)/shard_map/ppermute | solution.py:345
  38.1 0.0 collective-permute-start.11
  38.1 1.2 %collective-permute-done.15 = bf16[32,16,128]{2,1,0:T(8,128)(2,1)S(1)} collective-permute-done((bf16[32,16,128]{2,1,0:T(8,128)(2,1)S(1)}, bf16[32,16,128]{2,1,0:T(8,128)(2,1)S(1)}, u32[]{:S(2)}, u32[]{:S(2)}) %collective-permute-start.15) | collective-permute-done | bytes 131104 | tf_op jit(solution)/shard_map/ppermute | solution.py:345
  39.3 0.0 collective-permute-start.12
  39.3 1.1 %collective-permute-done.16 = bf16[32,16,128]{2,1,0:T(8,128)(2,1)S(1)} collective-permute-done((bf16[32,16,128]{2,1,0:T(8,128)(2,1)S(1)}, bf16[32,16,128]{2,1,0:T(8,128)(2,1)S(1)}, u32[]{:S(2)}, u32[]{:S(2)}) %collective-permute-start.16) | collective-permute-done | bytes 131104 | tf_op jit(solution)/shard_map/ppermute | solution.py:345
  40.4 0.0 collective-permute-start.17
  40.5 0.0 collective-permute-done.7
  40.5 0.6 %collective-permute-start.18 = (bf16[64,16,128]{2,1,0:T(8,128)(2,1)S(1)}, bf16[64,16,128]{2,1,0:T(8,128)(2,1)S(1)}, u32[]{:S(2)}, u32[]{:S(2)}) collective-permute-start(bf16[64,16,128]{2,1,0:T(8,128)(2,1)S(1)} %pad_maximum_fusion.2), channel_id=1, source_target_pairs={{0,4},{1,5},{2,6},{3,7},{4,0},{5,1},{6,2},{7,3},{8,12},{9,13},{10,... | collective-permute-start | bytes 786440 | tf_op jit(solution)/shard_map/ppermute | solution.py:345
  41.1 0.0 collective-permute-done.8
  41.2 0.0 collective-permute-done.11
  41.3 0.0 collective-permute-done.12
  41.5 0.5 %collective-permute-done.17 = bf16[64,16,128]{2,1,0:T(8,128)(2,1)S(1)} collective-permute-done((bf16[64,16,128]{2,1,0:T(8,128)(2,1)S(1)}, bf16[64,16,128]{2,1,0:T(8,128)(2,1)S(1)}, u32[]{:S(2)}, u32[]{:S(2)}) %collective-permute-start.17) | collective-permute-done | bytes 262176 | tf_op jit(solution)/shard_map/ppermute | solution.py:345
  42.0 0.3 collective-permute-done.18
  42.4 0.0 copy-done
  42.4 0.0 copy-done.1
  42.4 0.0 copy-done.2
  42.4 0.0 copy-done.3
  42.4 0.0 copy-done.4
  42.4 3.8 %downward.1 = bf16[64,32,128]{2,1,0:T(8,128)(2,1)} custom-call(s32[1]{0:T(128)} %bitcast.me_ref, s32[8,32]{1,0:T(8,128)S(1)} %bitcast.6, s32[8,32]{1,0:T(8,128)S(1)} %bitcast.7, bf16[1024,16,128]{2,1,0:T(8,128)(2,1)S(1)} %constant_dynamic-update-slice_fusion.2.table, bf16[32,64,512]{2,1,0:T(8,128)(2,1)S(1)} %copy-done.2, bf16[32,64,128]{2,1,0:T(8,128)(2,1)S(1)} %copy-done.1, ...), custom_call_target="tpu_custom_call" | custom-call | tf_op jit(solution)/shard_map/downward/pallas_call | solution.py:312
  (26 shorter events, 0.7 us)
Async XLA Ops:
  0.0 24.1 %copy-start.5 = (s32[64,3]{0,1:T(4,128)S(1)}, s32[64,3]{0,1:T(4,128)}, u32[]{:S(2)}) copy-start(s32[64,3]{0,1:T(4,128)} %param.16) | copy-start | bytes 2308
  0.0 24.1 %copy-start.6 = (s32[64,4]{0,1:T(4,128)S(1)}, s32[64,4]{0,1:T(4,128)}, u32[]{:S(2)}) copy-start(s32[64,4]{0,1:T(4,128)} %param.17) | copy-start | bytes 3076
  2.7 9.4 %collective-permute-start = (bf16[41,16,128]{2,1,0:T(8,128)(2,1)S(1)}, bf16[41,16,128]{2,1,0:T(8,128)(2,1)S(1)}, u32[]{:S(2)}, u32[]{:S(2)}) collective-permute-start(bf16[41,16,128]{2,1,0:T(8,128)(2,1)S(1)} %get-tuple-element.10), channel_id=1, source_target_pairs={{0,1},{1,0},{2,3},{3,2},{4,5},{5,4},{6,7},{7,6},{8,9},{9,8},{10,11... | collective-permute-start | bytes 503816 | tf_op jit(solution)/shard_map/ppermute | solution.py:345
  5.9 13.7 %collective-permute-start.1 = (bf16[32,16,128]{2,1,0:T(8,128)(2,1)S(1)}, bf16[32,16,128]{2,1,0:T(8,128)(2,1)S(1)}, u32[]{:S(2)}, u32[]{:S(2)}) collective-permute-start(bf16[32,16,128]{2,1,0:T(8,128)(2,1)S(1)} %get-tuple-element.17), channel_id=1, source_target_pairs={{0,2},{1,3},{2,0},{3,1},{4,6},{5,7},{6,4},{7,5},{8,10},{9,11},{10,... | collective-permute-start | bytes 393224 | tf_op jit(solution)/shard_map/ppermute | solution.py:345
  8.5 11.1 %collective-permute-start.2 = (bf16[32,16,128]{2,1,0:T(8,128)(2,1)S(1)}, bf16[32,16,128]{2,1,0:T(8,128)(2,1)S(1)}, u32[]{:S(2)}, u32[]{:S(2)}) collective-permute-start(bf16[32,16,128]{2,1,0:T(8,128)(2,1)S(1)} %get-tuple-element.17), channel_id=1, source_target_pairs={{0,3},{1,2},{2,1},{3,0},{4,7},{5,6},{6,5},{7,4},{8,11},{9,10},{10,... | collective-permute-start | bytes 393224 | tf_op jit(solution)/shard_map/ppermute | solution.py:345
  8.5 13.9 %collective-permute-start.19 = (bf16[9,16,128]{2,1,0:T(8,128)(2,1)S(1)}, bf16[9,16,128]{2,1,0:T(8,128)(2,1)S(1)}, u32[]{:S(2)}, u32[]{:S(2)}) collective-permute-start(bf16[9,16,128]{2,1,0:T(8,128)(2,1)S(1)} %get-tuple-element.12), channel_id=1, source_target_pairs={{1,2},{3,4},{5,6},{7,8},{9,10},{11,12},{13,14},{15,16},{17,18},{19... | collective-permute-start | bytes 110600 | tf_op jit(solution)/shard_map/ppermute | solution.py:349
  12.2 18.8 %collective-permute-start.5 = (bf16[64,16,128]{2,1,0:T(8,128)(2,1)S(1)}, bf16[64,16,128]{2,1,0:T(8,128)(2,1)S(1)}, u32[]{:S(2)}, u32[]{:S(2)}) collective-permute-start(bf16[64,16,128]{2,1,0:T(8,128)(2,1)S(1)} %pad_maximum_fusion), channel_id=1, source_target_pairs={{0,8},{1,9},{2,10},{3,11},{4,12},{5,13},{6,14},{7,15},{8,0},{9,1},... | collective-permute-start | bytes 786440 | tf_op jit(solution)/shard_map/ppermute | solution.py:345
  14.5 8.9 %collective-permute-start.9 = (bf16[64,16,128]{2,1,0:T(8,128)(2,1)S(1)}, bf16[64,16,128]{2,1,0:T(8,128)(2,1)S(1)}, u32[]{:S(2)}, u32[]{:S(2)}) collective-permute-start(bf16[64,16,128]{2,1,0:T(8,128)(2,1)S(1)} %pad_maximum_fusion), channel_id=1, source_target_pairs={{0,16},{1,17},{2,18},{3,19},{4,20},{5,21},{6,22},{7,23},{8,24},{9,... | collective-permute-start | bytes 786440 | tf_op jit(solution)/shard_map/ppermute | solution.py:345
  19.7 11.9 %collective-permute-start.10 = (bf16[64,16,128]{2,1,0:T(8,128)(2,1)S(1)}, bf16[64,16,128]{2,1,0:T(8,128)(2,1)S(1)}, u32[]{:S(2)}, u32[]{:S(2)}) collective-permute-start(bf16[64,16,128]{2,1,0:T(8,128)(2,1)S(1)} %get-tuple-element.19), channel_id=1, source_target_pairs={{0,16},{1,17},{2,18},{3,19},{4,20},{5,21},{6,22},{7,23},{8,24},{9,... | collective-permute-start | bytes 786440 | tf_op jit(solution)/shard_map/ppermute | solution.py:345
  21.3 12.5 %collective-permute-start.6 = (bf16[64,16,128]{2,1,0:T(8,128)(2,1)S(1)}, bf16[64,16,128]{2,1,0:T(8,128)(2,1)S(1)}, u32[]{:S(2)}, u32[]{:S(2)}) collective-permute-start(bf16[64,16,128]{2,1,0:T(8,128)(2,1)S(1)} %get-tuple-element.19), channel_id=1, source_target_pairs={{0,8},{1,9},{2,10},{3,11},{4,12},{5,13},{6,14},{7,15},{8,0},{9,1},... | collective-permute-start | bytes 786440 | tf_op jit(solution)/shard_map/ppermute | solution.py:345
  22.4 12.6 %collective-permute-start.3 = (bf16[64,16,128]{2,1,0:T(8,128)(2,1)S(1)}, bf16[64,16,128]{2,1,0:T(8,128)(2,1)S(1)}, u32[]{:S(2)}, u32[]{:S(2)}) collective-permute-start(bf16[64,16,128]{2,1,0:T(8,128)(2,1)S(1)} %pad_maximum_fusion), channel_id=1, source_target_pairs={{0,4},{1,5},{2,6},{3,7},{4,0},{5,1},{6,2},{7,3},{8,12},{9,13},{10,... | collective-permute-start | bytes 786440 | tf_op jit(solution)/shard_map/ppermute | solution.py:345
  23.3 12.1 %collective-permute-start.4 = (bf16[64,16,128]{2,1,0:T(8,128)(2,1)S(1)}, bf16[64,16,128]{2,1,0:T(8,128)(2,1)S(1)}, u32[]{:S(2)}, u32[]{:S(2)}) collective-permute-start(bf16[64,16,128]{2,1,0:T(8,128)(2,1)S(1)} %get-tuple-element.19), channel_id=1, source_target_pairs={{0,4},{1,5},{2,6},{3,7},{4,0},{5,1},{6,2},{7,3},{8,12},{9,13},{10,... | collective-permute-start | bytes 786440 | tf_op jit(solution)/shard_map/ppermute | solution.py:345
  31.0 5.6 %collective-permute-start.13 = (bf16[32,16,128]{2,1,0:T(8,128)(2,1)S(1)}, bf16[32,16,128]{2,1,0:T(8,128)(2,1)S(1)}, u32[]{:S(2)}, u32[]{:S(2)}) collective-permute-start(bf16[32,16,128]{2,1,0:T(8,128)(2,1)S(1)} %slice.25), channel_id=1, source_target_pairs={{0,8},{1,9},{2,10},{3,11},{4,12},{5,13},{6,14},{7,15},{8,0},{9,1},... | collective-permute-start | bytes 393224 | tf_op jit(solution)/shard_map/ppermute | solution.py:345
  31.7 6.4 %collective-permute-start.14 = (bf16[32,16,128]{2,1,0:T(8,128)(2,1)S(1)}, bf16[32,16,128]{2,1,0:T(8,128)(2,1)S(1)}, u32[]{:S(2)}, u32[]{:S(2)}) collective-permute-start(bf16[32,16,128]{2,1,0:T(8,128)(2,1)S(1)} %slice.26), channel_id=1, source_target_pairs={{0,16},{1,17},{2,18},{3,19},{4,20},{5,21},{6,22},{7,23},{8,24},{9,... | collective-permute-start | bytes 393224 | tf_op jit(solution)/shard_map/ppermute | solution.py:345
  33.8 5.6 %collective-permute-start.15 = (bf16[32,16,128]{2,1,0:T(8,128)(2,1)S(1)}, bf16[32,16,128]{2,1,0:T(8,128)(2,1)S(1)}, u32[]{:S(2)}, u32[]{:S(2)}) collective-permute-start(bf16[32,16,128]{2,1,0:T(8,128)(2,1)S(1)} %slice.27), channel_id=1, source_target_pairs={{0,8},{1,9},{2,10},{3,11},{4,12},{5,13},{6,14},{7,15},{8,0},{9,1},... | collective-permute-start | bytes 393224 | tf_op jit(solution)/shard_map/ppermute | solution.py:345
  35.0 5.5 %collective-permute-start.16 = (bf16[32,16,128]{2,1,0:T(8,128)(2,1)S(1)}, bf16[32,16,128]{2,1,0:T(8,128)(2,1)S(1)}, u32[]{:S(2)}, u32[]{:S(2)}) collective-permute-start(bf16[32,16,128]{2,1,0:T(8,128)(2,1)S(1)} %slice.28), channel_id=1, source_target_pairs={{0,16},{1,17},{2,18},{3,19},{4,20},{5,21},{6,22},{7,23},{8,24},{9,... | collective-permute-start | bytes 393224 | tf_op jit(solution)/shard_map/ppermute | solution.py:345
  35.4 7.0 %copy-start = (bf16[64,64,128]{2,1,0:T(8,128)(2,1)S(1)}, bf16[64,64,128]{2,1,0:T(8,128)(2,1)}, u32[]{:S(2)}) copy-start(bf16[64,64,128]{2,1,0:T(8,128)(2,1)} %basis_ref.1) | copy-start | bytes 3145732
  35.4 7.0 %copy-start.1 = (bf16[32,64,128]{2,1,0:T(8,128)(2,1)S(1)}, bf16[32,64,128]{2,1,0:T(8,128)(2,1)}, u32[]{:S(2)}) copy-start(bf16[32,64,128]{2,1,0:T(8,128)(2,1)} %trans_ref.1) | copy-start | bytes 1572868
  35.4 7.0 %copy-start.2 = (bf16[32,64,512]{2,1,0:T(8,128)(2,1)S(1)}, bf16[32,64,512]{2,1,0:T(8,128)(2,1)}, u32[]{:S(2)}) copy-start(bf16[32,64,512]{2,1,0:T(8,128)(2,1)} %coup_ref.1) | copy-start | bytes 6291460
  35.4 7.0 %copy-start.3 = (s32[32,8]{0,1:T(8,128)S(1)}, s32[32,8]{0,1:T(8,128)}, u32[]{:S(2)}) copy-start(s32[32,8]{0,1:T(8,128)} %param.18) | copy-start | bytes 3076
  35.4 7.0 %copy-start.4 = (s32[32,8]{0,1:T(8,128)S(1)}, s32[32,8]{0,1:T(8,128)}, u32[]{:S(2)}) copy-start(s32[32,8]{0,1:T(8,128)} %param.19) | copy-start | bytes 3076
  35.5 5.0 %collective-permute-start.7 = (bf16[64,16,128]{2,1,0:T(8,128)(2,1)S(1)}, bf16[64,16,128]{2,1,0:T(8,128)(2,1)S(1)}, u32[]{:S(2)}, u32[]{:S(2)}) collective-permute-start(bf16[64,16,128]{2,1,0:T(8,128)(2,1)S(1)} %collective-permute-done.5), channel_id=1, source_target_pairs={{0,4},{1,5},{2,6},{3,7},{4,0},{5,1},{6,2},{7,3},{8,12},{9,13},{10,... | collective-permute-start | bytes 786440 | tf_op jit(solution)/shard_map/ppermute | solution.py:345
  36.7 4.4 %collective-permute-start.8 = (bf16[64,16,128]{2,1,0:T(8,128)(2,1)S(1)}, bf16[64,16,128]{2,1,0:T(8,128)(2,1)S(1)}, u32[]{:S(2)}, u32[]{:S(2)}) collective-permute-start(bf16[64,16,128]{2,1,0:T(8,128)(2,1)S(1)} %collective-permute-done.6), channel_id=1, source_target_pairs={{0,4},{1,5},{2,6},{3,7},{4,0},{5,1},{6,2},{7,3},{8,12},{9,13},{10,... | collective-permute-start | bytes 786440 | tf_op jit(solution)/shard_map/ppermute | solution.py:345
  38.1 3.1 %collective-permute-start.11 = (bf16[64,16,128]{2,1,0:T(8,128)(2,1)S(1)}, bf16[64,16,128]{2,1,0:T(8,128)(2,1)S(1)}, u32[]{:S(2)}, u32[]{:S(2)}) collective-permute-start(bf16[64,16,128]{2,1,0:T(8,128)(2,1)S(1)} %collective-permute-done.9), channel_id=1, source_target_pairs={{0,4},{1,5},{2,6},{3,7},{4,0},{5,1},{6,2},{7,3},{8,12},{9,13},{10,... | collective-permute-start | bytes 786440 | tf_op jit(solution)/shard_map/ppermute | solution.py:345
  39.3 2.0 %collective-permute-start.12 = (bf16[64,16,128]{2,1,0:T(8,128)(2,1)S(1)}, bf16[64,16,128]{2,1,0:T(8,128)(2,1)S(1)}, u32[]{:S(2)}, u32[]{:S(2)}) collective-permute-start(bf16[64,16,128]{2,1,0:T(8,128)(2,1)S(1)} %collective-permute-done.10), channel_id=1, source_target_pairs={{0,4},{1,5},{2,6},{3,7},{4,0},{5,1},{6,2},{7,3},{8,12},{9,13},{10,... | collective-permute-start | bytes 786440 | tf_op jit(solution)/shard_map/ppermute | solution.py:345
  40.4 1.5 %collective-permute-start.17 = (bf16[64,16,128]{2,1,0:T(8,128)(2,1)S(1)}, bf16[64,16,128]{2,1,0:T(8,128)(2,1)S(1)}, u32[]{:S(2)}, u32[]{:S(2)}) collective-permute-start(bf16[64,16,128]{2,1,0:T(8,128)(2,1)S(1)} %pad_maximum_fusion.1), channel_id=1, source_target_pairs={{0,4},{1,5},{2,6},{3,7},{4,0},{5,1},{6,2},{7,3},{8,12},{9,13},{10,... | collective-permute-start | bytes 786440 | tf_op jit(solution)/shard_map/ppermute | solution.py:345
  40.5 1.9 %collective-permute-start.18 = (bf16[64,16,128]{2,1,0:T(8,128)(2,1)S(1)}, bf16[64,16,128]{2,1,0:T(8,128)(2,1)S(1)}, u32[]{:S(2)}, u32[]{:S(2)}) collective-permute-start(bf16[64,16,128]{2,1,0:T(8,128)(2,1)S(1)} %pad_maximum_fusion.2), channel_id=1, source_target_pairs={{0,4},{1,5},{2,6},{3,7},{4,0},{5,1},{6,2},{7,3},{8,12},{9,13},{10,... | collective-permute-start | bytes 786440 | tf_op jit(solution)/shard_map/ppermute | solution.py:345

commit v2 on v1

--- a/solution.py
+++ b/solution.py
@@ -14,7 +14,7 @@
 F32 = jnp.float32
 BF16 = jnp.bfloat16
 
-AHEAD = 3
+AHEAD = 2
 LIMIT = 16 * 1024 * 1024
 
 
@@ -61,7 +61,7 @@
 
 
 def upward_kernel(
-    par_ref, pts_hbm, basis_hbm, trans_hbm, coeff_ref, pay_ref, side_ref, pts_ref, basis_ref, trans_ref, sems, *, steps
+    me_ref, pts_hbm, basis_hbm, trans_hbm, coeff_ref, pay_ref, side_ref, pts_ref, basis_ref, trans_ref, sems, *, steps
 ):
     leaves, n, _ = pts_ref.shape
     parents = trans_ref.shape[0]
@@ -109,7 +109,7 @@
             ref[at + FAR + 2 * q] = x[: n // 2]
             ref[at + FAR + 2 * q + 1] = x[n // 2 :]
 
-    odd = par_ref[0] == 1
+    odd = me_ref[0] & 1 == 1
 
     @pl.when(odd)
     def _():
@@ -122,7 +122,7 @@
         edge(pay_ref, parents, False)
 
 
-def upward(par, points, basis, transfer):
+def upward(me, points, basis, transfer):
     leaves, n, _ = points.shape
     parents, rank, _ = transfer.shape
     steps = 2
@@ -148,31 +148,35 @@
         ],
         compiler_params=pltpu.CompilerParams(vmem_limit_bytes=LIMIT),
         name="upward",
-    )(par, *[in_hbm(x) for x in (points, basis, transfer)])
+    )(me, *[in_hbm(x) for x in (points, basis, transfer)])
 
 
 def local_kernel(
-    par_ref, noff_ref, coff_ref, pts_hbm, near_hbm, coup_hbm, coeff_ref, pay_ref, side_ref,
-    near_out, field_out, pts_pad, coeff_pad, near_ref, coup_ref, sems, pts_sem, *, steps
+    me_ref, noff_hbm, coff_hbm, pts_hbm, near_hbm, coup_hbm, coeff_ref, *refs, leafs, base, stride, edges
 ):
+    if edges:
+        pay_ref, side_ref, hop_ref, *refs = refs
+    near_out, field_out, noff_ref, coff_ref, pts_pad, coeff_pad, near_ref, coup_ref, sems, first_sems = refs
     leaves, n, _ = pts_hbm.shape
-    chunk = leaves // steps
-    slots = near_ref.shape[1]
+    steps, chunk, slots = near_ref.shape[:3]
     far_slots = coff_ref.shape[0]
-    halo = side_ref.shape[0]
-    at = pay_ref.shape[0] - halo
     mask = left_half(n // 2, 128)
 
     def copies(i):
-        own = pl.ds(i * chunk, chunk)
+        own = pl.ds(base + stride * i, chunk)
         return (
-            pltpu.make_async_copy(near_hbm.at[own], near_ref.at[own], sems.at[0, i]),
-            pltpu.make_async_copy(coup_hbm.at[own], coup_ref.at[own], sems.at[1, i]),
+            pltpu.make_async_copy(near_hbm.at[own], near_ref.at[i], sems.at[0, i]),
+            pltpu.make_async_copy(coup_hbm.at[own], coup_ref.at[i], sems.at[1, i]),
         )
 
-    points_in = pltpu.make_async_copy(pts_hbm, pts_pad.at[pl.ds(NEAR, leaves)], pts_sem)
-    points_in.start()
-    for i in range(AHEAD):
+    early = (
+        pltpu.make_async_copy(noff_hbm, noff_ref, first_sems.at[0]),
+        pltpu.make_async_copy(coff_hbm, coff_ref, first_sems.at[1]),
+        pltpu.make_async_copy(pts_hbm, pts_pad.at[pl.ds(NEAR, leaves)], first_sems.at[2]),
+    )
+    for c in early:
+        c.start()
+    for i in range(min(AHEAD, steps)):
         for c in copies(i):
             c.start()
 
@@ -187,19 +191,34 @@
             pts_pad[po + q, : n // 2] = ref[at + FAR + 2 * q]
             pts_pad[po + q, n // 2 :] = ref[at + FAR + 2 * q + 1]
 
-    odd = par_ref[0] == 1
-
-    @pl.when(odd)
-    def _():
-        put(pay_ref, at, True)
-        put(side_ref, 0, False)
-
-    @pl.when(jnp.logical_not(odd))
-    def _():
-        put(side_ref, 0, True)
-        put(pay_ref, at, False)
-
-    points_in.wait()
+    if edges:
+        at = pay_ref.shape[0] - side_ref.shape[0]
+        leaf = me_ref[0] & (leafs - 1)
+        odd = leaf & 1 == 1
+
+        def put_side(low):
+            last = leaf == (0 if low else leafs - 1)
+
+            @pl.when(last)
+            def _():
+                put(hop_ref, 0, low)
+
+            @pl.when(jnp.logical_not(last))
+            def _():
+                put(side_ref, 0, low)
+
+        @pl.when(odd)
+        def _():
+            put(pay_ref, at, True)
+            put_side(False)
+
+        @pl.when(jnp.logical_not(odd))
+        def _():
+            put_side(True)
+            put(pay_ref, at, False)
+
+    for c in early:
+        c.wait()
 
     def body(i, carry):
         for c in copies(i):
@@ -212,14 +231,14 @@
 
         nears, fields = [], []
         for j in range(chunk):
-            c = i * chunk + j
+            c = base + stride * i + j
             xs = [pts_pad[c + NEAR + noff_ref[k, c]] for k in range(slots)]
-            ws = [near_ref[c, k] for k in range(slots)]
+            ws = [near_ref[i, j, k] for k in range(slots)]
             nears.append(dot_t(jnp.concatenate(xs, axis=1), jnp.concatenate(ws, axis=1)))
         for j in range(chunk):
-            c = i * chunk + j
+            c = base + stride * i + j
             lhs = beside([coeff_pad[c + FAR + coff_ref[k, c]] for k in range(far_slots)], mask)
-            fields.append(dot_t(lhs, coup_ref[c]))
+            fields.append(dot_t(lhs, coup_ref[i, j]))
         for j in range(chunk):
             near_out[i * chunk + j] = nears[j]
         for j in range(0, chunk, 2):
@@ -229,98 +248,111 @@
     lax.fori_loop(0, steps, body, 0)
 
 
-def local_terms(par, near_offsets, coupling_offsets, points, coeffs, payload, side, near_blocks, leaf_coupling):
+def local_terms(
+    me, near_offsets, coupling_offsets, points, coeffs, halos, near_blocks, leaf_coupling, leafs, base, stride, steps, chunk
+):
     leaves, n, size = points.shape
     rank = leaf_coupling.shape[1]
-    steps = 8
-    tile = side.shape[1:]
+    tile = coeffs.shape[1:]
     smem = pl.BlockSpec(memory_space=pltpu.SMEM)
     vmem = pl.BlockSpec(memory_space=pltpu.VMEM)
     hbm = pl.BlockSpec(memory_space=pltpu.HBM)
     return pl.pallas_call(
-        functools.partial(local_kernel, steps=steps),
+        functools.partial(local_kernel, leafs=leafs, base=base, stride=stride, edges=bool(halos)),
         out_shape=(
-            jax.ShapeDtypeStruct((leaves, n, size), F32),
-            jax.ShapeDtypeStruct((leaves // 2, n, 2 * rank), F32),
+            jax.ShapeDtypeStruct((steps * chunk, n, size), F32),
+            jax.ShapeDtypeStruct((steps * chunk // 2, n, 2 * rank), F32),
         ),
-        in_specs=[smem] * 3 + [hbm] * 3 + [vmem] * 3,
+        in_specs=[smem] + [hbm] * 5 + [vmem] * (1 + len(halos)),
         out_specs=[vmem] * 2,
         scratch_shapes=[
+            pltpu.SMEM(near_offsets.shape, jnp.int32),
+            pltpu.SMEM(coupling_offsets.shape, jnp.int32),
             pltpu.VMEM((leaves + 2 * NEAR, n, size), BF16),
             pltpu.VMEM((leaves + 2 * FAR,) + tile, BF16),
-            pltpu.VMEM(near_blocks.shape, BF16),
-            pltpu.VMEM(leaf_coupling.shape, BF16),
+            pltpu.VMEM((steps, chunk) + near_blocks.shape[1:], BF16),
+            pltpu.VMEM((steps, chunk) + leaf_coupling.shape[1:], BF16),
             pltpu.SemaphoreType.DMA((2, steps)),
-            pltpu.SemaphoreType.DMA,
+            pltpu.SemaphoreType.DMA((3,)),
         ],
         compiler_params=pltpu.CompilerParams(vmem_limit_bytes=LIMIT),
         name="local_terms",
     )(
-        par, near_offsets, coupling_offsets, in_hbm(points), in_hbm(near_blocks), in_hbm(leaf_coupling),
-        coeffs, payload, side,
+        me, *[in_hbm(x) for x in (near_offsets, coupling_offsets, points, near_blocks, leaf_coupling)],
+        coeffs, *halos,
     )
 
 
 def downward_kernel(
-    me_ref, owner_ref, local_ref, table, coup_ref, trans_ref, basis_ref, near_ref, field_ref, out_hbm, out_ref, sems,
-    *, batch
+    place_hbm, table, coup_ref, trans_ref, basis_ref, near_mid, field_mid, near_rim, field_rim, out_hbm,
+    place_ref, out_ref, sems, place_sem, *, batch
 ):
     parents = trans_ref.shape[0]
-    n = near_ref.shape[1]
-    size = near_ref.shape[2]
-    slots = owner_ref.shape[0]
+    n, size = near_mid.shape[1:]
+    slots = place_ref.shape[0]
     mask = left_half(n // 2, 128)
-    me = me_ref[0]
-
-    def copy(step):
-        own = pl.ds(2 * batch * step, 2 * batch)
-        return pltpu.make_async_copy(out_ref.at[own], out_hbm.at[own], sems.at[step])
-
-    def rows(step, carry):
-        own = [step * batch + q for q in range(batch)]
+    rim = field_rim.shape[0] // 2
+    fetch = pltpu.make_async_copy(place_hbm, place_ref, place_sem)
+    fetch.start()
+    fetch.wait()
+
+    def run(own, near_ref, field_ref, at):
         halves = []
         for p in own:
-            tiles = [table[(owner_ref[k, p] ^ me) * parents + local_ref[k, p]] for k in range(slots)]
+            tiles = [table[place_ref[k, p]] for k in range(slots)]
             halves.append(dot_t(beside(tiles, mask), coup_ref[p]).astype(BF16))
-        totals = [
-            (field_ref[p] + dot_n(half, trans_ref[p])).astype(BF16) for p, half in zip(own, halves)
-        ]
+        totals = []
+        for q, (p, half) in enumerate(zip(own, halves)):
+            totals.append((field_ref[at + q] + dot_n(half, trans_ref[p])).astype(BF16))
         fars = []
         for p, total in zip(own, totals):
-            spread = diagonal(basis_ref[2 * p], basis_ref[2 * p + 1])
-            fars.append(dot_n(total, spread))
-        outs = []
-        for p, far in zip(own, fars):
-            outs.append((far[:, :size] + near_ref[2 * p]).astype(BF16))
-            outs.append((far[:, size:] + near_ref[2 * p + 1]).astype(BF16))
-        for q, out in enumerate(outs):
-            out_ref[2 * batch * step + q] = out
-        copy(step).start()
+            fars.append(dot_n(total, diagonal(basis_ref[2 * p], basis_ref[2 * p + 1])))
+        for q, (p, far) in enumerate(zip(own, fars)):
+            out_ref[2 * p] = (far[:, :size] + near_ref[2 * (at + q)]).astype(BF16)
+            out_ref[2 * p + 1] = (far[:, size:] + near_ref[2 * (at + q) + 1]).astype(BF16)
+
+    def copy(first, count, sem):
+        own = pl.ds(2 * first, 2 * count)
+        return pltpu.make_async_copy(out_ref.at[own], out_hbm.at[own], sem)
+
+    def rows(step, carry):
+        first = rim + step * batch
+        run([first + q for q in range(batch)], near_mid, field_mid, step * batch)
+        copy(first, batch, sems.at[step]).start()
         return carry
 
-    lax.fori_loop(0, parents // batch, rows, 0)
-    for step in range(parents // batch):
-        copy(step).wait()
-
-
-def downward(me, owner, local, table, coupling, transfer, basis, near, field):
-    leaves, n, size = near.shape
-    smem = pl.BlockSpec(memory_space=pltpu.SMEM)
+    steps = (parents - 2 * rim) // batch
+    lax.fori_loop(0, steps, rows, 0)
+    run(list(range(rim)) + list(range(parents - rim, parents)), near_rim, field_rim, 0)
+    ends = [copy(0, rim, sems.at[steps]), copy(parents - rim, rim, sems.at[steps + 1])]
+    for c in ends:
+        c.start()
+    for step in range(steps):
+        copy(rim + step * batch, batch, sems.at[step]).wait()
+    for c in ends:
+        c.wait()
+
+
+def downward(place, table, coupling, transfer, basis, mid, rim):
+    leaves, _, size = basis.shape
+    n = mid[0].shape[1]
     vmem = pl.BlockSpec(memory_space=pltpu.VMEM)
-    big = [pltpu.with_memory_space_constraint(x, pltpu.VMEM) for x in (table, coupling, transfer, basis, near, field)]
-    batch = 8
+    big = [pltpu.with_memory_space_constraint(x, pltpu.VMEM) for x in (table, coupling, transfer, basis, *mid, *rim)]
+    batch = mid[1].shape[0] // 2
     return pl.pallas_call(
         functools.partial(downward_kernel, batch=batch),
         out_shape=jax.ShapeDtypeStruct((leaves, n, size), BF16),
-        in_specs=[smem] * 3 + [vmem] * 6,
+        in_specs=[pl.BlockSpec(memory_space=pl.ANY)] + [vmem] * len(big),
         out_specs=pl.BlockSpec(memory_space=pltpu.HBM),
         scratch_shapes=[
+            pltpu.SMEM(place.shape, jnp.int32),
             pltpu.VMEM((leaves, n, size), BF16),
-            pltpu.SemaphoreType.DMA((transfer.shape[0] // batch,)),
+            pltpu.SemaphoreType.DMA((4,)),
+            pltpu.SemaphoreType.DMA,
         ],
         compiler_params=pltpu.CompilerParams(vmem_limit_bytes=LIMIT),
         name="downward",
-    )(me, owner, local, *big)
+    )(place, *big)
 
 
 def on_device(
@@ -339,20 +371,37 @@
     devices = streams * leafs
     parents = transfer.shape[0]
     me = lax.axis_index(AXES).astype(jnp.int32)
-    par = (me % 2).reshape(1)
+    flag = me.reshape(1)
+
+    my_leaf = me % leafs
+
+    def permute(x, pairs):
+        return lax.ppermute(x, AXES, pairs)
 
     def swap(x, bits):
-        return lax.ppermute(x, AXES, [(i, i ^ bits) for i in range(devices)])
-
-    coeffs, payload, side = upward(par, points_rhs, leaf_basis, transfer)
-    odd_pairs = [(i, i + 1) for i in range(1, devices - 1, 2)]
-    side_in = lax.ppermute(side, AXES, odd_pairs + [(b, a) for a, b in odd_pairs])
+        return permute(x, [(i, i ^ bits) for i in range(devices)])
+
+    coeffs, payload, side = upward(flag, points_rhs, leaf_basis, transfer)
 
     got = swap(payload, 1)
     line = [payload[:parents], got[:parents]]
-    line += [swap(line[0], k) for k in range(2, leafs)]
+    sides = None
+    for k in range(2, leafs):
+        if k & (k + 1):
+            line.append(swap(line[0], k))
+            continue
+        both = swap(jnp.concatenate([line[0], side], axis=0), k)
+        line.append(both[:parents])
+        if sides is None:
+            sides = both[parents:]
+        else:
+            away = my_leaf ^ jnp.where(my_leaf % 2 == 1, my_leaf + 1, my_leaf - 1)
+            sides = jnp.where((away == k) | (k == leafs - 1) & (away > k) | (away < 0), both[parents:], sides)
+    ends = [(s * leafs, (s + 1) * leafs) for s in range(streams - 1)]
+    ends += [(s * leafs + leafs - 1, s * leafs - 1) for s in range(1, streams)]
+    hop = permute(sides, ends)
+
     groups = [(0, jnp.concatenate(line[:2], axis=0)), (2, jnp.concatenate(line[2:], axis=0))]
-
     pieces = {}
     for base, group in groups:
         have = {0: group}
@@ -373,12 +422,14 @@
             pieces[s * leafs + base] = g
     table = jnp.concatenate([pieces[k] for k in sorted(pieces)], axis=0)
 
-    near, field = local_terms(
-        par, near_offsets.T, coupling_offsets.T, points_rhs, coeffs, got, side_in, near_blocks, leaf_coupling
-    )
-    return downward(
-        me.reshape(1), parent_owner.T, parent_local.T, table, parent_coupling, transfer, leaf_basis, near, field
-    )
+    leaves = points_rhs.shape[0]
+    rim = 8
+    chunk = (leaves - 2 * rim) // 3
+    args = (flag, near_offsets.T, coupling_offsets.T, points_rhs, coeffs)
+    mid = local_terms(*args, (), near_blocks, leaf_coupling, leafs, rim, chunk, 3, chunk)
+    edge = local_terms(*args, (got, sides, hop), near_blocks, leaf_coupling, leafs, 0, leaves - rim, 2, rim)
+    place = (parent_owner.T ^ me) * parents + parent_local.T
+    return downward(place, table, parent_coupling, transfer, leaf_basis, mid, edge)
 
 
 def solution(mesh):

time: 46.4 us -> 47.5 us (1.024)
  starting transfers between devices: 18.5 us -> 20.7 us
  waiting for transfers between devices: 13.1 us -> 12 us
    ppermute x20, starting transfers between devices: 18.5 us -> 20.7 us  [permute(): return lax.ppermute(x, AXES, pairs)]
    ppermute x20, waiting for transfers between devices: 13.1 us -> 12 us  [permute(): return lax.ppermute(x, AXES, pairs)]
    pallas_call x1 -> x2, Pallas kernels: 6.94 us -> 7.61 us  [local_terms(): pl.pallas_call(functools.partial(local_kernel, leafs=leafs, base=base, st...]
    pallas_call x1, Pallas kernels: 3.81 us -> 3.18 us  [downward(): pl.pallas_call(functools.partial(downward_kernel, batch=batch), out_shape...]
  transfers between devices with their start and end apart: 20 -> 20, of which waited for: 9 -> 8; matrix products, arithmetic and copies ran while one was open for 2% -> 2% of each run, Pallas kernels for 15% -> 16%
where the time goes in v2:
time: 47.5 us; the launch traced here: 47.3 us
  starting transfers between devices  20.7 us (44%)
  Pallas kernels  13.5 us (28%)
  waiting for transfers between devices  12 us (25%)
  local copies, waits for them, and re-layouts  0.73 us (2%)
    ppermute x20, starting transfers between devices, permute(): return lax.ppermute(x, AXES, pairs)  20.7 us
    ppermute x20, waiting for transfers between devices, permute(): return lax.ppermute(x, AXES, pairs)  12 us
    pallas_call x2, Pallas kernels, local_terms(): pl.pallas_call(functools.partial(local_kernel, leafs=leafs, base=base, st...  7.61 us
    pallas_call x1, Pallas kernels, downward(): pl.pallas_call(functools.partial(downward_kernel, batch=batch), out_shape...  3.18 us
    pallas_call x1, Pallas kernels, upward(): pl.pallas_call(functools.partial(upward_kernel, steps=steps), out_shape=(...  2.67 us
  transfers between devices with their start and end apart: 20, of which 8 were waited for; matrix products, arithmetic and copies ran while one was open for 2% of the time, Pallas kernels for 16%

profile of v2, /device:TPU:0, one launch (start us, length us, event | category | flops | bytes accessed | tf_op | source)
XLA Modules:
  0.0 47.3 jit_solution(9089201013047786356)
XLA Ops:
  0.0 2.7 %upward.1 = (bf16[64,16,128]{2,1,0:T(8,128)(2,1)S(1)}, bf16[41,16,128]{2,1,0:T(8,128)(2,1)S(1)}, bf16[9,16,128]{2,1,0:T(8,128)(2,1)S(1)}) custom-call(s32[1]{0:T(128)} %bitcast.1.me_ref, bf16[64,32,128]{2,1,0:T(8,128)(2,1)} %pts_hbm.5, bf16[64,64,128]{2,1,0:T(8,128)(2,1)} %basis_ref.1, bf16[32,64,128]{2,1,0:T(8,128)(2,1)} %trans_ref.1), custom_call_target="tpu_custom_call" | custom-call | tf_op jit(solution)/shard_map/upward/pallas_call | solution.py:134
  2.7 3.1 %collective-permute-start = (bf16[41,16,128]{2,1,0:T(8,128)(2,1)S(1)}, bf16[41,16,128]{2,1,0:T(8,128)(2,1)S(1)}, u32[]{:S(2)}, u32[]{:S(2)}) collective-permute-start(bf16[41,16,128]{2,1,0:T(8,128)(2,1)S(1)} %get-tuple-element.12), channel_id=1, source_target_pairs={{0,1},{1,0},{2,3},{3,2},{4,5},{5,4},{6,7},{7,6},{8,9},{9,8},{10,11... | collective-permute-start | bytes 503816 | tf_op jit(solution)/shard_map/ppermute | solution.py:379
  5.8 2.7 %collective-permute-start.1 = (bf16[32,16,128]{2,1,0:T(8,128)(2,1)S(1)}, bf16[32,16,128]{2,1,0:T(8,128)(2,1)S(1)}, u32[]{:S(2)}, u32[]{:S(2)}) collective-permute-start(bf16[32,16,128]{2,1,0:T(8,128)(2,1)S(1)} %get-tuple-element.23), channel_id=1, source_target_pairs={{0,2},{1,3},{2,0},{3,1},{4,6},{5,7},{6,4},{7,5},{8,10},{9,11},{10,... | collective-permute-start | bytes 393224 | tf_op jit(solution)/shard_map/ppermute | solution.py:379
  8.5 0.1 collective-permute-start.2
  8.6 3.5 %collective-permute-done.refs_0_ = bf16[41,16,128]{2,1,0:T(8,128)(2,1)S(1)} collective-permute-done((bf16[41,16,128]{2,1,0:T(8,128)(2,1)S(1)}, bf16[41,16,128]{2,1,0:T(8,128)(2,1)S(1)}, u32[]{:S(2)}, u32[]{:S(2)}) %collective-permute-start) | collective-permute-done | bytes 167968 | tf_op jit(solution)/shard_map/ppermute | solution.py:379
  12.2 1.8 %collective-permute-start.5 = (bf16[64,16,128]{2,1,0:T(8,128)(2,1)S(1)}, bf16[64,16,128]{2,1,0:T(8,128)(2,1)S(1)}, u32[]{:S(2)}, u32[]{:S(2)}) collective-permute-start(bf16[64,16,128]{2,1,0:T(8,128)(2,1)S(1)} %pad_maximum_fusion), channel_id=1, source_target_pairs={{0,8},{1,9},{2,10},{3,11},{4,12},{5,13},{6,14},{7,15},{8,0},{9,1},... | collective-permute-start | bytes 786440 | tf_op jit(solution)/shard_map/ppermute | solution.py:379
  14.0 1.5 %collective-permute-start.9 = (bf16[64,16,128]{2,1,0:T(8,128)(2,1)S(1)}, bf16[64,16,128]{2,1,0:T(8,128)(2,1)S(1)}, u32[]{:S(2)}, u32[]{:S(2)}) collective-permute-start(bf16[64,16,128]{2,1,0:T(8,128)(2,1)S(1)} %pad_maximum_fusion), channel_id=1, source_target_pairs={{0,16},{1,17},{2,18},{3,19},{4,20},{5,21},{6,22},{7,23},{8,24},{9,... | collective-permute-start | bytes 786440 | tf_op jit(solution)/shard_map/ppermute | solution.py:379
  15.5 3.3 %collective-permute-done.2 = bf16[41,16,128]{2,1,0:T(8,128)(2,1)S(1)} collective-permute-done((bf16[41,16,128]{2,1,0:T(8,128)(2,1)S(1)}, bf16[41,16,128]{2,1,0:T(8,128)(2,1)S(1)}, u32[]{:S(2)}, u32[]{:S(2)}) %collective-permute-start.2) | collective-permute-done | bytes 167968 | tf_op jit(solution)/shard_map/ppermute | solution.py:379
  18.8 1.3 %collective-permute-start.19 = (bf16[9,16,128]{2,1,0:T(8,128)(2,1)S(1)}, bf16[9,16,128]{2,1,0:T(8,128)(2,1)S(1)}, u32[]{:S(2)}, u32[]{:S(2)}) collective-permute-start(bf16[9,16,128]{2,1,0:T(8,128)(2,1)S(1)} %slice.38.refs_1_), channel_id=1, source_target_pairs={{0,4},{4,8},{8,12},{12,16},{16,20},{20,24},{24,28},{7,3},{11,7},{1... | collective-permute-start | bytes 110600 | tf_op jit(solution)/shard_map/ppermute | solution.py:379
  20.1 0.0 collective-permute-done.1
  20.2 2.2 %collective-permute-start.10 = (bf16[64,16,128]{2,1,0:T(8,128)(2,1)S(1)}, bf16[64,16,128]{2,1,0:T(8,128)(2,1)S(1)}, u32[]{:S(2)}, u32[]{:S(2)}) collective-permute-start(bf16[64,16,128]{2,1,0:T(8,128)(2,1)S(1)} %pad_maximum_fusion.1), channel_id=1, source_target_pairs={{0,16},{1,17},{2,18},{3,19},{4,20},{5,21},{6,22},{7,23},{8,24},{9,... | collective-permute-start | bytes 786440 | tf_op jit(solution)/shard_map/ppermute | solution.py:379
  22.4 1.5 %collective-permute-start.6 = (bf16[64,16,128]{2,1,0:T(8,128)(2,1)S(1)}, bf16[64,16,128]{2,1,0:T(8,128)(2,1)S(1)}, u32[]{:S(2)}, u32[]{:S(2)}) collective-permute-start(bf16[64,16,128]{2,1,0:T(8,128)(2,1)S(1)} %pad_maximum_fusion.1), channel_id=1, source_target_pairs={{0,8},{1,9},{2,10},{3,11},{4,12},{5,13},{6,14},{7,15},{8,0},{9,1},... | collective-permute-start | bytes 786440 | tf_op jit(solution)/shard_map/ppermute | solution.py:379
  23.9 0.0 collective-permute-done.19.refs_2_
  23.9 0.0 collective-permute-start.3
  23.9 0.0 copy-start.3
  23.9 0.0 copy-start.4
  23.9 4.9 %local_terms.2 = (f32[48,32,128]{2,1,0:T(8,128)S(1)}, f32[24,32,128]{2,1,0:T(8,128)S(1)}) custom-call(s32[1]{0:T(128)} %bitcast.1.me_ref, s32[3,64]{1,0:T(4,128)} %bitcast.5, s32[4,64]{1,0:T(4,128)} %bitcast.7, bf16[64,32,128]{2,1,0:T(8,128)(2,1)} %pts_hbm.5, bf16[64,3,128,128]{3,2,1,0:T(8,128)(2,1)} %near_hbm.3, bf16[64,64,256]{2,1,0:T(8,128)(2,1)} %coup_hbm.3, ...), custom_call_target="tpu_custom_call" | custom-call | tf_op jit(solution)/shard_map/local_terms/pallas_call | solution.py:260
  28.8 0.0 collective-permute-done.9
  28.8 0.6 %collective-permute-start.4 = (bf16[64,16,128]{2,1,0:T(8,128)(2,1)S(1)}, bf16[64,16,128]{2,1,0:T(8,128)(2,1)S(1)}, u32[]{:S(2)}, u32[]{:S(2)}) collective-permute-start(bf16[64,16,128]{2,1,0:T(8,128)(2,1)S(1)} %pad_maximum_fusion.1), channel_id=1, source_target_pairs={{0,4},{1,5},{2,6},{3,7},{4,0},{5,1},{6,2},{7,3},{8,12},{9,13},{10,... | collective-permute-start | bytes 786440 | tf_op jit(solution)/shard_map/ppermute | solution.py:379
  29.4 0.0 copy-done.3
  29.4 0.0 copy-done.4
  29.4 2.7 %local_terms.3 = (f32[16,32,128]{2,1,0:T(8,128)S(1)}, f32[8,32,128]{2,1,0:T(8,128)S(1)}) custom-call(s32[1]{0:T(128)} %bitcast.1.me_ref, s32[3,64]{1,0:T(4,128)} %bitcast.6, s32[4,64]{1,0:T(4,128)} %bitcast.8, bf16[64,32,128]{2,1,0:T(8,128)(2,1)} %pts_hbm.5, bf16[64,3,128,128]{3,2,1,0:T(8,128)(2,1)} %near_hbm.3, bf16[64,64,256]{2,1,0:T(8,128)(2,1)} %coup_hbm.3, ...), custom_call_target="tpu_custom_call" | custom-call | tf_op jit(solution)/shard_map/local_terms/pallas_call | solution.py:260
  32.2 0.0 collective-permute-done.5
  32.2 1.7 %collective-permute-start.13 = (bf16[32,16,128]{2,1,0:T(8,128)(2,1)S(1)}, bf16[32,16,128]{2,1,0:T(8,128)(2,1)S(1)}, u32[]{:S(2)}, u32[]{:S(2)}) collective-permute-start(bf16[32,16,128]{2,1,0:T(8,128)(2,1)S(1)} %slice.34), channel_id=1, source_target_pairs={{0,8},{1,9},{2,10},{3,11},{4,12},{5,13},{6,14},{7,15},{8,0},{9,1},... | collective-permute-start | bytes 393224 | tf_op jit(solution)/shard_map/ppermute | solution.py:379
  33.9 0.0 collective-permute-done.10
  33.9 1.6 %collective-permute-start.14 = (bf16[32,16,128]{2,1,0:T(8,128)(2,1)S(1)}, bf16[32,16,128]{2,1,0:T(8,128)(2,1)S(1)}, u32[]{:S(2)}, u32[]{:S(2)}) collective-permute-start(bf16[32,16,128]{2,1,0:T(8,128)(2,1)S(1)} %slice.35), channel_id=1, source_target_pairs={{0,16},{1,17},{2,18},{3,19},{4,20},{5,21},{6,22},{7,23},{8,24},{9,... | collective-permute-start | bytes 393224 | tf_op jit(solution)/shard_map/ppermute | solution.py:379
  35.5 0.0 collective-permute-done.6
  35.5 1.6 %collective-permute-start.15 = (bf16[32,16,128]{2,1,0:T(8,128)(2,1)S(1)}, bf16[32,16,128]{2,1,0:T(8,128)(2,1)S(1)}, u32[]{:S(2)}, u32[]{:S(2)}) collective-permute-start(bf16[32,16,128]{2,1,0:T(8,128)(2,1)S(1)} %slice.36), channel_id=1, source_target_pairs={{0,8},{1,9},{2,10},{3,11},{4,12},{5,13},{6,14},{7,15},{8,0},{9,1},... | collective-permute-start | bytes 393224 | tf_op jit(solution)/shard_map/ppermute | solution.py:379
  37.1 0.0 collective-permute-done.3
  37.1 0.1 collective-permute-start.16
  37.2 0.0 copy-start
  37.2 0.0 copy-start.1
  37.2 0.0 copy-start.2
  37.3 0.0 collective-permute-done.4
  37.3 0.1 collective-permute-start.7
  37.5 0.2 collective-permute-done.13
  37.7 0.4 collective-permute-start.8
  38.1 1.3 %collective-permute-done.14 = bf16[32,16,128]{2,1,0:T(8,128)(2,1)S(1)} collective-permute-done((bf16[32,16,128]{2,1,0:T(8,128)(2,1)S(1)}, bf16[32,16,128]{2,1,0:T(8,128)(2,1)S(1)}, u32[]{:S(2)}, u32[]{:S(2)}) %collective-permute-start.14) | collective-permute-done | bytes 131104 | tf_op jit(solution)/shard_map/ppermute | solution.py:379
  39.4 0.0 collective-permute-start.11
  39.4 1.1 %collective-permute-done.15 = bf16[32,16,128]{2,1,0:T(8,128)(2,1)S(1)} collective-permute-done((bf16[32,16,128]{2,1,0:T(8,128)(2,1)S(1)}, bf16[32,16,128]{2,1,0:T(8,128)(2,1)S(1)}, u32[]{:S(2)}, u32[]{:S(2)}) %collective-permute-start.15) | collective-permute-done | bytes 131104 | tf_op jit(solution)/shard_map/ppermute | solution.py:379
  40.5 0.0 collective-permute-start.12
  40.5 1.6 %collective-permute-done.16 = bf16[32,16,128]{2,1,0:T(8,128)(2,1)S(1)} collective-permute-done((bf16[32,16,128]{2,1,0:T(8,128)(2,1)S(1)}, bf16[32,16,128]{2,1,0:T(8,128)(2,1)S(1)}, u32[]{:S(2)}, u32[]{:S(2)}) %collective-permute-start.16) | collective-permute-done | bytes 131104 | tf_op jit(solution)/shard_map/ppermute | solution.py:379
  42.2 0.0 collective-permute-start.17
  42.2 0.0 collective-permute-done.7
  42.2 0.6 %collective-permute-start.18 = (bf16[64,16,128]{2,1,0:T(8,128)(2,1)S(1)}, bf16[64,16,128]{2,1,0:T(8,128)(2,1)S(1)}, u32[]{:S(2)}, u32[]{:S(2)}) collective-permute-start(bf16[64,16,128]{2,1,0:T(8,128)(2,1)S(1)} %pad_maximum_fusion.3), channel_id=1, source_target_pairs={{0,4},{1,5},{2,6},{3,7},{4,0},{5,1},{6,2},{7,3},{8,12},{9,13},{10,... | collective-permute-start | bytes 786440 | tf_op jit(solution)/shard_map/ppermute | solution.py:379
  42.8 0.0 collective-permute-done.8
  43.0 0.0 collective-permute-done.11
  43.0 0.0 collective-permute-done.12
  43.2 0.5 %collective-permute-done.17 = bf16[64,16,128]{2,1,0:T(8,128)(2,1)S(1)} collective-permute-done((bf16[64,16,128]{2,1,0:T(8,128)(2,1)S(1)}, bf16[64,16,128]{2,1,0:T(8,128)(2,1)S(1)}, u32[]{:S(2)}, u32[]{:S(2)}) %collective-permute-start.17) | collective-permute-done | bytes 262176 | tf_op jit(solution)/shard_map/ppermute | solution.py:379
  43.7 0.3 collective-permute-done.18
  44.1 0.0 copy-done
  44.1 0.0 copy-done.1
  44.1 0.0 copy-done.2
  44.1 3.2 %downward.1 = bf16[64,32,128]{2,1,0:T(8,128)(2,1)} custom-call(s32[8,32]{1,0:T(8,128)S(1)} %add_bitcast_fusion.place_hbm, bf16[1024,16,128]{2,1,0:T(8,128)(2,1)S(1)} %constant_dynamic-update-slice_fusion.table, bf16[32,64,512]{2,1,0:T(8,128)(2,1)S(1)} %copy-done.2, bf16[32,64,128]{2,1,0:T(8,128)(2,1)S(1)} %copy-done.1, bf16[64,64,128]{2,1,0:T(8,128)(2,1)S(1)} %copy-done, ...), custom_call_target="tpu_custom_call" | custom-call | tf_op jit(solution)/shard_map/downward/pallas_call | solution.py:342
  (31 shorter events, 0.8 us)
Async XLA Ops:
  2.7 9.4 %collective-permute-start = (bf16[41,16,128]{2,1,0:T(8,128)(2,1)S(1)}, bf16[41,16,128]{2,1,0:T(8,128)(2,1)S(1)}, u32[]{:S(2)}, u32[]{:S(2)}) collective-permute-start(bf16[41,16,128]{2,1,0:T(8,128)(2,1)S(1)} %get-tuple-element.12), channel_id=1, source_target_pairs={{0,1},{1,0},{2,3},{3,2},{4,5},{5,4},{6,7},{7,6},{8,9},{9,8},{10,11... | collective-permute-start | bytes 503816 | tf_op jit(solution)/shard_map/ppermute | solution.py:379
  5.8 14.3 %collective-permute-start.1 = (bf16[32,16,128]{2,1,0:T(8,128)(2,1)S(1)}, bf16[32,16,128]{2,1,0:T(8,128)(2,1)S(1)}, u32[]{:S(2)}, u32[]{:S(2)}) collective-permute-start(bf16[32,16,128]{2,1,0:T(8,128)(2,1)S(1)} %get-tuple-element.23), channel_id=1, source_target_pairs={{0,2},{1,3},{2,0},{3,1},{4,6},{5,7},{6,4},{7,5},{8,10},{9,11},{10,... | collective-permute-start | bytes 393224 | tf_op jit(solution)/shard_map/ppermute | solution.py:379
  8.5 10.3 %collective-permute-start.2 = (bf16[41,16,128]{2,1,0:T(8,128)(2,1)S(1)}, bf16[41,16,128]{2,1,0:T(8,128)(2,1)S(1)}, u32[]{:S(2)}, u32[]{:S(2)}) collective-permute-start(bf16[41,16,128]{2,1,0:T(8,128)(2,1)S(1)} %pad_maximum_fusion.4), channel_id=1, source_target_pairs={{0,3},{1,2},{2,1},{3,0},{4,7},{5,6},{6,5},{7,4},{8,11},{9,10},{10,... | collective-permute-start | bytes 503816 | tf_op jit(solution)/shard_map/ppermute | solution.py:379
  12.2 20.0 %collective-permute-start.5 = (bf16[64,16,128]{2,1,0:T(8,128)(2,1)S(1)}, bf16[64,16,128]{2,1,0:T(8,128)(2,1)S(1)}, u32[]{:S(2)}, u32[]{:S(2)}) collective-permute-start(bf16[64,16,128]{2,1,0:T(8,128)(2,1)S(1)} %pad_maximum_fusion), channel_id=1, source_target_pairs={{0,8},{1,9},{2,10},{3,11},{4,12},{5,13},{6,14},{7,15},{8,0},{9,1},... | collective-permute-start | bytes 786440 | tf_op jit(solution)/shard_map/ppermute | solution.py:379
  14.0 14.8 %collective-permute-start.9 = (bf16[64,16,128]{2,1,0:T(8,128)(2,1)S(1)}, bf16[64,16,128]{2,1,0:T(8,128)(2,1)S(1)}, u32[]{:S(2)}, u32[]{:S(2)}) collective-permute-start(bf16[64,16,128]{2,1,0:T(8,128)(2,1)S(1)} %pad_maximum_fusion), channel_id=1, source_target_pairs={{0,16},{1,17},{2,18},{3,19},{4,20},{5,21},{6,22},{7,23},{8,24},{9,... | collective-permute-start | bytes 786440 | tf_op jit(solution)/shard_map/ppermute | solution.py:379
  18.8 5.1 %collective-permute-start.19 = (bf16[9,16,128]{2,1,0:T(8,128)(2,1)S(1)}, bf16[9,16,128]{2,1,0:T(8,128)(2,1)S(1)}, u32[]{:S(2)}, u32[]{:S(2)}) collective-permute-start(bf16[9,16,128]{2,1,0:T(8,128)(2,1)S(1)} %slice.38.refs_1_), channel_id=1, source_target_pairs={{0,4},{4,8},{8,12},{12,16},{16,20},{20,24},{24,28},{7,3},{11,7},{1... | collective-permute-start | bytes 110600 | tf_op jit(solution)/shard_map/ppermute | solution.py:379
  20.2 13.7 %collective-permute-start.10 = (bf16[64,16,128]{2,1,0:T(8,128)(2,1)S(1)}, bf16[64,16,128]{2,1,0:T(8,128)(2,1)S(1)}, u32[]{:S(2)}, u32[]{:S(2)}) collective-permute-start(bf16[64,16,128]{2,1,0:T(8,128)(2,1)S(1)} %pad_maximum_fusion.1), channel_id=1, source_target_pairs={{0,16},{1,17},{2,18},{3,19},{4,20},{5,21},{6,22},{7,23},{8,24},{9,... | collective-permute-start | bytes 786440 | tf_op jit(solution)/shard_map/ppermute | solution.py:379
  22.4 13.1 %collective-permute-start.6 = (bf16[64,16,128]{2,1,0:T(8,128)(2,1)S(1)}, bf16[64,16,128]{2,1,0:T(8,128)(2,1)S(1)}, u32[]{:S(2)}, u32[]{:S(2)}) collective-permute-start(bf16[64,16,128]{2,1,0:T(8,128)(2,1)S(1)} %pad_maximum_fusion.1), channel_id=1, source_target_pairs={{0,8},{1,9},{2,10},{3,11},{4,12},{5,13},{6,14},{7,15},{8,0},{9,1},... | collective-permute-start | bytes 786440 | tf_op jit(solution)/shard_map/ppermute | solution.py:379
  23.9 13.2 %collective-permute-start.3 = (bf16[64,16,128]{2,1,0:T(8,128)(2,1)S(1)}, bf16[64,16,128]{2,1,0:T(8,128)(2,1)S(1)}, u32[]{:S(2)}, u32[]{:S(2)}) collective-permute-start(bf16[64,16,128]{2,1,0:T(8,128)(2,1)S(1)} %pad_maximum_fusion), channel_id=1, source_target_pairs={{0,4},{1,5},{2,6},{3,7},{4,0},{5,1},{6,2},{7,3},{8,12},{9,13},{10,... | collective-permute-start | bytes 786440 | tf_op jit(solution)/shard_map/ppermute | solution.py:379
  23.9 5.5 %copy-start.3 = (s32[32,8]{0,1:T(8,128)S(1)}, s32[32,8]{0,1:T(8,128)}, u32[]{:S(2)}) copy-start(s32[32,8]{0,1:T(8,128)} %param.19) | copy-start | bytes 3076
  23.9 5.5 %copy-start.4 = (s32[32,8]{0,1:T(8,128)S(1)}, s32[32,8]{0,1:T(8,128)}, u32[]{:S(2)}) copy-start(s32[32,8]{0,1:T(8,128)} %param.18) | copy-start | bytes 3076
  28.8 8.5 %collective-permute-start.4 = (bf16[64,16,128]{2,1,0:T(8,128)(2,1)S(1)}, bf16[64,16,128]{2,1,0:T(8,128)(2,1)S(1)}, u32[]{:S(2)}, u32[]{:S(2)}) collective-permute-start(bf16[64,16,128]{2,1,0:T(8,128)(2,1)S(1)} %pad_maximum_fusion.1), channel_id=1, source_target_pairs={{0,4},{1,5},{2,6},{3,7},{4,0},{5,1},{6,2},{7,3},{8,12},{9,13},{10,... | collective-permute-start | bytes 786440 | tf_op jit(solution)/shard_map/ppermute | solution.py:379
  32.2 5.5 %collective-permute-start.13 = (bf16[32,16,128]{2,1,0:T(8,128)(2,1)S(1)}, bf16[32,16,128]{2,1,0:T(8,128)(2,1)S(1)}, u32[]{:S(2)}, u32[]{:S(2)}) collective-permute-start(bf16[32,16,128]{2,1,0:T(8,128)(2,1)S(1)} %slice.34), channel_id=1, source_target_pairs={{0,8},{1,9},{2,10},{3,11},{4,12},{5,13},{6,14},{7,15},{8,0},{9,1},... | collective-permute-start | bytes 393224 | tf_op jit(solution)/shard_map/ppermute | solution.py:379
  33.9 5.5 %collective-permute-start.14 = (bf16[32,16,128]{2,1,0:T(8,128)(2,1)S(1)}, bf16[32,16,128]{2,1,0:T(8,128)(2,1)S(1)}, u32[]{:S(2)}, u32[]{:S(2)}) collective-permute-start(bf16[32,16,128]{2,1,0:T(8,128)(2,1)S(1)} %slice.35), channel_id=1, source_target_pairs={{0,16},{1,17},{2,18},{3,19},{4,20},{5,21},{6,22},{7,23},{8,24},{9,... | collective-permute-start | bytes 393224 | tf_op jit(solution)/shard_map/ppermute | solution.py:379
  35.5 5.0 %collective-permute-start.15 = (bf16[32,16,128]{2,1,0:T(8,128)(2,1)S(1)}, bf16[32,16,128]{2,1,0:T(8,128)(2,1)S(1)}, u32[]{:S(2)}, u32[]{:S(2)}) collective-permute-start(bf16[32,16,128]{2,1,0:T(8,128)(2,1)S(1)} %slice.36), channel_id=1, source_target_pairs={{0,8},{1,9},{2,10},{3,11},{4,12},{5,13},{6,14},{7,15},{8,0},{9,1},... | collective-permute-start | bytes 393224 | tf_op jit(solution)/shard_map/ppermute | solution.py:379
  37.1 5.0 %collective-permute-start.16 = (bf16[32,16,128]{2,1,0:T(8,128)(2,1)S(1)}, bf16[32,16,128]{2,1,0:T(8,128)(2,1)S(1)}, u32[]{:S(2)}, u32[]{:S(2)}) collective-permute-start(bf16[32,16,128]{2,1,0:T(8,128)(2,1)S(1)} %slice.37), channel_id=1, source_target_pairs={{0,16},{1,17},{2,18},{3,19},{4,20},{5,21},{6,22},{7,23},{8,24},{9,... | collective-permute-start | bytes 393224 | tf_op jit(solution)/shard_map/ppermute | solution.py:379
  37.2 6.9 %copy-start = (bf16[64,64,128]{2,1,0:T(8,128)(2,1)S(1)}, bf16[64,64,128]{2,1,0:T(8,128)(2,1)}, u32[]{:S(2)}) copy-start(bf16[64,64,128]{2,1,0:T(8,128)(2,1)} %basis_ref.1) | copy-start | bytes 3145732
  37.2 6.9 %copy-start.1 = (bf16[32,64,128]{2,1,0:T(8,128)(2,1)S(1)}, bf16[32,64,128]{2,1,0:T(8,128)(2,1)}, u32[]{:S(2)}) copy-start(bf16[32,64,128]{2,1,0:T(8,128)(2,1)} %trans_ref.1) | copy-start | bytes 1572868
  37.2 6.9 %copy-start.2 = (bf16[32,64,512]{2,1,0:T(8,128)(2,1)S(1)}, bf16[32,64,512]{2,1,0:T(8,128)(2,1)}, u32[]{:S(2)}) copy-start(bf16[32,64,512]{2,1,0:T(8,128)(2,1)} %coup_ref.1) | copy-start | bytes 6291460
  37.3 4.9 %collective-permute-start.7 = (bf16[64,16,128]{2,1,0:T(8,128)(2,1)S(1)}, bf16[64,16,128]{2,1,0:T(8,128)(2,1)S(1)}, u32[]{:S(2)}, u32[]{:S(2)}) collective-permute-start(bf16[64,16,128]{2,1,0:T(8,128)(2,1)S(1)} %collective-permute-done.5), channel_id=1, source_target_pairs={{0,4},{1,5},{2,6},{3,7},{4,0},{5,1},{6,2},{7,3},{8,12},{9,13},{10,... | collective-permute-start | bytes 786440 | tf_op jit(solution)/shard_map/ppermute | solution.py:379
  37.7 5.1 %collective-permute-start.8 = (bf16[64,16,128]{2,1,0:T(8,128)(2,1)S(1)}, bf16[64,16,128]{2,1,0:T(8,128)(2,1)S(1)}, u32[]{:S(2)}, u32[]{:S(2)}) collective-permute-start(bf16[64,16,128]{2,1,0:T(8,128)(2,1)S(1)} %collective-permute-done.6), channel_id=1, source_target_pairs={{0,4},{1,5},{2,6},{3,7},{4,0},{5,1},{6,2},{7,3},{8,12},{9,13},{10,... | collective-permute-start | bytes 786440 | tf_op jit(solution)/shard_map/ppermute | solution.py:379
  39.4 3.6 %collective-permute-start.11 = (bf16[64,16,128]{2,1,0:T(8,128)(2,1)S(1)}, bf16[64,16,128]{2,1,0:T(8,128)(2,1)S(1)}, u32[]{:S(2)}, u32[]{:S(2)}) collective-permute-start(bf16[64,16,128]{2,1,0:T(8,128)(2,1)S(1)} %collective-permute-done.9), channel_id=1, source_target_pairs={{0,4},{1,5},{2,6},{3,7},{4,0},{5,1},{6,2},{7,3},{8,12},{9,13},{10,... | collective-permute-start | bytes 786440 | tf_op jit(solution)/shard_map/ppermute | solution.py:379
  40.5 2.5 %collective-permute-start.12 = (bf16[64,16,128]{2,1,0:T(8,128)(2,1)S(1)}, bf16[64,16,128]{2,1,0:T(8,128)(2,1)S(1)}, u32[]{:S(2)}, u32[]{:S(2)}) collective-permute-start(bf16[64,16,128]{2,1,0:T(8,128)(2,1)S(1)} %collective-permute-done.10), channel_id=1, source_target_pairs={{0,4},{1,5},{2,6},{3,7},{4,0},{5,1},{6,2},{7,3},{8,12},{9,13},{10,... | collective-permute-start | bytes 786440 | tf_op jit(solution)/shard_map/ppermute | solution.py:379
  42.2 1.5 %collective-permute-start.17 = (bf16[64,16,128]{2,1,0:T(8,128)(2,1)S(1)}, bf16[64,16,128]{2,1,0:T(8,128)(2,1)S(1)}, u32[]{:S(2)}, u32[]{:S(2)}) collective-permute-start(bf16[64,16,128]{2,1,0:T(8,128)(2,1)S(1)} %pad_maximum_fusion.2), channel_id=1, source_target_pairs={{0,4},{1,5},{2,6},{3,7},{4,0},{5,1},{6,2},{7,3},{8,12},{9,13},{10,... | collective-permute-start | bytes 786440 | tf_op jit(solution)/shard_map/ppermute | solution.py:379
  42.2 1.9 %collective-permute-start.18 = (bf16[64,16,128]{2,1,0:T(8,128)(2,1)S(1)}, bf16[64,16,128]{2,1,0:T(8,128)(2,1)S(1)}, u32[]{:S(2)}, u32[]{:S(2)}) collective-permute-start(bf16[64,16,128]{2,1,0:T(8,128)(2,1)S(1)} %pad_maximum_fusion.3), channel_id=1, source_target_pairs={{0,4},{1,5},{2,6},{3,7},{4,0},{5,1},{6,2},{7,3},{8,12},{9,13},{10,... | collective-permute-start | bytes 786440 | tf_op jit(solution)/shard_map/ppermute | solution.py:379

commit v3 on v2

--- a/solution.py
+++ b/solution.py
@@ -61,7 +61,8 @@
 
 
 def upward_kernel(
-    me_ref, pts_hbm, basis_hbm, trans_hbm, coeff_ref, pay_ref, side_ref, pts_ref, basis_ref, trans_ref, sems, *, steps
+    me_ref, pts_hbm, basis_hbm, trans_hbm, owner_hbm, local_hbm, coeff_ref, pay_ref, side_ref, place_ref,
+    pts_ref, basis_ref, trans_ref, owner_ref, local_ref, sems, place_sems, *, steps
 ):
     leaves, n, _ = pts_ref.shape
     parents = trans_ref.shape[0]
@@ -79,7 +80,13 @@
 
     for i in range(steps):
         for c in copies(i):
-            c.start()
+            c.start(priority=min(i, 1))
+    listed = (
+        pltpu.make_async_copy(owner_hbm, owner_ref, place_sems.at[0]),
+        pltpu.make_async_copy(local_hbm, local_ref, place_sems.at[1]),
+    )
+    for c in listed:
+        c.start(priority=1)
 
     for i in range(steps):
         for c in copies(i):
@@ -121,8 +128,12 @@
         edge(side_ref, 0, True)
         edge(pay_ref, parents, False)
 
-
-def upward(me, points, basis, transfer):
+    for c in listed:
+        c.wait()
+    place_ref[...] = (owner_ref[...] ^ me_ref[0]) * parents + local_ref[...]
+
+
+def upward(me, points, basis, transfer, owner, local):
     leaves, n, _ = points.shape
     parents, rank, _ = transfer.shape
     steps = 2
@@ -137,18 +148,22 @@
             jax.ShapeDtypeStruct((leaves,) + tile, BF16),
             jax.ShapeDtypeStruct((parents + halo,) + tile, BF16),
             jax.ShapeDtypeStruct((halo,) + tile, BF16),
+            jax.ShapeDtypeStruct(owner.shape, jnp.int32),
         ),
-        in_specs=[smem] + [hbm] * 3,
-        out_specs=[vmem] * 3,
+        in_specs=[smem] + [hbm] * 5,
+        out_specs=[vmem] * 4,
         scratch_shapes=[
             pltpu.VMEM(points.shape, BF16),
             pltpu.VMEM(basis.shape, BF16),
             pltpu.VMEM(transfer.shape, BF16),
+            pltpu.VMEM(owner.shape, jnp.int32),
+            pltpu.VMEM(owner.shape, jnp.int32),
             pltpu.SemaphoreType.DMA((3, steps)),
+            pltpu.SemaphoreType.DMA((2,)),
         ],
         compiler_params=pltpu.CompilerParams(vmem_limit_bytes=LIMIT),
         name="upward",
-    )(me, *[in_hbm(x) for x in (points, basis, transfer)])
+    )(me, *[in_hbm(x) for x in (points, basis, transfer, owner, local)])
 
 
 def local_kernel(
@@ -381,7 +396,7 @@
     def swap(x, bits):
         return permute(x, [(i, i ^ bits) for i in range(devices)])
 
-    coeffs, payload, side = upward(flag, points_rhs, leaf_basis, transfer)
+    coeffs, payload, side, place = upward(flag, points_rhs, leaf_basis, transfer, parent_owner.T, parent_local.T)
 
     got = swap(payload, 1)
     line = [payload[:parents], got[:parents]]
@@ -401,22 +416,26 @@
     ends += [(s * leafs + leafs - 1, s * leafs - 1) for s in range(1, streams)]
     hop = permute(sides, ends)
 
-    groups = [(0, jnp.concatenate(line[:2], axis=0)), (2, jnp.concatenate(line[2:], axis=0))]
+    def join(parts):
+        return parts[0] if len(parts) == 1 else jnp.concatenate(parts, axis=0)
+
+    groups = [(0, [join(line[:2])]), (2, [join(line[2:])])]
     pieces = {}
-    for base, group in groups:
-        have = {0: group}
+    for base, parts in groups:
+        have = {0: parts}
         for s in range(2, streams, 2):
             low = s & -s
             high = 1 << (s.bit_length() - 1)
             if low == high:
-                have[s] = swap(have[s ^ low], s * leafs)
-            else:
-                rows = group.shape[0] // 2
-                have[s] = jnp.concatenate(
-                    [swap(have[s ^ low][:rows], low * leafs), swap(have[s ^ high][rows:], high * leafs)],
-                    axis=0,
-                )
+                have[s] = [swap(x, s * leafs) for x in have[s ^ low]]
+                continue
+            near, far = have[s ^ low], have[s ^ high]
+            if len(near) == 1:
+                rows = near[0].shape[0] // 2
+                near, far = (near[0][:rows], None), (None, far[0][rows:])
+            have[s] = [swap(far[j], high * leafs) if j % 2 else swap(near[j], low * leafs) for j in range(len(near))]
         for s in list(have):
+            have[s] = join(have[s])
             have[s ^ 1] = swap(have[s], leafs)
         for s, g in have.items():
             pieces[s * leafs + base] = g
@@ -428,7 +447,6 @@
     args = (flag, near_offsets.T, coupling_offsets.T, points_rhs, coeffs)
     mid = local_terms(*args, (), near_blocks, leaf_coupling, leafs, rim, chunk, 3, chunk)
     edge = local_terms(*args, (got, sides, hop), near_blocks, leaf_coupling, leafs, 0, leaves - rim, 2, rim)
-    place = (parent_owner.T ^ me) * parents + parent_local.T
     return downward(place, table, parent_coupling, transfer, leaf_basis, mid, edge)
 
 

time: 47.5 us -> 47.4 us (level)
  no operation moved by 1% of the time
where the time goes in v3:
time: 47.4 us; the launch traced here: 47.2 us
  starting transfers between devices  20.5 us (43%)
  Pallas kernels  13.5 us (28%)
  waiting for transfers between devices  12.1 us (26%)
  local copies, waits for them, and re-layouts  0.72 us (2%)
    ppermute x20, starting transfers between devices, permute(): return lax.ppermute(x, AXES, pairs)  20.5 us
    ppermute x20, waiting for transfers between devices, permute(): return lax.ppermute(x, AXES, pairs)  12.1 us
    pallas_call x2, Pallas kernels, local_terms(): pl.pallas_call(functools.partial(local_kernel, leafs=leafs, base=base, st...  7.6 us
    pallas_call x1, Pallas kernels, downward(): pl.pallas_call(functools.partial(downward_kernel, batch=batch), out_shape...  3.19 us
    pallas_call x1, Pallas kernels, upward(): pl.pallas_call(functools.partial(upward_kernel, steps=steps), out_shape=(...  2.7 us
  transfers between devices with their start and end apart: 20, of which 8 were waited for; matrix products, arithmetic and copies ran while one was open for 2% of the time, Pallas kernels for 16%

profile of v3, /device:TPU:0, one launch (start us, length us, event | category | flops | bytes accessed | tf_op | source)
XLA Modules:
  0.0 47.2 jit_solution(1774947449381721028)
XLA Ops:
  0.0 2.7 %upward.1 = (bf16[64,16,128]{2,1,0:T(8,128)(2,1)S(1)}, bf16[41,16,128]{2,1,0:T(8,128)(2,1)S(1)}, bf16[9,16,128]{2,1,0:T(8,128)(2,1)S(1)}, s32[8,32]{1,0:T(8,128)S(1)}) custom-call(s32[1]{0:T(128)} %bitcast.me_ref, bf16[64,32,128]{2,1,0:T(8,128)(2,1)} %pts_hbm.5, bf16[64,64,128]{2,1,0:T(8,128)(2,1)} %basis_ref.1, bf16[32,64,128]{2,1,0:T(8,128)(2,1)} %trans_ref.1, ...), custom_call_target="tpu_custom_call" | custom-call | tf_op jit(solution)/shard_map/upward/pallas_call | solution.py:145
  2.7 3.1 %collective-permute-start = (bf16[41,16,128]{2,1,0:T(8,128)(2,1)S(1)}, bf16[41,16,128]{2,1,0:T(8,128)(2,1)S(1)}, u32[]{:S(2)}, u32[]{:S(2)}) collective-permute-start(bf16[41,16,128]{2,1,0:T(8,128)(2,1)S(1)} %get-tuple-element.14), channel_id=1, source_target_pairs={{0,1},{1,0},{2,3},{3,2},{4,5},{5,4},{6,7},{7,6},{8,9},{9,8},{10,11... | collective-permute-start | bytes 503816 | tf_op jit(solution)/shard_map/ppermute | solution.py:394
  5.9 2.7 %collective-permute-start.1 = (bf16[32,16,128]{2,1,0:T(8,128)(2,1)S(1)}, bf16[32,16,128]{2,1,0:T(8,128)(2,1)S(1)}, u32[]{:S(2)}, u32[]{:S(2)}) collective-permute-start(bf16[32,16,128]{2,1,0:T(8,128)(2,1)S(1)} %get-tuple-element.25), channel_id=1, source_target_pairs={{0,2},{1,3},{2,0},{3,1},{4,6},{5,7},{6,4},{7,5},{8,10},{9,11},{10,... | collective-permute-start | bytes 393224 | tf_op jit(solution)/shard_map/ppermute | solution.py:394
  8.5 0.1 collective-permute-start.2
  8.6 3.5 %collective-permute-done.refs_0_ = bf16[41,16,128]{2,1,0:T(8,128)(2,1)S(1)} collective-permute-done((bf16[41,16,128]{2,1,0:T(8,128)(2,1)S(1)}, bf16[41,16,128]{2,1,0:T(8,128)(2,1)S(1)}, u32[]{:S(2)}, u32[]{:S(2)}) %collective-permute-start) | collective-permute-done | bytes 167968 | tf_op jit(solution)/shard_map/ppermute | solution.py:394
  12.2 1.8 %collective-permute-start.5 = (bf16[64,16,128]{2,1,0:T(8,128)(2,1)S(1)}, bf16[64,16,128]{2,1,0:T(8,128)(2,1)S(1)}, u32[]{:S(2)}, u32[]{:S(2)}) collective-permute-start(bf16[64,16,128]{2,1,0:T(8,128)(2,1)S(1)} %pad_maximum_fusion), channel_id=1, source_target_pairs={{0,8},{1,9},{2,10},{3,11},{4,12},{5,13},{6,14},{7,15},{8,0},{9,1},... | collective-permute-start | bytes 786440 | tf_op jit(solution)/shard_map/ppermute | solution.py:394
  14.0 1.5 %collective-permute-start.9 = (bf16[64,16,128]{2,1,0:T(8,128)(2,1)S(1)}, bf16[64,16,128]{2,1,0:T(8,128)(2,1)S(1)}, u32[]{:S(2)}, u32[]{:S(2)}) collective-permute-start(bf16[64,16,128]{2,1,0:T(8,128)(2,1)S(1)} %pad_maximum_fusion), channel_id=1, source_target_pairs={{0,16},{1,17},{2,18},{3,19},{4,20},{5,21},{6,22},{7,23},{8,24},{9,... | collective-permute-start | bytes 786440 | tf_op jit(solution)/shard_map/ppermute | solution.py:394
  15.5 3.3 %collective-permute-done.2 = bf16[41,16,128]{2,1,0:T(8,128)(2,1)S(1)} collective-permute-done((bf16[41,16,128]{2,1,0:T(8,128)(2,1)S(1)}, bf16[41,16,128]{2,1,0:T(8,128)(2,1)S(1)}, u32[]{:S(2)}, u32[]{:S(2)}) %collective-permute-start.2) | collective-permute-done | bytes 167968 | tf_op jit(solution)/shard_map/ppermute | solution.py:394
  18.8 1.3 %collective-permute-start.19 = (bf16[9,16,128]{2,1,0:T(8,128)(2,1)S(1)}, bf16[9,16,128]{2,1,0:T(8,128)(2,1)S(1)}, u32[]{:S(2)}, u32[]{:S(2)}) collective-permute-start(bf16[9,16,128]{2,1,0:T(8,128)(2,1)S(1)} %slice.38.refs_1_), channel_id=1, source_target_pairs={{0,4},{4,8},{8,12},{12,16},{16,20},{20,24},{24,28},{7,3},{11,7},{1... | collective-permute-start | bytes 110600 | tf_op jit(solution)/shard_map/ppermute | solution.py:394
  20.1 0.0 collective-permute-done.1
  20.2 2.2 %collective-permute-start.10 = (bf16[64,16,128]{2,1,0:T(8,128)(2,1)S(1)}, bf16[64,16,128]{2,1,0:T(8,128)(2,1)S(1)}, u32[]{:S(2)}, u32[]{:S(2)}) collective-permute-start(bf16[64,16,128]{2,1,0:T(8,128)(2,1)S(1)} %pad_maximum_fusion.1), channel_id=1, source_target_pairs={{0,16},{1,17},{2,18},{3,19},{4,20},{5,21},{6,22},{7,23},{8,24},{9,... | collective-permute-start | bytes 786440 | tf_op jit(solution)/shard_map/ppermute | solution.py:394
  22.4 1.5 %collective-permute-start.6 = (bf16[64,16,128]{2,1,0:T(8,128)(2,1)S(1)}, bf16[64,16,128]{2,1,0:T(8,128)(2,1)S(1)}, u32[]{:S(2)}, u32[]{:S(2)}) collective-permute-start(bf16[64,16,128]{2,1,0:T(8,128)(2,1)S(1)} %pad_maximum_fusion.1), channel_id=1, source_target_pairs={{0,8},{1,9},{2,10},{3,11},{4,12},{5,13},{6,14},{7,15},{8,0},{9,1},... | collective-permute-start | bytes 786440 | tf_op jit(solution)/shard_map/ppermute | solution.py:394
  23.9 0.0 collective-permute-done.19.refs_2_
  23.9 0.0 collective-permute-start.3
  23.9 0.0 collective-permute-done.9
  23.9 0.5 %collective-permute-start.4 = (bf16[64,16,128]{2,1,0:T(8,128)(2,1)S(1)}, bf16[64,16,128]{2,1,0:T(8,128)(2,1)S(1)}, u32[]{:S(2)}, u32[]{:S(2)}) collective-permute-start(bf16[64,16,128]{2,1,0:T(8,128)(2,1)S(1)} %pad_maximum_fusion.1), channel_id=1, source_target_pairs={{0,4},{1,5},{2,6},{3,7},{4,0},{5,1},{6,2},{7,3},{8,12},{9,13},{10,... | collective-permute-start | bytes 786440 | tf_op jit(solution)/shard_map/ppermute | solution.py:394
  24.4 4.9 %local_terms.2 = (f32[48,32,128]{2,1,0:T(8,128)S(1)}, f32[24,32,128]{2,1,0:T(8,128)S(1)}) custom-call(s32[1]{0:T(128)} %bitcast.me_ref, s32[3,64]{1,0:T(4,128)} %bitcast.5, s32[4,64]{1,0:T(4,128)} %bitcast.7, bf16[64,32,128]{2,1,0:T(8,128)(2,1)} %pts_hbm.5, bf16[64,3,128,128]{3,2,1,0:T(8,128)(2,1)} %near_hbm.3, bf16[64,64,256]{2,1,0:T(8,128)(2,1)} %coup_hbm.3, ...), custom_call_target="tpu_custom_call" | custom-call | tf_op jit(solution)/shard_map/local_terms/pallas_call | solution.py:275
  29.3 2.7 %local_terms.3 = (f32[16,32,128]{2,1,0:T(8,128)S(1)}, f32[8,32,128]{2,1,0:T(8,128)S(1)}) custom-call(s32[1]{0:T(128)} %bitcast.me_ref, s32[3,64]{1,0:T(4,128)} %bitcast.6, s32[4,64]{1,0:T(4,128)} %bitcast.8, bf16[64,32,128]{2,1,0:T(8,128)(2,1)} %pts_hbm.5, bf16[64,3,128,128]{3,2,1,0:T(8,128)(2,1)} %near_hbm.3, bf16[64,64,256]{2,1,0:T(8,128)(2,1)} %coup_hbm.3, ...), custom_call_target="tpu_custom_call" | custom-call | tf_op jit(solution)/shard_map/local_terms/pallas_call | solution.py:275
  32.1 0.0 collective-permute-done.5
  32.1 1.7 %collective-permute-start.13 = (bf16[32,16,128]{2,1,0:T(8,128)(2,1)S(1)}, bf16[32,16,128]{2,1,0:T(8,128)(2,1)S(1)}, u32[]{:S(2)}, u32[]{:S(2)}) collective-permute-start(bf16[32,16,128]{2,1,0:T(8,128)(2,1)S(1)} %slice.34), channel_id=1, source_target_pairs={{0,8},{1,9},{2,10},{3,11},{4,12},{5,13},{6,14},{7,15},{8,0},{9,1},... | collective-permute-start | bytes 393224 | tf_op jit(solution)/shard_map/ppermute | solution.py:394
  33.8 0.0 collective-permute-done.10
  33.8 1.6 %collective-permute-start.14 = (bf16[32,16,128]{2,1,0:T(8,128)(2,1)S(1)}, bf16[32,16,128]{2,1,0:T(8,128)(2,1)S(1)}, u32[]{:S(2)}, u32[]{:S(2)}) collective-permute-start(bf16[32,16,128]{2,1,0:T(8,128)(2,1)S(1)} %slice.35), channel_id=1, source_target_pairs={{0,16},{1,17},{2,18},{3,19},{4,20},{5,21},{6,22},{7,23},{8,24},{9,... | collective-permute-start | bytes 393224 | tf_op jit(solution)/shard_map/ppermute | solution.py:394
  35.4 0.0 collective-permute-done.6
  35.4 1.6 %collective-permute-start.15 = (bf16[32,16,128]{2,1,0:T(8,128)(2,1)S(1)}, bf16[32,16,128]{2,1,0:T(8,128)(2,1)S(1)}, u32[]{:S(2)}, u32[]{:S(2)}) collective-permute-start(bf16[32,16,128]{2,1,0:T(8,128)(2,1)S(1)} %slice.36), channel_id=1, source_target_pairs={{0,8},{1,9},{2,10},{3,11},{4,12},{5,13},{6,14},{7,15},{8,0},{9,1},... | collective-permute-start | bytes 393224 | tf_op jit(solution)/shard_map/ppermute | solution.py:394
  37.0 0.0 collective-permute-done.3
  37.0 0.1 collective-permute-start.16
  37.1 0.0 copy-start
  37.1 0.0 copy-start.1
  37.1 0.0 copy-start.2
  37.2 0.0 collective-permute-done.4
  37.2 0.1 collective-permute-start.7
  37.4 0.3 collective-permute-done.13
  37.7 0.3 collective-permute-start.8
  38.0 1.3 %collective-permute-done.14 = bf16[32,16,128]{2,1,0:T(8,128)(2,1)S(1)} collective-permute-done((bf16[32,16,128]{2,1,0:T(8,128)(2,1)S(1)}, bf16[32,16,128]{2,1,0:T(8,128)(2,1)S(1)}, u32[]{:S(2)}, u32[]{:S(2)}) %collective-permute-start.14) | collective-permute-done | bytes 131104 | tf_op jit(solution)/shard_map/ppermute | solution.py:394
  39.3 0.0 collective-permute-start.11
  39.3 1.1 %collective-permute-done.15 = bf16[32,16,128]{2,1,0:T(8,128)(2,1)S(1)} collective-permute-done((bf16[32,16,128]{2,1,0:T(8,128)(2,1)S(1)}, bf16[32,16,128]{2,1,0:T(8,128)(2,1)S(1)}, u32[]{:S(2)}, u32[]{:S(2)}) %collective-permute-start.15) | collective-permute-done | bytes 131104 | tf_op jit(solution)/shard_map/ppermute | solution.py:394
  40.5 0.0 collective-permute-start.12
  40.5 1.6 %collective-permute-done.16 = bf16[32,16,128]{2,1,0:T(8,128)(2,1)S(1)} collective-permute-done((bf16[32,16,128]{2,1,0:T(8,128)(2,1)S(1)}, bf16[32,16,128]{2,1,0:T(8,128)(2,1)S(1)}, u32[]{:S(2)}, u32[]{:S(2)}) %collective-permute-start.16) | collective-permute-done | bytes 131104 | tf_op jit(solution)/shard_map/ppermute | solution.py:394
  42.1 0.0 collective-permute-start.17
  42.1 0.0 collective-permute-done.7
  42.1 0.6 %collective-permute-start.18 = (bf16[64,16,128]{2,1,0:T(8,128)(2,1)S(1)}, bf16[64,16,128]{2,1,0:T(8,128)(2,1)S(1)}, u32[]{:S(2)}, u32[]{:S(2)}) collective-permute-start(bf16[64,16,128]{2,1,0:T(8,128)(2,1)S(1)} %pad_maximum_fusion.3), channel_id=1, source_target_pairs={{0,4},{1,5},{2,6},{3,7},{4,0},{5,1},{6,2},{7,3},{8,12},{9,13},{10,... | collective-permute-start | bytes 786440 | tf_op jit(solution)/shard_map/ppermute | solution.py:394
  42.7 0.0 collective-permute-done.8
  42.9 0.0 collective-permute-done.11
  42.9 0.0 collective-permute-done.12
  43.1 0.5 %collective-permute-done.17 = bf16[64,16,128]{2,1,0:T(8,128)(2,1)S(1)} collective-permute-done((bf16[64,16,128]{2,1,0:T(8,128)(2,1)S(1)}, bf16[64,16,128]{2,1,0:T(8,128)(2,1)S(1)}, u32[]{:S(2)}, u32[]{:S(2)}) %collective-permute-start.17) | collective-permute-done | bytes 262176 | tf_op jit(solution)/shard_map/ppermute | solution.py:394
  43.7 0.3 collective-permute-done.18
  44.0 0.0 copy-done
  44.0 0.0 copy-done.1
  44.0 0.0 copy-done.2
  44.1 3.2 %downward.1 = bf16[64,32,128]{2,1,0:T(8,128)(2,1)} custom-call(s32[8,32]{1,0:T(8,128)S(1)} %get-tuple-element.13.place_hbm, bf16[1024,16,128]{2,1,0:T(8,128)(2,1)S(1)} %constant_dynamic-update-slice_fusion.table, bf16[32,64,512]{2,1,0:T(8,128)(2,1)S(1)} %copy-done.2, bf16[32,64,128]{2,1,0:T(8,128)(2,1)S(1)} %copy-done.1, bf16[64,64,128]{2,1,0:T(8,128)(2,1)S(1)} %copy-done, ...), custom_call_target="tpu_custom_call" | custom-call | tf_op jit(solution)/shard_map/downward/pallas_call | solution.py:357
  (30 shorter events, 0.8 us)
Async XLA Ops:
  2.7 9.4 %collective-permute-start = (bf16[41,16,128]{2,1,0:T(8,128)(2,1)S(1)}, bf16[41,16,128]{2,1,0:T(8,128)(2,1)S(1)}, u32[]{:S(2)}, u32[]{:S(2)}) collective-permute-start(bf16[41,16,128]{2,1,0:T(8,128)(2,1)S(1)} %get-tuple-element.14), channel_id=1, source_target_pairs={{0,1},{1,0},{2,3},{3,2},{4,5},{5,4},{6,7},{7,6},{8,9},{9,8},{10,11... | collective-permute-start | bytes 503816 | tf_op jit(solution)/shard_map/ppermute | solution.py:394
  5.9 14.3 %collective-permute-start.1 = (bf16[32,16,128]{2,1,0:T(8,128)(2,1)S(1)}, bf16[32,16,128]{2,1,0:T(8,128)(2,1)S(1)}, u32[]{:S(2)}, u32[]{:S(2)}) collective-permute-start(bf16[32,16,128]{2,1,0:T(8,128)(2,1)S(1)} %get-tuple-element.25), channel_id=1, source_target_pairs={{0,2},{1,3},{2,0},{3,1},{4,6},{5,7},{6,4},{7,5},{8,10},{9,11},{10,... | collective-permute-start | bytes 393224 | tf_op jit(solution)/shard_map/ppermute | solution.py:394
  8.5 10.3 %collective-permute-start.2 = (bf16[41,16,128]{2,1,0:T(8,128)(2,1)S(1)}, bf16[41,16,128]{2,1,0:T(8,128)(2,1)S(1)}, u32[]{:S(2)}, u32[]{:S(2)}) collective-permute-start(bf16[41,16,128]{2,1,0:T(8,128)(2,1)S(1)} %pad_maximum_fusion.4), channel_id=1, source_target_pairs={{0,3},{1,2},{2,1},{3,0},{4,7},{5,6},{6,5},{7,4},{8,11},{9,10},{10,... | collective-permute-start | bytes 503816 | tf_op jit(solution)/shard_map/ppermute | solution.py:394
  12.2 19.9 %collective-permute-start.5 = (bf16[64,16,128]{2,1,0:T(8,128)(2,1)S(1)}, bf16[64,16,128]{2,1,0:T(8,128)(2,1)S(1)}, u32[]{:S(2)}, u32[]{:S(2)}) collective-permute-start(bf16[64,16,128]{2,1,0:T(8,128)(2,1)S(1)} %pad_maximum_fusion), channel_id=1, source_target_pairs={{0,8},{1,9},{2,10},{3,11},{4,12},{5,13},{6,14},{7,15},{8,0},{9,1},... | collective-permute-start | bytes 786440 | tf_op jit(solution)/shard_map/ppermute | solution.py:394
  14.0 9.9 %collective-permute-start.9 = (bf16[64,16,128]{2,1,0:T(8,128)(2,1)S(1)}, bf16[64,16,128]{2,1,0:T(8,128)(2,1)S(1)}, u32[]{:S(2)}, u32[]{:S(2)}) collective-permute-start(bf16[64,16,128]{2,1,0:T(8,128)(2,1)S(1)} %pad_maximum_fusion), channel_id=1, source_target_pairs={{0,16},{1,17},{2,18},{3,19},{4,20},{5,21},{6,22},{7,23},{8,24},{9,... | collective-permute-start | bytes 786440 | tf_op jit(solution)/shard_map/ppermute | solution.py:394
  18.8 5.1 %collective-permute-start.19 = (bf16[9,16,128]{2,1,0:T(8,128)(2,1)S(1)}, bf16[9,16,128]{2,1,0:T(8,128)(2,1)S(1)}, u32[]{:S(2)}, u32[]{:S(2)}) collective-permute-start(bf16[9,16,128]{2,1,0:T(8,128)(2,1)S(1)} %slice.38.refs_1_), channel_id=1, source_target_pairs={{0,4},{4,8},{8,12},{12,16},{16,20},{20,24},{24,28},{7,3},{11,7},{1... | collective-permute-start | bytes 110600 | tf_op jit(solution)/shard_map/ppermute | solution.py:394
  20.2 13.6 %collective-permute-start.10 = (bf16[64,16,128]{2,1,0:T(8,128)(2,1)S(1)}, bf16[64,16,128]{2,1,0:T(8,128)(2,1)S(1)}, u32[]{:S(2)}, u32[]{:S(2)}) collective-permute-start(bf16[64,16,128]{2,1,0:T(8,128)(2,1)S(1)} %pad_maximum_fusion.1), channel_id=1, source_target_pairs={{0,16},{1,17},{2,18},{3,19},{4,20},{5,21},{6,22},{7,23},{8,24},{9,... | collective-permute-start | bytes 786440 | tf_op jit(solution)/shard_map/ppermute | solution.py:394
  22.4 13.0 %collective-permute-start.6 = (bf16[64,16,128]{2,1,0:T(8,128)(2,1)S(1)}, bf16[64,16,128]{2,1,0:T(8,128)(2,1)S(1)}, u32[]{:S(2)}, u32[]{:S(2)}) collective-permute-start(bf16[64,16,128]{2,1,0:T(8,128)(2,1)S(1)} %pad_maximum_fusion.1), channel_id=1, source_target_pairs={{0,8},{1,9},{2,10},{3,11},{4,12},{5,13},{6,14},{7,15},{8,0},{9,1},... | collective-permute-start | bytes 786440 | tf_op jit(solution)/shard_map/ppermute | solution.py:394
  23.9 13.1 %collective-permute-start.3 = (bf16[64,16,128]{2,1,0:T(8,128)(2,1)S(1)}, bf16[64,16,128]{2,1,0:T(8,128)(2,1)S(1)}, u32[]{:S(2)}, u32[]{:S(2)}) collective-permute-start(bf16[64,16,128]{2,1,0:T(8,128)(2,1)S(1)} %pad_maximum_fusion), channel_id=1, source_target_pairs={{0,4},{1,5},{2,6},{3,7},{4,0},{5,1},{6,2},{7,3},{8,12},{9,13},{10,... | collective-permute-start | bytes 786440 | tf_op jit(solution)/shard_map/ppermute | solution.py:394
  23.9 13.3 %collective-permute-start.4 = (bf16[64,16,128]{2,1,0:T(8,128)(2,1)S(1)}, bf16[64,16,128]{2,1,0:T(8,128)(2,1)S(1)}, u32[]{:S(2)}, u32[]{:S(2)}) collective-permute-start(bf16[64,16,128]{2,1,0:T(8,128)(2,1)S(1)} %pad_maximum_fusion.1), channel_id=1, source_target_pairs={{0,4},{1,5},{2,6},{3,7},{4,0},{5,1},{6,2},{7,3},{8,12},{9,13},{10,... | collective-permute-start | bytes 786440 | tf_op jit(solution)/shard_map/ppermute | solution.py:394
  32.1 5.6 %collective-permute-start.13 = (bf16[32,16,128]{2,1,0:T(8,128)(2,1)S(1)}, bf16[32,16,128]{2,1,0:T(8,128)(2,1)S(1)}, u32[]{:S(2)}, u32[]{:S(2)}) collective-permute-start(bf16[32,16,128]{2,1,0:T(8,128)(2,1)S(1)} %slice.34), channel_id=1, source_target_pairs={{0,8},{1,9},{2,10},{3,11},{4,12},{5,13},{6,14},{7,15},{8,0},{9,1},... | collective-permute-start | bytes 393224 | tf_op jit(solution)/shard_map/ppermute | solution.py:394
  33.8 5.5 %collective-permute-start.14 = (bf16[32,16,128]{2,1,0:T(8,128)(2,1)S(1)}, bf16[32,16,128]{2,1,0:T(8,128)(2,1)S(1)}, u32[]{:S(2)}, u32[]{:S(2)}) collective-permute-start(bf16[32,16,128]{2,1,0:T(8,128)(2,1)S(1)} %slice.35), channel_id=1, source_target_pairs={{0,16},{1,17},{2,18},{3,19},{4,20},{5,21},{6,22},{7,23},{8,24},{9,... | collective-permute-start | bytes 393224 | tf_op jit(solution)/shard_map/ppermute | solution.py:394
  35.4 5.0 %collective-permute-start.15 = (bf16[32,16,128]{2,1,0:T(8,128)(2,1)S(1)}, bf16[32,16,128]{2,1,0:T(8,128)(2,1)S(1)}, u32[]{:S(2)}, u32[]{:S(2)}) collective-permute-start(bf16[32,16,128]{2,1,0:T(8,128)(2,1)S(1)} %slice.36), channel_id=1, source_target_pairs={{0,8},{1,9},{2,10},{3,11},{4,12},{5,13},{6,14},{7,15},{8,0},{9,1},... | collective-permute-start | bytes 393224 | tf_op jit(solution)/shard_map/ppermute | solution.py:394
  37.0 5.0 %collective-permute-start.16 = (bf16[32,16,128]{2,1,0:T(8,128)(2,1)S(1)}, bf16[32,16,128]{2,1,0:T(8,128)(2,1)S(1)}, u32[]{:S(2)}, u32[]{:S(2)}) collective-permute-start(bf16[32,16,128]{2,1,0:T(8,128)(2,1)S(1)} %slice.37), channel_id=1, source_target_pairs={{0,16},{1,17},{2,18},{3,19},{4,20},{5,21},{6,22},{7,23},{8,24},{9,... | collective-permute-start | bytes 393224 | tf_op jit(solution)/shard_map/ppermute | solution.py:394
  37.1 6.9 %copy-start = (bf16[64,64,128]{2,1,0:T(8,128)(2,1)S(1)}, bf16[64,64,128]{2,1,0:T(8,128)(2,1)}, u32[]{:S(2)}) copy-start(bf16[64,64,128]{2,1,0:T(8,128)(2,1)} %basis_ref.1) | copy-start | bytes 3145732
  37.1 6.9 %copy-start.1 = (bf16[32,64,128]{2,1,0:T(8,128)(2,1)S(1)}, bf16[32,64,128]{2,1,0:T(8,128)(2,1)}, u32[]{:S(2)}) copy-start(bf16[32,64,128]{2,1,0:T(8,128)(2,1)} %trans_ref.1) | copy-start | bytes 1572868
  37.1 6.9 %copy-start.2 = (bf16[32,64,512]{2,1,0:T(8,128)(2,1)S(1)}, bf16[32,64,512]{2,1,0:T(8,128)(2,1)}, u32[]{:S(2)}) copy-start(bf16[32,64,512]{2,1,0:T(8,128)(2,1)} %coup_ref.1) | copy-start | bytes 6291460
  37.2 4.9 %collective-permute-start.7 = (bf16[64,16,128]{2,1,0:T(8,128)(2,1)S(1)}, bf16[64,16,128]{2,1,0:T(8,128)(2,1)S(1)}, u32[]{:S(2)}, u32[]{:S(2)}) collective-permute-start(bf16[64,16,128]{2,1,0:T(8,128)(2,1)S(1)} %collective-permute-done.5), channel_id=1, source_target_pairs={{0,4},{1,5},{2,6},{3,7},{4,0},{5,1},{6,2},{7,3},{8,12},{9,13},{10,... | collective-permute-start | bytes 786440 | tf_op jit(solution)/shard_map/ppermute | solution.py:394
  37.7 5.0 %collective-permute-start.8 = (bf16[64,16,128]{2,1,0:T(8,128)(2,1)S(1)}, bf16[64,16,128]{2,1,0:T(8,128)(2,1)S(1)}, u32[]{:S(2)}, u32[]{:S(2)}) collective-permute-start(bf16[64,16,128]{2,1,0:T(8,128)(2,1)S(1)} %collective-permute-done.6), channel_id=1, source_target_pairs={{0,4},{1,5},{2,6},{3,7},{4,0},{5,1},{6,2},{7,3},{8,12},{9,13},{10,... | collective-permute-start | bytes 786440 | tf_op jit(solution)/shard_map/ppermute | solution.py:394
  39.3 3.6 %collective-permute-start.11 = (bf16[64,16,128]{2,1,0:T(8,128)(2,1)S(1)}, bf16[64,16,128]{2,1,0:T(8,128)(2,1)S(1)}, u32[]{:S(2)}, u32[]{:S(2)}) collective-permute-start(bf16[64,16,128]{2,1,0:T(8,128)(2,1)S(1)} %collective-permute-done.9), channel_id=1, source_target_pairs={{0,4},{1,5},{2,6},{3,7},{4,0},{5,1},{6,2},{7,3},{8,12},{9,13},{10,... | collective-permute-start | bytes 786440 | tf_op jit(solution)/shard_map/ppermute | solution.py:394
  40.5 2.5 %collective-permute-start.12 = (bf16[64,16,128]{2,1,0:T(8,128)(2,1)S(1)}, bf16[64,16,128]{2,1,0:T(8,128)(2,1)S(1)}, u32[]{:S(2)}, u32[]{:S(2)}) collective-permute-start(bf16[64,16,128]{2,1,0:T(8,128)(2,1)S(1)} %collective-permute-done.10), channel_id=1, source_target_pairs={{0,4},{1,5},{2,6},{3,7},{4,0},{5,1},{6,2},{7,3},{8,12},{9,13},{10,... | collective-permute-start | bytes 786440 | tf_op jit(solution)/shard_map/ppermute | solution.py:394
  42.1 1.5 %collective-permute-start.17 = (bf16[64,16,128]{2,1,0:T(8,128)(2,1)S(1)}, bf16[64,16,128]{2,1,0:T(8,128)(2,1)S(1)}, u32[]{:S(2)}, u32[]{:S(2)}) collective-permute-start(bf16[64,16,128]{2,1,0:T(8,128)(2,1)S(1)} %pad_maximum_fusion.2), channel_id=1, source_target_pairs={{0,4},{1,5},{2,6},{3,7},{4,0},{5,1},{6,2},{7,3},{8,12},{9,13},{10,... | collective-permute-start | bytes 786440 | tf_op jit(solution)/shard_map/ppermute | solution.py:394
  42.1 1.9 %collective-permute-start.18 = (bf16[64,16,128]{2,1,0:T(8,128)(2,1)S(1)}, bf16[64,16,128]{2,1,0:T(8,128)(2,1)S(1)}, u32[]{:S(2)}, u32[]{:S(2)}) collective-permute-start(bf16[64,16,128]{2,1,0:T(8,128)(2,1)S(1)} %pad_maximum_fusion.3), channel_id=1, source_target_pairs={{0,4},{1,5},{2,6},{3,7},{4,0},{5,1},{6,2},{7,3},{8,12},{9,13},{10,... | collective-permute-start | bytes 786440 | tf_op jit(solution)/shard_map/ppermute | solution.py:394

commit v4 on v3

--- a/solution.py
+++ b/solution.py
@@ -61,7 +61,7 @@
 
 
 def upward_kernel(
-    me_ref, pts_hbm, basis_hbm, trans_hbm, owner_hbm, local_hbm, coeff_ref, pay_ref, side_ref, place_ref,
+    me_ref, pts_hbm, basis_hbm, trans_hbm, owner_hbm, local_hbm, coeff_ref, pay_ref, edge_ref, side_ref, place_ref,
     pts_ref, basis_ref, trans_ref, owner_ref, local_ref, sems, place_sems, *, steps
 ):
     leaves, n, _ = pts_ref.shape
@@ -106,27 +106,27 @@
             p = own[2 * q]
             pay_ref[p], pay_ref[p + 1] = dense(up, mask)
 
-    def edge(ref, at, first):
+    def edge(ref, first):
         lo = 0 if first else leaves - FAR
         for q in range(FAR):
-            ref[at + q] = coeff_ref[lo + q]
+            ref[q] = coeff_ref[lo + q]
         lo = 0 if first else leaves - NEAR
         for q in range(NEAR):
             x = pts_ref[lo + q]
-            ref[at + FAR + 2 * q] = x[: n // 2]
-            ref[at + FAR + 2 * q + 1] = x[n // 2 :]
+            ref[FAR + 2 * q] = x[: n // 2]
+            ref[FAR + 2 * q + 1] = x[n // 2 :]
 
     odd = me_ref[0] & 1 == 1
 
     @pl.when(odd)
     def _():
-        edge(pay_ref, parents, True)
-        edge(side_ref, 0, False)
+        edge(edge_ref, True)
+        edge(side_ref, False)
 
     @pl.when(jnp.logical_not(odd))
     def _():
-        edge(side_ref, 0, True)
-        edge(pay_ref, parents, False)
+        edge(side_ref, True)
+        edge(edge_ref, False)
 
     for c in listed:
         c.wait()
@@ -146,12 +146,13 @@
         functools.partial(upward_kernel, steps=steps),
         out_shape=(
             jax.ShapeDtypeStruct((leaves,) + tile, BF16),
-            jax.ShapeDtypeStruct((parents + halo,) + tile, BF16),
+            jax.ShapeDtypeStruct((parents,) + tile, BF16),
+            jax.ShapeDtypeStruct((halo,) + tile, BF16),
             jax.ShapeDtypeStruct((halo,) + tile, BF16),
             jax.ShapeDtypeStruct(owner.shape, jnp.int32),
         ),
         in_specs=[smem] + [hbm] * 5,
-        out_specs=[vmem] * 4,
+        out_specs=[vmem] * 5,
         scratch_shapes=[
             pltpu.VMEM(points.shape, BF16),
             pltpu.VMEM(basis.shape, BF16),
@@ -170,7 +171,7 @@
     me_ref, noff_hbm, coff_hbm, pts_hbm, near_hbm, coup_hbm, coeff_ref, *refs, leafs, base, stride, edges
 ):
     if edges:
-        pay_ref, side_ref, hop_ref, *refs = refs
+        edge_ref, side_ref, hop_ref, *refs = refs
     near_out, field_out, noff_ref, coff_ref, pts_pad, coeff_pad, near_ref, coup_ref, sems, first_sems = refs
     leaves, n, _ = pts_hbm.shape
     steps, chunk, slots = near_ref.shape[:3]
@@ -197,17 +198,16 @@
 
     coeff_pad[FAR : FAR + leaves] = coeff_ref[...]
 
-    def put(ref, at, low):
+    def put(ref, low):
         co = 0 if low else leaves + FAR
         po = 0 if low else leaves + NEAR
         for q in range(FAR):
-            coeff_pad[co + q] = ref[at + q]
+            coeff_pad[co + q] = ref[q]
         for q in range(NEAR):
-            pts_pad[po + q, : n // 2] = ref[at + FAR + 2 * q]
-            pts_pad[po + q, n // 2 :] = ref[at + FAR + 2 * q + 1]
+            pts_pad[po + q, : n // 2] = ref[FAR + 2 * q]
+            pts_pad[po + q, n // 2 :] = ref[FAR + 2 * q + 1]
 
     if edges:
-        at = pay_ref.shape[0] - side_ref.shape[0]
         leaf = me_ref[0] & (leafs - 1)
         odd = leaf & 1 == 1
 
@@ -216,21 +216,21 @@
 
             @pl.when(last)
             def _():
-                put(hop_ref, 0, low)
+                put(hop_ref, low)
 
             @pl.when(jnp.logical_not(last))
             def _():
-                put(side_ref, 0, low)
+                put(side_ref, low)
 
         @pl.when(odd)
         def _():
-            put(pay_ref, at, True)
+            put(edge_ref, True)
             put_side(False)
 
         @pl.when(jnp.logical_not(odd))
         def _():
             put_side(True)
-            put(pay_ref, at, False)
+            put(edge_ref, False)
 
     for c in early:
         c.wait()
@@ -300,7 +300,7 @@
 
 def downward_kernel(
     place_hbm, table, coup_ref, trans_ref, basis_ref, near_mid, field_mid, near_rim, field_rim, out_hbm,
-    place_ref, out_ref, sems, place_sem, *, batch
+    place_ref, half_ref, total_ref, out_ref, sems, place_sem, *, batch
 ):
     parents = trans_ref.shape[0]
     n, size = near_mid.shape[1:]
@@ -311,41 +311,30 @@
     fetch.start()
     fetch.wait()
 
-    def run(own, near_ref, field_ref, at):
-        halves = []
-        for p in own:
-            tiles = [table[place_ref[k, p]] for k in range(slots)]
-            halves.append(dot_t(beside(tiles, mask), coup_ref[p]).astype(BF16))
-        totals = []
-        for q, (p, half) in enumerate(zip(own, halves)):
-            totals.append((field_ref[at + q] + dot_n(half, trans_ref[p])).astype(BF16))
-        fars = []
-        for p, total in zip(own, totals):
-            fars.append(dot_n(total, diagonal(basis_ref[2 * p], basis_ref[2 * p + 1])))
-        for q, (p, far) in enumerate(zip(own, fars)):
-            out_ref[2 * p] = (far[:, :size] + near_ref[2 * (at + q)]).astype(BF16)
-            out_ref[2 * p + 1] = (far[:, size:] + near_ref[2 * (at + q) + 1]).astype(BF16)
-
-    def copy(first, count, sem):
-        own = pl.ds(2 * first, 2 * count)
-        return pltpu.make_async_copy(out_ref.at[own], out_hbm.at[own], sem)
-
-    def rows(step, carry):
-        first = rim + step * batch
-        run([first + q for q in range(batch)], near_mid, field_mid, step * batch)
-        copy(first, batch, sems.at[step]).start()
-        return carry
-
-    steps = (parents - 2 * rim) // batch
-    lax.fori_loop(0, steps, rows, 0)
-    run(list(range(rim)) + list(range(parents - rim, parents)), near_rim, field_rim, 0)
-    ends = [copy(0, rim, sems.at[steps]), copy(parents - rim, rim, sems.at[steps + 1])]
-    for c in ends:
-        c.start()
-    for step in range(steps):
-        copy(rim + step * batch, batch, sems.at[step]).wait()
-    for c in ends:
-        c.wait()
+    def local_at(p):
+        if rim <= p < parents - rim:
+            return near_mid, field_mid, p - rim
+        return near_rim, field_rim, p if p < rim else p - parents + 2 * rim
+
+    def copy(step):
+        own = pl.ds(2 * step * batch, 2 * batch)
+        return pltpu.make_async_copy(out_ref.at[own], out_hbm.at[own], sems.at[step])
+
+    for p in range(parents):
+        tiles = [table[place_ref[k, p]] for k in range(slots)]
+        half_ref[p] = dot_t(beside(tiles, mask), coup_ref[p]).astype(BF16)
+    for p in range(parents):
+        _, field_ref, at = local_at(p)
+        total_ref[p] = (field_ref[at] + dot_n(half_ref[p], trans_ref[p])).astype(BF16)
+    for step in range(parents // batch):
+        for p in range(step * batch, (step + 1) * batch):
+            near_ref, _, at = local_at(p)
+            far = dot_n(total_ref[p], diagonal(basis_ref[2 * p], basis_ref[2 * p + 1]))
+            out_ref[2 * p] = (far[:, :size] + near_ref[2 * at]).astype(BF16)
+            out_ref[2 * p + 1] = (far[:, size:] + near_ref[2 * at + 1]).astype(BF16)
+        copy(step).start()
+    for step in range(parents // batch):
+        copy(step).wait()
 
 
 def downward(place, table, coupling, transfer, basis, mid, rim):
@@ -353,7 +342,8 @@
     n = mid[0].shape[1]
     vmem = pl.BlockSpec(memory_space=pltpu.VMEM)
     big = [pltpu.with_memory_space_constraint(x, pltpu.VMEM) for x in (table, coupling, transfer, basis, *mid, *rim)]
-    batch = mid[1].shape[0] // 2
+    parents, rank, _ = transfer.shape
+    batch = parents // 4
     return pl.pallas_call(
         functools.partial(downward_kernel, batch=batch),
         out_shape=jax.ShapeDtypeStruct((leaves, n, size), BF16),
@@ -361,8 +351,10 @@
         out_specs=pl.BlockSpec(memory_space=pltpu.HBM),
         scratch_shapes=[
             pltpu.SMEM(place.shape, jnp.int32),
+            pltpu.VMEM((parents, n, rank), BF16),
+            pltpu.VMEM((parents, n, 2 * rank), BF16),
             pltpu.VMEM((leaves, n, size), BF16),
-            pltpu.SemaphoreType.DMA((4,)),
+            pltpu.SemaphoreType.DMA((parents // batch,)),
             pltpu.SemaphoreType.DMA,
         ],
         compiler_params=pltpu.CompilerParams(vmem_limit_bytes=LIMIT),
@@ -384,7 +376,6 @@
 ):
     streams, leafs = lax.axis_size("stream"), lax.axis_size("leaf")
     devices = streams * leafs
-    parents = transfer.shape[0]
     me = lax.axis_index(AXES).astype(jnp.int32)
     flag = me.reshape(1)
 
@@ -396,22 +387,19 @@
     def swap(x, bits):
         return permute(x, [(i, i ^ bits) for i in range(devices)])
 
-    coeffs, payload, side, place = upward(flag, points_rhs, leaf_basis, transfer, parent_owner.T, parent_local.T)
-
-    got = swap(payload, 1)
-    line = [payload[:parents], got[:parents]]
-    sides = None
-    for k in range(2, leafs):
-        if k & (k + 1):
-            line.append(swap(line[0], k))
-            continue
-        both = swap(jnp.concatenate([line[0], side], axis=0), k)
-        line.append(both[:parents])
+    coeffs, own, edge, side, place = upward(flag, points_rhs, leaf_basis, transfer, parent_owner.T, parent_local.T)
+
+    line = [own] + [swap(own, k) for k in range(1, leafs)]
+    edges = swap(edge, 1)
+    sides, k = None, 3
+    while k < leafs:
+        both = swap(side, k)
         if sides is None:
-            sides = both[parents:]
+            sides = both
         else:
             away = my_leaf ^ jnp.where(my_leaf % 2 == 1, my_leaf + 1, my_leaf - 1)
-            sides = jnp.where((away == k) | (k == leafs - 1) & (away > k) | (away < 0), both[parents:], sides)
+            sides = jnp.where((away == k) | (k == leafs - 1) & (away > k) | (away < 0), both, sides)
+        k = 2 * k + 1
     ends = [(s * leafs, (s + 1) * leafs) for s in range(streams - 1)]
     ends += [(s * leafs + leafs - 1, s * leafs - 1) for s in range(1, streams)]
     hop = permute(sides, ends)
@@ -446,7 +434,7 @@
     chunk = (leaves - 2 * rim) // 3
     args = (flag, near_offsets.T, coupling_offsets.T, points_rhs, coeffs)
     mid = local_terms(*args, (), near_blocks, leaf_coupling, leafs, rim, chunk, 3, chunk)
-    edge = local_terms(*args, (got, sides, hop), near_blocks, leaf_coupling, leafs, 0, leaves - rim, 2, rim)
+    edge = local_terms(*args, (edges, sides, hop), near_blocks, leaf_coupling, leafs, 0, leaves - rim, 2, rim)
     return downward(place, table, parent_coupling, transfer, leaf_basis, mid, edge)
 
 

time: 47.4 us -> 52.6 us (1.11)
  waiting for transfers between devices: 12.1 us -> 16.1 us
  starting transfers between devices: 20.5 us -> 22.4 us
  Pallas kernels: 13.5 us -> 12.8 us
    ppermute x20 -> x22, waiting for transfers between devices: 12.1 us -> 16.1 us  [permute(): return lax.ppermute(x, AXES, pairs)]
    ppermute x20 -> x22, starting transfers between devices: 20.5 us -> 22.4 us  [permute(): return lax.ppermute(x, AXES, pairs)]
    pallas_call x1, Pallas kernels: 3.19 us -> 2.49 us  [downward(): pl.pallas_call(functools.partial(downward_kernel, batch=batch), out_shape...]
  transfers between devices with their start and end apart: 20 -> 22, of which waited for: 8 -> 8; matrix products, arithmetic and copies ran while one was open for 2% -> 1% of each run, Pallas kernels for 16% -> 15%
where the time goes in v4:
time: 52.6 us; the launch traced here: 52.3 us
  starting transfers between devices  22.4 us (43%)
  waiting for transfers between devices  16.1 us (31%)
  Pallas kernels  12.8 us (24%)
  local copies, waits for them, and re-layouts  0.75 us (1%)
    ppermute x22, starting transfers between devices, permute(): return lax.ppermute(x, AXES, pairs)  22.4 us
    ppermute x22, waiting for transfers between devices, permute(): return lax.ppermute(x, AXES, pairs)  16.1 us
    pallas_call x2, Pallas kernels, local_terms(): pl.pallas_call(functools.partial(local_kernel, leafs=leafs, base=base, st...  7.6 us
    pallas_call x1, Pallas kernels, upward(): pl.pallas_call(functools.partial(upward_kernel, steps=steps), out_shape=(...  2.7 us
    pallas_call x1, Pallas kernels, downward(): pl.pallas_call(functools.partial(downward_kernel, batch=batch), out_shape...  2.49 us
  transfers between devices with their start and end apart: 22, of which 8 were waited for; matrix products, arithmetic and copies ran while one was open for 1% of the time, Pallas kernels for 15%

profile of v4, /device:TPU:0, one launch (start us, length us, event | category | flops | bytes accessed | tf_op | source)
XLA Modules:
  0.0 52.3 jit_solution(3162991329941198251)
XLA Ops:
  0.0 2.7 %upward.1 = (bf16[64,16,128]{2,1,0:T(8,128)(2,1)S(1)}, bf16[32,16,128]{2,1,0:T(8,128)(2,1)S(1)}, bf16[9,16,128]{2,1,0:T(8,128)(2,1)S(1)}, bf16[9,16,128]{2,1,0:T(8,128)(2,1)S(1)}, s32[8,32]{1,0:T(8,128)S(1)}) custom-call(s32[1]{0:T(128)} %bitcast.me_ref, bf16[64,32,128]{2,1,0:T(8,128)(2,1)} %pts_hbm.5, bf16[64,64,128]{2,1,0:T(8,128)(2,1)} %basis_ref.1, ...), custom_call_target="tpu_custom_call" | custom-call | tf_op jit(solution)/shard_map/upward/pallas_call | solution.py:145
  2.7 3.1 %collective-permute-start = (bf16[32,16,128]{2,1,0:T(8,128)(2,1)S(1)}, bf16[32,16,128]{2,1,0:T(8,128)(2,1)S(1)}, u32[]{:S(2)}, u32[]{:S(2)}) collective-permute-start(bf16[32,16,128]{2,1,0:T(8,128)(2,1)S(1)} %get-tuple-element.15), channel_id=1, source_target_pairs={{0,1},{1,0},{2,3},{3,2},{4,5},{5,4},{6,7},{7,6},{8,9},{9,8},{10,11... | collective-permute-start | bytes 393224 | tf_op jit(solution)/shard_map/ppermute | solution.py:385
  5.8 2.6 %collective-permute-start.1 = (bf16[32,16,128]{2,1,0:T(8,128)(2,1)S(1)}, bf16[32,16,128]{2,1,0:T(8,128)(2,1)S(1)}, u32[]{:S(2)}, u32[]{:S(2)}) collective-permute-start(bf16[32,16,128]{2,1,0:T(8,128)(2,1)S(1)} %get-tuple-element.15), channel_id=1, source_target_pairs={{0,2},{1,3},{2,0},{3,1},{4,6},{5,7},{6,4},{7,5},{8,10},{9,11},{10,... | collective-permute-start | bytes 393224 | tf_op jit(solution)/shard_map/ppermute | solution.py:385
  8.4 0.0 collective-permute-start.2
  8.4 3.8 %collective-permute-start.20 = (bf16[9,16,128]{2,1,0:T(8,128)(2,1)S(1)}, bf16[9,16,128]{2,1,0:T(8,128)(2,1)S(1)}, u32[]{:S(2)}, u32[]{:S(2)}) collective-permute-start(bf16[9,16,128]{2,1,0:T(8,128)(2,1)S(1)} %get-tuple-element.20), channel_id=1, source_target_pairs={{0,3},{1,2},{2,1},{3,0},{4,7},{5,6},{6,5},{7,4},{8,11},{9,10},{10,... | collective-permute-start | bytes 110600 | tf_op jit(solution)/shard_map/ppermute | solution.py:385
  12.2 0.0 collective-permute-start.19
  12.3 6.1 %collective-permute-done.20.refs_1_ = bf16[9,16,128]{2,1,0:T(8,128)(2,1)S(1)} collective-permute-done((bf16[9,16,128]{2,1,0:T(8,128)(2,1)S(1)}, bf16[9,16,128]{2,1,0:T(8,128)(2,1)S(1)}, u32[]{:S(2)}, u32[]{:S(2)}) %collective-permute-start.20) | collective-permute-done | bytes 36896 | tf_op jit(solution)/shard_map/ppermute | solution.py:385
  18.4 1.3 %collective-permute-start.21 = (bf16[9,16,128]{2,1,0:T(8,128)(2,1)S(1)}, bf16[9,16,128]{2,1,0:T(8,128)(2,1)S(1)}, u32[]{:S(2)}, u32[]{:S(2)}) collective-permute-start(bf16[9,16,128]{2,1,0:T(8,128)(2,1)S(1)} %collective-permute-done.20.refs_1_), channel_id=1, source_target_pairs={{0,4},{4,8},{8,12},{12,16},{16,20},{20,24},{24,28},{7,3},{11,7},{1... | collective-permute-start | bytes 110600 | tf_op jit(solution)/shard_map/ppermute | solution.py:385
  19.6 0.0 collective-permute-done
  19.7 0.1 constant_dynamic-update-slice_fusion
  19.7 2.2 %collective-permute-start.5 = (bf16[64,16,128]{2,1,0:T(8,128)(2,1)S(1)}, bf16[64,16,128]{2,1,0:T(8,128)(2,1)S(1)}, u32[]{:S(2)}, u32[]{:S(2)}) collective-permute-start(bf16[64,16,128]{2,1,0:T(8,128)(2,1)S(1)} %get-tuple-element.27), channel_id=1, source_target_pairs={{0,8},{1,9},{2,10},{3,11},{4,12},{5,13},{6,14},{7,15},{8,0},{9,1},... | collective-permute-start | bytes 786440 | tf_op jit(solution)/shard_map/ppermute | solution.py:385
  21.9 0.0 collective-permute-done.1
  21.9 1.5 %collective-permute-start.9 = (bf16[64,16,128]{2,1,0:T(8,128)(2,1)S(1)}, bf16[64,16,128]{2,1,0:T(8,128)(2,1)S(1)}, u32[]{:S(2)}, u32[]{:S(2)}) collective-permute-start(bf16[64,16,128]{2,1,0:T(8,128)(2,1)S(1)} %get-tuple-element.27), channel_id=1, source_target_pairs={{0,16},{1,17},{2,18},{3,19},{4,20},{5,21},{6,22},{7,23},{8,24},{9,... | collective-permute-start | bytes 786440 | tf_op jit(solution)/shard_map/ppermute | solution.py:385
  23.5 0.0 collective-permute-done.2
  23.5 0.1 constant_dynamic-update-slice_fusion.2
  23.5 0.6 %collective-permute-start.10 = (bf16[64,16,128]{2,1,0:T(8,128)(2,1)S(1)}, bf16[64,16,128]{2,1,0:T(8,128)(2,1)S(1)}, u32[]{:S(2)}, u32[]{:S(2)}) collective-permute-start(bf16[64,16,128]{2,1,0:T(8,128)(2,1)S(1)} %get-tuple-element.23), channel_id=1, source_target_pairs={{0,16},{1,17},{2,18},{3,19},{4,20},{5,21},{6,22},{7,23},{8,24},{9,... | collective-permute-start | bytes 786440 | tf_op jit(solution)/shard_map/ppermute | solution.py:385
  24.1 0.0 collective-permute-done.19.refs_0_
  24.1 0.1 collective-permute-start.6
  24.2 0.0 collective-permute-done.21.refs_2_
  24.2 0.9 %collective-permute-start.3 = (bf16[64,16,128]{2,1,0:T(8,128)(2,1)S(1)}, bf16[64,16,128]{2,1,0:T(8,128)(2,1)S(1)}, u32[]{:S(2)}, u32[]{:S(2)}) collective-permute-start(bf16[64,16,128]{2,1,0:T(8,128)(2,1)S(1)} %get-tuple-element.27), channel_id=1, source_target_pairs={{0,4},{1,5},{2,6},{3,7},{4,0},{5,1},{6,2},{7,3},{8,12},{9,13},{10,... | collective-permute-start | bytes 786440 | tf_op jit(solution)/shard_map/ppermute | solution.py:385
  25.1 5.6 %collective-permute-done.9 = bf16[64,16,128]{2,1,0:T(8,128)(2,1)S(1)} collective-permute-done((bf16[64,16,128]{2,1,0:T(8,128)(2,1)S(1)}, bf16[64,16,128]{2,1,0:T(8,128)(2,1)S(1)}, u32[]{:S(2)}, u32[]{:S(2)}) %collective-permute-start.9) | collective-permute-done | bytes 262176 | tf_op jit(solution)/shard_map/ppermute | solution.py:385
  30.7 0.8 %collective-permute-start.4 = (bf16[64,16,128]{2,1,0:T(8,128)(2,1)S(1)}, bf16[64,16,128]{2,1,0:T(8,128)(2,1)S(1)}, u32[]{:S(2)}, u32[]{:S(2)}) collective-permute-start(bf16[64,16,128]{2,1,0:T(8,128)(2,1)S(1)} %get-tuple-element.23), channel_id=1, source_target_pairs={{0,4},{1,5},{2,6},{3,7},{4,0},{5,1},{6,2},{7,3},{8,12},{9,13},{10,... | collective-permute-start | bytes 786440 | tf_op jit(solution)/shard_map/ppermute | solution.py:385
  31.5 4.9 %local_terms.2 = (f32[48,32,128]{2,1,0:T(8,128)S(1)}, f32[24,32,128]{2,1,0:T(8,128)S(1)}) custom-call(s32[1]{0:T(128)} %bitcast.me_ref, s32[3,64]{1,0:T(4,128)} %bitcast.5, s32[4,64]{1,0:T(4,128)} %bitcast.7, bf16[64,32,128]{2,1,0:T(8,128)(2,1)} %pts_hbm.5, bf16[64,3,128,128]{3,2,1,0:T(8,128)(2,1)} %near_hbm.3, bf16[64,64,256]{2,1,0:T(8,128)(2,1)} %coup_hbm.3, ...), custom_call_target="tpu_custom_call" | custom-call | tf_op jit(solution)/shard_map/local_terms/pallas_call | solution.py:275
  36.4 2.7 %local_terms.3 = (f32[16,32,128]{2,1,0:T(8,128)S(1)}, f32[8,32,128]{2,1,0:T(8,128)S(1)}) custom-call(s32[1]{0:T(128)} %bitcast.me_ref, s32[3,64]{1,0:T(4,128)} %bitcast.6, s32[4,64]{1,0:T(4,128)} %bitcast.8, bf16[64,32,128]{2,1,0:T(8,128)(2,1)} %pts_hbm.5, bf16[64,3,128,128]{3,2,1,0:T(8,128)(2,1)} %near_hbm.3, bf16[64,64,256]{2,1,0:T(8,128)(2,1)} %coup_hbm.3, ...), custom_call_target="tpu_custom_call" | custom-call | tf_op jit(solution)/shard_map/local_terms/pallas_call | solution.py:275
  39.2 0.0 collective-permute-done.5
  39.2 0.6 %collective-permute-start.13 = (bf16[32,16,128]{2,1,0:T(8,128)(2,1)S(1)}, bf16[32,16,128]{2,1,0:T(8,128)(2,1)S(1)}, u32[]{:S(2)}, u32[]{:S(2)}) collective-permute-start(bf16[32,16,128]{2,1,0:T(8,128)(2,1)S(1)} %slice.16), channel_id=1, source_target_pairs={{0,8},{1,9},{2,10},{3,11},{4,12},{5,13},{6,14},{7,15},{8,0},{9,1},... | collective-permute-start | bytes 393224 | tf_op jit(solution)/shard_map/ppermute | solution.py:385
  39.8 0.0 collective-permute-done.10
  39.8 1.6 %collective-permute-start.14 = (bf16[32,16,128]{2,1,0:T(8,128)(2,1)S(1)}, bf16[32,16,128]{2,1,0:T(8,128)(2,1)S(1)}, u32[]{:S(2)}, u32[]{:S(2)}) collective-permute-start(bf16[32,16,128]{2,1,0:T(8,128)(2,1)S(1)} %slice.17), channel_id=1, source_target_pairs={{0,16},{1,17},{2,18},{3,19},{4,20},{5,21},{6,22},{7,23},{8,24},{9,... | collective-permute-start | bytes 393224 | tf_op jit(solution)/shard_map/ppermute | solution.py:385
  41.4 0.0 collective-permute-done.6
  41.4 1.1 %collective-permute-start.15 = (bf16[32,16,128]{2,1,0:T(8,128)(2,1)S(1)}, bf16[32,16,128]{2,1,0:T(8,128)(2,1)S(1)}, u32[]{:S(2)}, u32[]{:S(2)}) collective-permute-start(bf16[32,16,128]{2,1,0:T(8,128)(2,1)S(1)} %slice.18), channel_id=1, source_target_pairs={{0,8},{1,9},{2,10},{3,11},{4,12},{5,13},{6,14},{7,15},{8,0},{9,1},... | collective-permute-start | bytes 393224 | tf_op jit(solution)/shard_map/ppermute | solution.py:385
  42.5 0.0 collective-permute-done.3
  42.5 1.0 %collective-permute-start.16 = (bf16[32,16,128]{2,1,0:T(8,128)(2,1)S(1)}, bf16[32,16,128]{2,1,0:T(8,128)(2,1)S(1)}, u32[]{:S(2)}, u32[]{:S(2)}) collective-permute-start(bf16[32,16,128]{2,1,0:T(8,128)(2,1)S(1)} %slice.19), channel_id=1, source_target_pairs={{0,16},{1,17},{2,18},{3,19},{4,20},{5,21},{6,22},{7,23},{8,24},{9,... | collective-permute-start | bytes 393224 | tf_op jit(solution)/shard_map/ppermute | solution.py:385
  43.6 0.0 copy-start
  43.6 0.0 copy-start.1
  43.6 0.0 copy-start.2
  43.6 0.0 collective-permute-done.4
  43.6 0.1 collective-permute-start.7
  43.8 1.8 %collective-permute-done.13 = bf16[32,16,128]{2,1,0:T(8,128)(2,1)S(1)} collective-permute-done((bf16[32,16,128]{2,1,0:T(8,128)(2,1)S(1)}, bf16[32,16,128]{2,1,0:T(8,128)(2,1)S(1)}, u32[]{:S(2)}, u32[]{:S(2)}) %collective-permute-start.13) | collective-permute-done | bytes 131104 | tf_op jit(solution)/shard_map/ppermute | solution.py:385
  45.6 0.0 collective-permute-start.8
  45.6 0.0 collective-permute-done.14
  45.6 0.5 collective-permute-start.11
  46.2 1.3 %collective-permute-done.15 = bf16[32,16,128]{2,1,0:T(8,128)(2,1)S(1)} collective-permute-done((bf16[32,16,128]{2,1,0:T(8,128)(2,1)S(1)}, bf16[32,16,128]{2,1,0:T(8,128)(2,1)S(1)}, u32[]{:S(2)}, u32[]{:S(2)}) %collective-permute-start.15) | collective-permute-done | bytes 131104 | tf_op jit(solution)/shard_map/ppermute | solution.py:385
  47.5 0.0 collective-permute-start.12
  47.5 0.3 collective-permute-done.16
  47.8 0.2 collective-permute-start.17
  48.0 0.0 collective-permute-done.7
  48.0 0.4 collective-permute-start.18
  48.5 0.0 collective-permute-done.8
  48.6 0.0 collective-permute-done.11
  48.7 0.3 collective-permute-done.12
  49.2 0.2 collective-permute-done.17
  49.4 0.3 collective-permute-done.18
  49.8 0.0 copy-done
  49.8 0.0 copy-done.1
  49.8 0.0 copy-done.2
  49.8 2.5 %downward.1 = bf16[64,32,128]{2,1,0:T(8,128)(2,1)} custom-call(s32[8,32]{1,0:T(8,128)S(1)} %get-tuple-element.14.place_hbm, bf16[1024,16,128]{2,1,0:T(8,128)(2,1)S(1)} %constant_dynamic-update-slice_fusion.4.table, bf16[32,64,512]{2,1,0:T(8,128)(2,1)S(1)} %copy-done.2, bf16[32,64,128]{2,1,0:T(8,128)(2,1)S(1)} %copy-done.1, bf16[64,64,128]{2,1,0:T(8,128)(2,1)S(1)} %copy-done, ...), custom_call_target="tpu_custom_call" | custom-call | tf_op jit(solution)/shard_map/downward/pallas_call | solution.py:347
  (24 shorter events, 0.7 us)
Async XLA Ops:
  2.7 16.9 %collective-permute-start = (bf16[32,16,128]{2,1,0:T(8,128)(2,1)S(1)}, bf16[32,16,128]{2,1,0:T(8,128)(2,1)S(1)}, u32[]{:S(2)}, u32[]{:S(2)}) collective-permute-start(bf16[32,16,128]{2,1,0:T(8,128)(2,1)S(1)} %get-tuple-element.15), channel_id=1, source_target_pairs={{0,1},{1,0},{2,3},{3,2},{4,5},{5,4},{6,7},{7,6},{8,9},{9,8},{10,11... | collective-permute-start | bytes 393224 | tf_op jit(solution)/shard_map/ppermute | solution.py:385
  5.8 16.1 %collective-permute-start.1 = (bf16[32,16,128]{2,1,0:T(8,128)(2,1)S(1)}, bf16[32,16,128]{2,1,0:T(8,128)(2,1)S(1)}, u32[]{:S(2)}, u32[]{:S(2)}) collective-permute-start(bf16[32,16,128]{2,1,0:T(8,128)(2,1)S(1)} %get-tuple-element.15), channel_id=1, source_target_pairs={{0,2},{1,3},{2,0},{3,1},{4,6},{5,7},{6,4},{7,5},{8,10},{9,11},{10,... | collective-permute-start | bytes 393224 | tf_op jit(solution)/shard_map/ppermute | solution.py:385
  8.4 15.1 %collective-permute-start.2 = (bf16[32,16,128]{2,1,0:T(8,128)(2,1)S(1)}, bf16[32,16,128]{2,1,0:T(8,128)(2,1)S(1)}, u32[]{:S(2)}, u32[]{:S(2)}) collective-permute-start(bf16[32,16,128]{2,1,0:T(8,128)(2,1)S(1)} %get-tuple-element.15), channel_id=1, source_target_pairs={{0,3},{1,2},{2,1},{3,0},{4,7},{5,6},{6,5},{7,4},{8,11},{9,10},{10,... | collective-permute-start | bytes 393224 | tf_op jit(solution)/shard_map/ppermute | solution.py:385
  8.4 9.9 %collective-permute-start.20 = (bf16[9,16,128]{2,1,0:T(8,128)(2,1)S(1)}, bf16[9,16,128]{2,1,0:T(8,128)(2,1)S(1)}, u32[]{:S(2)}, u32[]{:S(2)}) collective-permute-start(bf16[9,16,128]{2,1,0:T(8,128)(2,1)S(1)} %get-tuple-element.20), channel_id=1, source_target_pairs={{0,3},{1,2},{2,1},{3,0},{4,7},{5,6},{6,5},{7,4},{8,11},{9,10},{10,... | collective-permute-start | bytes 110600 | tf_op jit(solution)/shard_map/ppermute | solution.py:385
  12.2 11.9 %collective-permute-start.19 = (bf16[9,16,128]{2,1,0:T(8,128)(2,1)S(1)}, bf16[9,16,128]{2,1,0:T(8,128)(2,1)S(1)}, u32[]{:S(2)}, u32[]{:S(2)}) collective-permute-start(bf16[9,16,128]{2,1,0:T(8,128)(2,1)S(1)} %get-tuple-element.19), channel_id=1, source_target_pairs={{0,1},{1,0},{2,3},{3,2},{4,5},{5,4},{6,7},{7,6},{8,9},{9,8},{10,11... | collective-permute-start | bytes 110600 | tf_op jit(solution)/shard_map/ppermute | solution.py:385
  18.4 5.9 %collective-permute-start.21 = (bf16[9,16,128]{2,1,0:T(8,128)(2,1)S(1)}, bf16[9,16,128]{2,1,0:T(8,128)(2,1)S(1)}, u32[]{:S(2)}, u32[]{:S(2)}) collective-permute-start(bf16[9,16,128]{2,1,0:T(8,128)(2,1)S(1)} %collective-permute-done.20.refs_1_), channel_id=1, source_target_pairs={{0,4},{4,8},{8,12},{12,16},{16,20},{20,24},{24,28},{7,3},{11,7},{1... | collective-permute-start | bytes 110600 | tf_op jit(solution)/shard_map/ppermute | solution.py:385
  19.7 19.5 %collective-permute-start.5 = (bf16[64,16,128]{2,1,0:T(8,128)(2,1)S(1)}, bf16[64,16,128]{2,1,0:T(8,128)(2,1)S(1)}, u32[]{:S(2)}, u32[]{:S(2)}) collective-permute-start(bf16[64,16,128]{2,1,0:T(8,128)(2,1)S(1)} %get-tuple-element.27), channel_id=1, source_target_pairs={{0,8},{1,9},{2,10},{3,11},{4,12},{5,13},{6,14},{7,15},{8,0},{9,1},... | collective-permute-start | bytes 786440 | tf_op jit(solution)/shard_map/ppermute | solution.py:385
  21.9 8.8 %collective-permute-start.9 = (bf16[64,16,128]{2,1,0:T(8,128)(2,1)S(1)}, bf16[64,16,128]{2,1,0:T(8,128)(2,1)S(1)}, u32[]{:S(2)}, u32[]{:S(2)}) collective-permute-start(bf16[64,16,128]{2,1,0:T(8,128)(2,1)S(1)} %get-tuple-element.27), channel_id=1, source_target_pairs={{0,16},{1,17},{2,18},{3,19},{4,20},{5,21},{6,22},{7,23},{8,24},{9,... | collective-permute-start | bytes 786440 | tf_op jit(solution)/shard_map/ppermute | solution.py:385
  23.5 16.3 %collective-permute-start.10 = (bf16[64,16,128]{2,1,0:T(8,128)(2,1)S(1)}, bf16[64,16,128]{2,1,0:T(8,128)(2,1)S(1)}, u32[]{:S(2)}, u32[]{:S(2)}) collective-permute-start(bf16[64,16,128]{2,1,0:T(8,128)(2,1)S(1)} %get-tuple-element.23), channel_id=1, source_target_pairs={{0,16},{1,17},{2,18},{3,19},{4,20},{5,21},{6,22},{7,23},{8,24},{9,... | collective-permute-start | bytes 786440 | tf_op jit(solution)/shard_map/ppermute | solution.py:385
  24.1 17.3 %collective-permute-start.6 = (bf16[64,16,128]{2,1,0:T(8,128)(2,1)S(1)}, bf16[64,16,128]{2,1,0:T(8,128)(2,1)S(1)}, u32[]{:S(2)}, u32[]{:S(2)}) collective-permute-start(bf16[64,16,128]{2,1,0:T(8,128)(2,1)S(1)} %get-tuple-element.23), channel_id=1, source_target_pairs={{0,8},{1,9},{2,10},{3,11},{4,12},{5,13},{6,14},{7,15},{8,0},{9,1},... | collective-permute-start | bytes 786440 | tf_op jit(solution)/shard_map/ppermute | solution.py:385
  24.2 18.3 %collective-permute-start.3 = (bf16[64,16,128]{2,1,0:T(8,128)(2,1)S(1)}, bf16[64,16,128]{2,1,0:T(8,128)(2,1)S(1)}, u32[]{:S(2)}, u32[]{:S(2)}) collective-permute-start(bf16[64,16,128]{2,1,0:T(8,128)(2,1)S(1)} %get-tuple-element.27), channel_id=1, source_target_pairs={{0,4},{1,5},{2,6},{3,7},{4,0},{5,1},{6,2},{7,3},{8,12},{9,13},{10,... | collective-permute-start | bytes 786440 | tf_op jit(solution)/shard_map/ppermute | solution.py:385
  30.7 12.9 %collective-permute-start.4 = (bf16[64,16,128]{2,1,0:T(8,128)(2,1)S(1)}, bf16[64,16,128]{2,1,0:T(8,128)(2,1)S(1)}, u32[]{:S(2)}, u32[]{:S(2)}) collective-permute-start(bf16[64,16,128]{2,1,0:T(8,128)(2,1)S(1)} %get-tuple-element.23), channel_id=1, source_target_pairs={{0,4},{1,5},{2,6},{3,7},{4,0},{5,1},{6,2},{7,3},{8,12},{9,13},{10,... | collective-permute-start | bytes 786440 | tf_op jit(solution)/shard_map/ppermute | solution.py:385
  39.2 6.4 %collective-permute-start.13 = (bf16[32,16,128]{2,1,0:T(8,128)(2,1)S(1)}, bf16[32,16,128]{2,1,0:T(8,128)(2,1)S(1)}, u32[]{:S(2)}, u32[]{:S(2)}) collective-permute-start(bf16[32,16,128]{2,1,0:T(8,128)(2,1)S(1)} %slice.16), channel_id=1, source_target_pairs={{0,8},{1,9},{2,10},{3,11},{4,12},{5,13},{6,14},{7,15},{8,0},{9,1},... | collective-permute-start | bytes 393224 | tf_op jit(solution)/shard_map/ppermute | solution.py:385
  39.8 5.8 %collective-permute-start.14 = (bf16[32,16,128]{2,1,0:T(8,128)(2,1)S(1)}, bf16[32,16,128]{2,1,0:T(8,128)(2,1)S(1)}, u32[]{:S(2)}, u32[]{:S(2)}) collective-permute-start(bf16[32,16,128]{2,1,0:T(8,128)(2,1)S(1)} %slice.17), channel_id=1, source_target_pairs={{0,16},{1,17},{2,18},{3,19},{4,20},{5,21},{6,22},{7,23},{8,24},{9,... | collective-permute-start | bytes 393224 | tf_op jit(solution)/shard_map/ppermute | solution.py:385
  41.4 6.0 %collective-permute-start.15 = (bf16[32,16,128]{2,1,0:T(8,128)(2,1)S(1)}, bf16[32,16,128]{2,1,0:T(8,128)(2,1)S(1)}, u32[]{:S(2)}, u32[]{:S(2)}) collective-permute-start(bf16[32,16,128]{2,1,0:T(8,128)(2,1)S(1)} %slice.18), channel_id=1, source_target_pairs={{0,8},{1,9},{2,10},{3,11},{4,12},{5,13},{6,14},{7,15},{8,0},{9,1},... | collective-permute-start | bytes 393224 | tf_op jit(solution)/shard_map/ppermute | solution.py:385
  42.5 5.3 %collective-permute-start.16 = (bf16[32,16,128]{2,1,0:T(8,128)(2,1)S(1)}, bf16[32,16,128]{2,1,0:T(8,128)(2,1)S(1)}, u32[]{:S(2)}, u32[]{:S(2)}) collective-permute-start(bf16[32,16,128]{2,1,0:T(8,128)(2,1)S(1)} %slice.19), channel_id=1, source_target_pairs={{0,16},{1,17},{2,18},{3,19},{4,20},{5,21},{6,22},{7,23},{8,24},{9,... | collective-permute-start | bytes 393224 | tf_op jit(solution)/shard_map/ppermute | solution.py:385
  43.6 6.2 %copy-start = (bf16[64,64,128]{2,1,0:T(8,128)(2,1)S(1)}, bf16[64,64,128]{2,1,0:T(8,128)(2,1)}, u32[]{:S(2)}) copy-start(bf16[64,64,128]{2,1,0:T(8,128)(2,1)} %basis_ref.1) | copy-start | bytes 3145732
  43.6 6.2 %copy-start.1 = (bf16[32,64,128]{2,1,0:T(8,128)(2,1)S(1)}, bf16[32,64,128]{2,1,0:T(8,128)(2,1)}, u32[]{:S(2)}) copy-start(bf16[32,64,128]{2,1,0:T(8,128)(2,1)} %trans_ref.1) | copy-start | bytes 1572868
  43.6 6.2 %copy-start.2 = (bf16[32,64,512]{2,1,0:T(8,128)(2,1)S(1)}, bf16[32,64,512]{2,1,0:T(8,128)(2,1)}, u32[]{:S(2)}) copy-start(bf16[32,64,512]{2,1,0:T(8,128)(2,1)} %coup_ref.1) | copy-start | bytes 6291460
  43.6 4.4 %collective-permute-start.7 = (bf16[64,16,128]{2,1,0:T(8,128)(2,1)S(1)}, bf16[64,16,128]{2,1,0:T(8,128)(2,1)S(1)}, u32[]{:S(2)}, u32[]{:S(2)}) collective-permute-start(bf16[64,16,128]{2,1,0:T(8,128)(2,1)S(1)} %collective-permute-done.5), channel_id=1, source_target_pairs={{0,4},{1,5},{2,6},{3,7},{4,0},{5,1},{6,2},{7,3},{8,12},{9,13},{10,... | collective-permute-start | bytes 786440 | tf_op jit(solution)/shard_map/ppermute | solution.py:385
  45.6 2.9 %collective-permute-start.8 = (bf16[64,16,128]{2,1,0:T(8,128)(2,1)S(1)}, bf16[64,16,128]{2,1,0:T(8,128)(2,1)S(1)}, u32[]{:S(2)}, u32[]{:S(2)}) collective-permute-start(bf16[64,16,128]{2,1,0:T(8,128)(2,1)S(1)} %collective-permute-done.6), channel_id=1, source_target_pairs={{0,4},{1,5},{2,6},{3,7},{4,0},{5,1},{6,2},{7,3},{8,12},{9,13},{10,... | collective-permute-start | bytes 786440 | tf_op jit(solution)/shard_map/ppermute | solution.py:385
  45.6 3.0 %collective-permute-start.11 = (bf16[64,16,128]{2,1,0:T(8,128)(2,1)S(1)}, bf16[64,16,128]{2,1,0:T(8,128)(2,1)S(1)}, u32[]{:S(2)}, u32[]{:S(2)}) collective-permute-start(bf16[64,16,128]{2,1,0:T(8,128)(2,1)S(1)} %collective-permute-done.9), channel_id=1, source_target_pairs={{0,4},{1,5},{2,6},{3,7},{4,0},{5,1},{6,2},{7,3},{8,12},{9,13},{10,... | collective-permute-start | bytes 786440 | tf_op jit(solution)/shard_map/ppermute | solution.py:385
  47.5 1.5 %collective-permute-start.12 = (bf16[64,16,128]{2,1,0:T(8,128)(2,1)S(1)}, bf16[64,16,128]{2,1,0:T(8,128)(2,1)S(1)}, u32[]{:S(2)}, u32[]{:S(2)}) collective-permute-start(bf16[64,16,128]{2,1,0:T(8,128)(2,1)S(1)} %collective-permute-done.10), channel_id=1, source_target_pairs={{0,4},{1,5},{2,6},{3,7},{4,0},{5,1},{6,2},{7,3},{8,12},{9,13},{10,... | collective-permute-start | bytes 786440 | tf_op jit(solution)/shard_map/ppermute | solution.py:385
  47.8 1.6 %collective-permute-start.17 = (bf16[64,16,128]{2,1,0:T(8,128)(2,1)S(1)}, bf16[64,16,128]{2,1,0:T(8,128)(2,1)S(1)}, u32[]{:S(2)}, u32[]{:S(2)}) collective-permute-start(bf16[64,16,128]{2,1,0:T(8,128)(2,1)S(1)} %pad_maximum_fusion), channel_id=1, source_target_pairs={{0,4},{1,5},{2,6},{3,7},{4,0},{5,1},{6,2},{7,3},{8,12},{9,13},{10,... | collective-permute-start | bytes 786440 | tf_op jit(solution)/shard_map/ppermute | solution.py:385
  48.0 1.7 %collective-permute-start.18 = (bf16[64,16,128]{2,1,0:T(8,128)(2,1)S(1)}, bf16[64,16,128]{2,1,0:T(8,128)(2,1)S(1)}, u32[]{:S(2)}, u32[]{:S(2)}) collective-permute-start(bf16[64,16,128]{2,1,0:T(8,128)(2,1)S(1)} %pad_maximum_fusion.1), channel_id=1, source_target_pairs={{0,4},{1,5},{2,6},{3,7},{4,0},{5,1},{6,2},{7,3},{8,12},{9,13},{10,... | collective-permute-start | bytes 786440 | tf_op jit(solution)/shard_map/ppermute | solution.py:385

commit v5 on v4

--- a/solution.py
+++ b/solution.py
@@ -14,7 +14,7 @@
 F32 = jnp.float32
 BF16 = jnp.bfloat16
 
-AHEAD = 2
+AHEAD = 3
 LIMIT = 16 * 1024 * 1024
 
 
@@ -431,9 +431,9 @@
 
     leaves = points_rhs.shape[0]
     rim = 8
-    chunk = (leaves - 2 * rim) // 3
+    chunk = (leaves - 2 * rim) // 6
     args = (flag, near_offsets.T, coupling_offsets.T, points_rhs, coeffs)
-    mid = local_terms(*args, (), near_blocks, leaf_coupling, leafs, rim, chunk, 3, chunk)
+    mid = local_terms(*args, (), near_blocks, leaf_coupling, leafs, rim, chunk, 6, chunk)
     edge = local_terms(*args, (edges, sides, hop), near_blocks, leaf_coupling, leafs, 0, leaves - rim, 2, rim)
     return downward(place, table, parent_coupling, transfer, leaf_basis, mid, edge)
 

time: 52.6 us -> 53 us (level)
  no operation moved by 1% of the time
where the time goes in v5:
time: 53 us; the launch traced here: 52.7 us
  starting transfers between devices  22.4 us (42%)
  waiting for transfers between devices  16.1 us (30%)
  Pallas kernels  13.2 us (25%)
  local copies, waits for them, and re-layouts  0.75 us (1%)
    ppermute x22, starting transfers between devices, permute(): return lax.ppermute(x, AXES, pairs)  22.4 us
    ppermute x22, waiting for transfers between devices, permute(): return lax.ppermute(x, AXES, pairs)  16.1 us
    pallas_call x2, Pallas kernels, local_terms(): pl.pallas_call(functools.partial(local_kernel, leafs=leafs, base=base, st...  7.99 us
    pallas_call x1, Pallas kernels, upward(): pl.pallas_call(functools.partial(upward_kernel, steps=steps), out_shape=(...  2.7 us
    pallas_call x1, Pallas kernels, downward(): pl.pallas_call(functools.partial(downward_kernel, batch=batch), out_shape...  2.49 us
  transfers between devices with their start and end apart: 22, of which 8 were waited for; matrix products, arithmetic and copies ran while one was open for 1% of the time, Pallas kernels for 15%

profile of v5, /device:TPU:0, one launch (start us, length us, event | category | flops | bytes accessed | tf_op | source)
XLA Modules:
  0.0 52.7 jit_solution(9583472724979054354)
XLA Ops:
  0.0 2.7 %upward.1 = (bf16[64,16,128]{2,1,0:T(8,128)(2,1)S(1)}, bf16[32,16,128]{2,1,0:T(8,128)(2,1)S(1)}, bf16[9,16,128]{2,1,0:T(8,128)(2,1)S(1)}, bf16[9,16,128]{2,1,0:T(8,128)(2,1)S(1)}, s32[8,32]{1,0:T(8,128)S(1)}) custom-call(s32[1]{0:T(128)} %bitcast.me_ref, bf16[64,32,128]{2,1,0:T(8,128)(2,1)} %pts_hbm.5, bf16[64,64,128]{2,1,0:T(8,128)(2,1)} %basis_ref.1, ...), custom_call_target="tpu_custom_call" | custom-call | tf_op jit(solution)/shard_map/upward/pallas_call | solution.py:145
  2.7 3.1 %collective-permute-start = (bf16[32,16,128]{2,1,0:T(8,128)(2,1)S(1)}, bf16[32,16,128]{2,1,0:T(8,128)(2,1)S(1)}, u32[]{:S(2)}, u32[]{:S(2)}) collective-permute-start(bf16[32,16,128]{2,1,0:T(8,128)(2,1)S(1)} %get-tuple-element.15), channel_id=1, source_target_pairs={{0,1},{1,0},{2,3},{3,2},{4,5},{5,4},{6,7},{7,6},{8,9},{9,8},{10,11... | collective-permute-start | bytes 393224 | tf_op jit(solution)/shard_map/ppermute | solution.py:385
  5.8 2.6 %collective-permute-start.1 = (bf16[32,16,128]{2,1,0:T(8,128)(2,1)S(1)}, bf16[32,16,128]{2,1,0:T(8,128)(2,1)S(1)}, u32[]{:S(2)}, u32[]{:S(2)}) collective-permute-start(bf16[32,16,128]{2,1,0:T(8,128)(2,1)S(1)} %get-tuple-element.15), channel_id=1, source_target_pairs={{0,2},{1,3},{2,0},{3,1},{4,6},{5,7},{6,4},{7,5},{8,10},{9,11},{10,... | collective-permute-start | bytes 393224 | tf_op jit(solution)/shard_map/ppermute | solution.py:385
  8.4 0.0 collective-permute-start.2
  8.4 3.8 %collective-permute-start.20 = (bf16[9,16,128]{2,1,0:T(8,128)(2,1)S(1)}, bf16[9,16,128]{2,1,0:T(8,128)(2,1)S(1)}, u32[]{:S(2)}, u32[]{:S(2)}) collective-permute-start(bf16[9,16,128]{2,1,0:T(8,128)(2,1)S(1)} %get-tuple-element.20), channel_id=1, source_target_pairs={{0,3},{1,2},{2,1},{3,0},{4,7},{5,6},{6,5},{7,4},{8,11},{9,10},{10,... | collective-permute-start | bytes 110600 | tf_op jit(solution)/shard_map/ppermute | solution.py:385
  12.2 0.0 collective-permute-start.19
  12.3 6.1 %collective-permute-done.20.refs_1_ = bf16[9,16,128]{2,1,0:T(8,128)(2,1)S(1)} collective-permute-done((bf16[9,16,128]{2,1,0:T(8,128)(2,1)S(1)}, bf16[9,16,128]{2,1,0:T(8,128)(2,1)S(1)}, u32[]{:S(2)}, u32[]{:S(2)}) %collective-permute-start.20) | collective-permute-done | bytes 36896 | tf_op jit(solution)/shard_map/ppermute | solution.py:385
  18.4 1.3 %collective-permute-start.21 = (bf16[9,16,128]{2,1,0:T(8,128)(2,1)S(1)}, bf16[9,16,128]{2,1,0:T(8,128)(2,1)S(1)}, u32[]{:S(2)}, u32[]{:S(2)}) collective-permute-start(bf16[9,16,128]{2,1,0:T(8,128)(2,1)S(1)} %collective-permute-done.20.refs_1_), channel_id=1, source_target_pairs={{0,4},{4,8},{8,12},{12,16},{16,20},{20,24},{24,28},{7,3},{11,7},{1... | collective-permute-start | bytes 110600 | tf_op jit(solution)/shard_map/ppermute | solution.py:385
  19.6 0.0 collective-permute-done
  19.7 0.1 constant_dynamic-update-slice_fusion
  19.7 2.2 %collective-permute-start.5 = (bf16[64,16,128]{2,1,0:T(8,128)(2,1)S(1)}, bf16[64,16,128]{2,1,0:T(8,128)(2,1)S(1)}, u32[]{:S(2)}, u32[]{:S(2)}) collective-permute-start(bf16[64,16,128]{2,1,0:T(8,128)(2,1)S(1)} %get-tuple-element.27), channel_id=1, source_target_pairs={{0,8},{1,9},{2,10},{3,11},{4,12},{5,13},{6,14},{7,15},{8,0},{9,1},... | collective-permute-start | bytes 786440 | tf_op jit(solution)/shard_map/ppermute | solution.py:385
  21.9 0.0 collective-permute-done.1
  21.9 1.5 %collective-permute-start.9 = (bf16[64,16,128]{2,1,0:T(8,128)(2,1)S(1)}, bf16[64,16,128]{2,1,0:T(8,128)(2,1)S(1)}, u32[]{:S(2)}, u32[]{:S(2)}) collective-permute-start(bf16[64,16,128]{2,1,0:T(8,128)(2,1)S(1)} %get-tuple-element.27), channel_id=1, source_target_pairs={{0,16},{1,17},{2,18},{3,19},{4,20},{5,21},{6,22},{7,23},{8,24},{9,... | collective-permute-start | bytes 786440 | tf_op jit(solution)/shard_map/ppermute | solution.py:385
  23.5 0.0 collective-permute-done.2
  23.5 0.1 constant_dynamic-update-slice_fusion.2
  23.5 0.6 %collective-permute-start.10 = (bf16[64,16,128]{2,1,0:T(8,128)(2,1)S(1)}, bf16[64,16,128]{2,1,0:T(8,128)(2,1)S(1)}, u32[]{:S(2)}, u32[]{:S(2)}) collective-permute-start(bf16[64,16,128]{2,1,0:T(8,128)(2,1)S(1)} %get-tuple-element.23), channel_id=1, source_target_pairs={{0,16},{1,17},{2,18},{3,19},{4,20},{5,21},{6,22},{7,23},{8,24},{9,... | collective-permute-start | bytes 786440 | tf_op jit(solution)/shard_map/ppermute | solution.py:385
  24.1 0.0 collective-permute-done.19.refs_0_
  24.1 0.1 collective-permute-start.6
  24.2 0.0 collective-permute-done.21.refs_2_
  24.2 0.9 %collective-permute-start.3 = (bf16[64,16,128]{2,1,0:T(8,128)(2,1)S(1)}, bf16[64,16,128]{2,1,0:T(8,128)(2,1)S(1)}, u32[]{:S(2)}, u32[]{:S(2)}) collective-permute-start(bf16[64,16,128]{2,1,0:T(8,128)(2,1)S(1)} %get-tuple-element.27), channel_id=1, source_target_pairs={{0,4},{1,5},{2,6},{3,7},{4,0},{5,1},{6,2},{7,3},{8,12},{9,13},{10,... | collective-permute-start | bytes 786440 | tf_op jit(solution)/shard_map/ppermute | solution.py:385
  25.1 5.6 %collective-permute-done.9 = bf16[64,16,128]{2,1,0:T(8,128)(2,1)S(1)} collective-permute-done((bf16[64,16,128]{2,1,0:T(8,128)(2,1)S(1)}, bf16[64,16,128]{2,1,0:T(8,128)(2,1)S(1)}, u32[]{:S(2)}, u32[]{:S(2)}) %collective-permute-start.9) | collective-permute-done | bytes 262176 | tf_op jit(solution)/shard_map/ppermute | solution.py:385
  30.7 0.8 %collective-permute-start.4 = (bf16[64,16,128]{2,1,0:T(8,128)(2,1)S(1)}, bf16[64,16,128]{2,1,0:T(8,128)(2,1)S(1)}, u32[]{:S(2)}, u32[]{:S(2)}) collective-permute-start(bf16[64,16,128]{2,1,0:T(8,128)(2,1)S(1)} %get-tuple-element.23), channel_id=1, source_target_pairs={{0,4},{1,5},{2,6},{3,7},{4,0},{5,1},{6,2},{7,3},{8,12},{9,13},{10,... | collective-permute-start | bytes 786440 | tf_op jit(solution)/shard_map/ppermute | solution.py:385
  31.5 5.3 %local_terms.2 = (f32[48,32,128]{2,1,0:T(8,128)S(1)}, f32[24,32,128]{2,1,0:T(8,128)S(1)}) custom-call(s32[1]{0:T(128)} %bitcast.me_ref, s32[3,64]{1,0:T(4,128)} %bitcast.5, s32[4,64]{1,0:T(4,128)} %bitcast.7, bf16[64,32,128]{2,1,0:T(8,128)(2,1)} %pts_hbm.5, bf16[64,3,128,128]{3,2,1,0:T(8,128)(2,1)} %near_hbm.3, bf16[64,64,256]{2,1,0:T(8,128)(2,1)} %coup_hbm.3, ...), custom_call_target="tpu_custom_call" | custom-call | tf_op jit(solution)/shard_map/local_terms/pallas_call | solution.py:275
  36.8 2.7 %local_terms.3 = (f32[16,32,128]{2,1,0:T(8,128)S(1)}, f32[8,32,128]{2,1,0:T(8,128)S(1)}) custom-call(s32[1]{0:T(128)} %bitcast.me_ref, s32[3,64]{1,0:T(4,128)} %bitcast.6, s32[4,64]{1,0:T(4,128)} %bitcast.8, bf16[64,32,128]{2,1,0:T(8,128)(2,1)} %pts_hbm.5, bf16[64,3,128,128]{3,2,1,0:T(8,128)(2,1)} %near_hbm.3, bf16[64,64,256]{2,1,0:T(8,128)(2,1)} %coup_hbm.3, ...), custom_call_target="tpu_custom_call" | custom-call | tf_op jit(solution)/shard_map/local_terms/pallas_call | solution.py:275
  39.6 0.0 collective-permute-done.5
  39.6 0.6 %collective-permute-start.13 = (bf16[32,16,128]{2,1,0:T(8,128)(2,1)S(1)}, bf16[32,16,128]{2,1,0:T(8,128)(2,1)S(1)}, u32[]{:S(2)}, u32[]{:S(2)}) collective-permute-start(bf16[32,16,128]{2,1,0:T(8,128)(2,1)S(1)} %slice.16), channel_id=1, source_target_pairs={{0,8},{1,9},{2,10},{3,11},{4,12},{5,13},{6,14},{7,15},{8,0},{9,1},... | collective-permute-start | bytes 393224 | tf_op jit(solution)/shard_map/ppermute | solution.py:385
  40.2 0.0 collective-permute-done.10
  40.2 1.6 %collective-permute-start.14 = (bf16[32,16,128]{2,1,0:T(8,128)(2,1)S(1)}, bf16[32,16,128]{2,1,0:T(8,128)(2,1)S(1)}, u32[]{:S(2)}, u32[]{:S(2)}) collective-permute-start(bf16[32,16,128]{2,1,0:T(8,128)(2,1)S(1)} %slice.17), channel_id=1, source_target_pairs={{0,16},{1,17},{2,18},{3,19},{4,20},{5,21},{6,22},{7,23},{8,24},{9,... | collective-permute-start | bytes 393224 | tf_op jit(solution)/shard_map/ppermute | solution.py:385
  41.8 0.0 collective-permute-done.6
  41.8 1.1 %collective-permute-start.15 = (bf16[32,16,128]{2,1,0:T(8,128)(2,1)S(1)}, bf16[32,16,128]{2,1,0:T(8,128)(2,1)S(1)}, u32[]{:S(2)}, u32[]{:S(2)}) collective-permute-start(bf16[32,16,128]{2,1,0:T(8,128)(2,1)S(1)} %slice.18), channel_id=1, source_target_pairs={{0,8},{1,9},{2,10},{3,11},{4,12},{5,13},{6,14},{7,15},{8,0},{9,1},... | collective-permute-start | bytes 393224 | tf_op jit(solution)/shard_map/ppermute | solution.py:385
  42.9 0.0 collective-permute-done.3
  42.9 1.0 %collective-permute-start.16 = (bf16[32,16,128]{2,1,0:T(8,128)(2,1)S(1)}, bf16[32,16,128]{2,1,0:T(8,128)(2,1)S(1)}, u32[]{:S(2)}, u32[]{:S(2)}) collective-permute-start(bf16[32,16,128]{2,1,0:T(8,128)(2,1)S(1)} %slice.19), channel_id=1, source_target_pairs={{0,16},{1,17},{2,18},{3,19},{4,20},{5,21},{6,22},{7,23},{8,24},{9,... | collective-permute-start | bytes 393224 | tf_op jit(solution)/shard_map/ppermute | solution.py:385
  44.0 0.0 copy-start
  44.0 0.0 copy-start.1
  44.0 0.0 copy-start.2
  44.0 0.0 collective-permute-done.4
  44.0 0.1 collective-permute-start.7
  44.2 1.8 %collective-permute-done.13 = bf16[32,16,128]{2,1,0:T(8,128)(2,1)S(1)} collective-permute-done((bf16[32,16,128]{2,1,0:T(8,128)(2,1)S(1)}, bf16[32,16,128]{2,1,0:T(8,128)(2,1)S(1)}, u32[]{:S(2)}, u32[]{:S(2)}) %collective-permute-start.13) | collective-permute-done | bytes 131104 | tf_op jit(solution)/shard_map/ppermute | solution.py:385
  46.0 0.0 collective-permute-start.8
  46.0 0.0 collective-permute-done.14
  46.0 0.5 collective-permute-start.11
  46.6 1.3 %collective-permute-done.15 = bf16[32,16,128]{2,1,0:T(8,128)(2,1)S(1)} collective-permute-done((bf16[32,16,128]{2,1,0:T(8,128)(2,1)S(1)}, bf16[32,16,128]{2,1,0:T(8,128)(2,1)S(1)}, u32[]{:S(2)}, u32[]{:S(2)}) %collective-permute-start.15) | collective-permute-done | bytes 131104 | tf_op jit(solution)/shard_map/ppermute | solution.py:385
  47.9 0.0 collective-permute-start.12
  47.9 0.3 collective-permute-done.16
  48.2 0.2 collective-permute-start.17
  48.4 0.0 collective-permute-done.7
  48.4 0.4 collective-permute-start.18
  48.9 0.0 collective-permute-done.8
  49.0 0.0 collective-permute-done.11
  49.1 0.3 collective-permute-done.12
  49.5 0.2 collective-permute-done.17
  49.8 0.3 collective-permute-done.18
  50.2 0.0 copy-done
  50.2 0.0 copy-done.1
  50.2 0.0 copy-done.2
  50.2 2.5 %downward.1 = bf16[64,32,128]{2,1,0:T(8,128)(2,1)} custom-call(s32[8,32]{1,0:T(8,128)S(1)} %get-tuple-element.14.place_hbm, bf16[1024,16,128]{2,1,0:T(8,128)(2,1)S(1)} %constant_dynamic-update-slice_fusion.4.table, bf16[32,64,512]{2,1,0:T(8,128)(2,1)S(1)} %copy-done.2, bf16[32,64,128]{2,1,0:T(8,128)(2,1)S(1)} %copy-done.1, bf16[64,64,128]{2,1,0:T(8,128)(2,1)S(1)} %copy-done, ...), custom_call_target="tpu_custom_call" | custom-call | tf_op jit(solution)/shard_map/downward/pallas_call | solution.py:347
  (24 shorter events, 0.7 us)
Async XLA Ops:
  2.7 16.9 %collective-permute-start = (bf16[32,16,128]{2,1,0:T(8,128)(2,1)S(1)}, bf16[32,16,128]{2,1,0:T(8,128)(2,1)S(1)}, u32[]{:S(2)}, u32[]{:S(2)}) collective-permute-start(bf16[32,16,128]{2,1,0:T(8,128)(2,1)S(1)} %get-tuple-element.15), channel_id=1, source_target_pairs={{0,1},{1,0},{2,3},{3,2},{4,5},{5,4},{6,7},{7,6},{8,9},{9,8},{10,11... | collective-permute-start | bytes 393224 | tf_op jit(solution)/shard_map/ppermute | solution.py:385
  5.8 16.1 %collective-permute-start.1 = (bf16[32,16,128]{2,1,0:T(8,128)(2,1)S(1)}, bf16[32,16,128]{2,1,0:T(8,128)(2,1)S(1)}, u32[]{:S(2)}, u32[]{:S(2)}) collective-permute-start(bf16[32,16,128]{2,1,0:T(8,128)(2,1)S(1)} %get-tuple-element.15), channel_id=1, source_target_pairs={{0,2},{1,3},{2,0},{3,1},{4,6},{5,7},{6,4},{7,5},{8,10},{9,11},{10,... | collective-permute-start | bytes 393224 | tf_op jit(solution)/shard_map/ppermute | solution.py:385
  8.4 15.1 %collective-permute-start.2 = (bf16[32,16,128]{2,1,0:T(8,128)(2,1)S(1)}, bf16[32,16,128]{2,1,0:T(8,128)(2,1)S(1)}, u32[]{:S(2)}, u32[]{:S(2)}) collective-permute-start(bf16[32,16,128]{2,1,0:T(8,128)(2,1)S(1)} %get-tuple-element.15), channel_id=1, source_target_pairs={{0,3},{1,2},{2,1},{3,0},{4,7},{5,6},{6,5},{7,4},{8,11},{9,10},{10,... | collective-permute-start | bytes 393224 | tf_op jit(solution)/shard_map/ppermute | solution.py:385
  8.4 9.9 %collective-permute-start.20 = (bf16[9,16,128]{2,1,0:T(8,128)(2,1)S(1)}, bf16[9,16,128]{2,1,0:T(8,128)(2,1)S(1)}, u32[]{:S(2)}, u32[]{:S(2)}) collective-permute-start(bf16[9,16,128]{2,1,0:T(8,128)(2,1)S(1)} %get-tuple-element.20), channel_id=1, source_target_pairs={{0,3},{1,2},{2,1},{3,0},{4,7},{5,6},{6,5},{7,4},{8,11},{9,10},{10,... | collective-permute-start | bytes 110600 | tf_op jit(solution)/shard_map/ppermute | solution.py:385
  12.2 11.9 %collective-permute-start.19 = (bf16[9,16,128]{2,1,0:T(8,128)(2,1)S(1)}, bf16[9,16,128]{2,1,0:T(8,128)(2,1)S(1)}, u32[]{:S(2)}, u32[]{:S(2)}) collective-permute-start(bf16[9,16,128]{2,1,0:T(8,128)(2,1)S(1)} %get-tuple-element.19), channel_id=1, source_target_pairs={{0,1},{1,0},{2,3},{3,2},{4,5},{5,4},{6,7},{7,6},{8,9},{9,8},{10,11... | collective-permute-start | bytes 110600 | tf_op jit(solution)/shard_map/ppermute | solution.py:385
  18.4 5.9 %collective-permute-start.21 = (bf16[9,16,128]{2,1,0:T(8,128)(2,1)S(1)}, bf16[9,16,128]{2,1,0:T(8,128)(2,1)S(1)}, u32[]{:S(2)}, u32[]{:S(2)}) collective-permute-start(bf16[9,16,128]{2,1,0:T(8,128)(2,1)S(1)} %collective-permute-done.20.refs_1_), channel_id=1, source_target_pairs={{0,4},{4,8},{8,12},{12,16},{16,20},{20,24},{24,28},{7,3},{11,7},{1... | collective-permute-start | bytes 110600 | tf_op jit(solution)/shard_map/ppermute | solution.py:385
  19.7 19.9 %collective-permute-start.5 = (bf16[64,16,128]{2,1,0:T(8,128)(2,1)S(1)}, bf16[64,16,128]{2,1,0:T(8,128)(2,1)S(1)}, u32[]{:S(2)}, u32[]{:S(2)}) collective-permute-start(bf16[64,16,128]{2,1,0:T(8,128)(2,1)S(1)} %get-tuple-element.27), channel_id=1, source_target_pairs={{0,8},{1,9},{2,10},{3,11},{4,12},{5,13},{6,14},{7,15},{8,0},{9,1},... | collective-permute-start | bytes 786440 | tf_op jit(solution)/shard_map/ppermute | solution.py:385
  21.9 8.8 %collective-permute-start.9 = (bf16[64,16,128]{2,1,0:T(8,128)(2,1)S(1)}, bf16[64,16,128]{2,1,0:T(8,128)(2,1)S(1)}, u32[]{:S(2)}, u32[]{:S(2)}) collective-permute-start(bf16[64,16,128]{2,1,0:T(8,128)(2,1)S(1)} %get-tuple-element.27), channel_id=1, source_target_pairs={{0,16},{1,17},{2,18},{3,19},{4,20},{5,21},{6,22},{7,23},{8,24},{9,... | collective-permute-start | bytes 786440 | tf_op jit(solution)/shard_map/ppermute | solution.py:385
  23.5 16.7 %collective-permute-start.10 = (bf16[64,16,128]{2,1,0:T(8,128)(2,1)S(1)}, bf16[64,16,128]{2,1,0:T(8,128)(2,1)S(1)}, u32[]{:S(2)}, u32[]{:S(2)}) collective-permute-start(bf16[64,16,128]{2,1,0:T(8,128)(2,1)S(1)} %get-tuple-element.23), channel_id=1, source_target_pairs={{0,16},{1,17},{2,18},{3,19},{4,20},{5,21},{6,22},{7,23},{8,24},{9,... | collective-permute-start | bytes 786440 | tf_op jit(solution)/shard_map/ppermute | solution.py:385
  24.1 17.7 %collective-permute-start.6 = (bf16[64,16,128]{2,1,0:T(8,128)(2,1)S(1)}, bf16[64,16,128]{2,1,0:T(8,128)(2,1)S(1)}, u32[]{:S(2)}, u32[]{:S(2)}) collective-permute-start(bf16[64,16,128]{2,1,0:T(8,128)(2,1)S(1)} %get-tuple-element.23), channel_id=1, source_target_pairs={{0,8},{1,9},{2,10},{3,11},{4,12},{5,13},{6,14},{7,15},{8,0},{9,1},... | collective-permute-start | bytes 786440 | tf_op jit(solution)/shard_map/ppermute | solution.py:385
  24.2 18.7 %collective-permute-start.3 = (bf16[64,16,128]{2,1,0:T(8,128)(2,1)S(1)}, bf16[64,16,128]{2,1,0:T(8,128)(2,1)S(1)}, u32[]{:S(2)}, u32[]{:S(2)}) collective-permute-start(bf16[64,16,128]{2,1,0:T(8,128)(2,1)S(1)} %get-tuple-element.27), channel_id=1, source_target_pairs={{0,4},{1,5},{2,6},{3,7},{4,0},{5,1},{6,2},{7,3},{8,12},{9,13},{10,... | collective-permute-start | bytes 786440 | tf_op jit(solution)/shard_map/ppermute | solution.py:385
  30.7 13.3 %collective-permute-start.4 = (bf16[64,16,128]{2,1,0:T(8,128)(2,1)S(1)}, bf16[64,16,128]{2,1,0:T(8,128)(2,1)S(1)}, u32[]{:S(2)}, u32[]{:S(2)}) collective-permute-start(bf16[64,16,128]{2,1,0:T(8,128)(2,1)S(1)} %get-tuple-element.23), channel_id=1, source_target_pairs={{0,4},{1,5},{2,6},{3,7},{4,0},{5,1},{6,2},{7,3},{8,12},{9,13},{10,... | collective-permute-start | bytes 786440 | tf_op jit(solution)/shard_map/ppermute | solution.py:385
  39.6 6.4 %collective-permute-start.13 = (bf16[32,16,128]{2,1,0:T(8,128)(2,1)S(1)}, bf16[32,16,128]{2,1,0:T(8,128)(2,1)S(1)}, u32[]{:S(2)}, u32[]{:S(2)}) collective-permute-start(bf16[32,16,128]{2,1,0:T(8,128)(2,1)S(1)} %slice.16), channel_id=1, source_target_pairs={{0,8},{1,9},{2,10},{3,11},{4,12},{5,13},{6,14},{7,15},{8,0},{9,1},... | collective-permute-start | bytes 393224 | tf_op jit(solution)/shard_map/ppermute | solution.py:385
  40.2 5.8 %collective-permute-start.14 = (bf16[32,16,128]{2,1,0:T(8,128)(2,1)S(1)}, bf16[32,16,128]{2,1,0:T(8,128)(2,1)S(1)}, u32[]{:S(2)}, u32[]{:S(2)}) collective-permute-start(bf16[32,16,128]{2,1,0:T(8,128)(2,1)S(1)} %slice.17), channel_id=1, source_target_pairs={{0,16},{1,17},{2,18},{3,19},{4,20},{5,21},{6,22},{7,23},{8,24},{9,... | collective-permute-start | bytes 393224 | tf_op jit(solution)/shard_map/ppermute | solution.py:385
  41.8 6.0 %collective-permute-start.15 = (bf16[32,16,128]{2,1,0:T(8,128)(2,1)S(1)}, bf16[32,16,128]{2,1,0:T(8,128)(2,1)S(1)}, u32[]{:S(2)}, u32[]{:S(2)}) collective-permute-start(bf16[32,16,128]{2,1,0:T(8,128)(2,1)S(1)} %slice.18), channel_id=1, source_target_pairs={{0,8},{1,9},{2,10},{3,11},{4,12},{5,13},{6,14},{7,15},{8,0},{9,1},... | collective-permute-start | bytes 393224 | tf_op jit(solution)/shard_map/ppermute | solution.py:385
  42.9 5.3 %collective-permute-start.16 = (bf16[32,16,128]{2,1,0:T(8,128)(2,1)S(1)}, bf16[32,16,128]{2,1,0:T(8,128)(2,1)S(1)}, u32[]{:S(2)}, u32[]{:S(2)}) collective-permute-start(bf16[32,16,128]{2,1,0:T(8,128)(2,1)S(1)} %slice.19), channel_id=1, source_target_pairs={{0,16},{1,17},{2,18},{3,19},{4,20},{5,21},{6,22},{7,23},{8,24},{9,... | collective-permute-start | bytes 393224 | tf_op jit(solution)/shard_map/ppermute | solution.py:385
  44.0 6.2 %copy-start = (bf16[64,64,128]{2,1,0:T(8,128)(2,1)S(1)}, bf16[64,64,128]{2,1,0:T(8,128)(2,1)}, u32[]{:S(2)}) copy-start(bf16[64,64,128]{2,1,0:T(8,128)(2,1)} %basis_ref.1) | copy-start | bytes 3145732
  44.0 6.2 %copy-start.1 = (bf16[32,64,128]{2,1,0:T(8,128)(2,1)S(1)}, bf16[32,64,128]{2,1,0:T(8,128)(2,1)}, u32[]{:S(2)}) copy-start(bf16[32,64,128]{2,1,0:T(8,128)(2,1)} %trans_ref.1) | copy-start | bytes 1572868
  44.0 6.2 %copy-start.2 = (bf16[32,64,512]{2,1,0:T(8,128)(2,1)S(1)}, bf16[32,64,512]{2,1,0:T(8,128)(2,1)}, u32[]{:S(2)}) copy-start(bf16[32,64,512]{2,1,0:T(8,128)(2,1)} %coup_ref.1) | copy-start | bytes 6291460
  44.0 4.4 %collective-permute-start.7 = (bf16[64,16,128]{2,1,0:T(8,128)(2,1)S(1)}, bf16[64,16,128]{2,1,0:T(8,128)(2,1)S(1)}, u32[]{:S(2)}, u32[]{:S(2)}) collective-permute-start(bf16[64,16,128]{2,1,0:T(8,128)(2,1)S(1)} %collective-permute-done.5), channel_id=1, source_target_pairs={{0,4},{1,5},{2,6},{3,7},{4,0},{5,1},{6,2},{7,3},{8,12},{9,13},{10,... | collective-permute-start | bytes 786440 | tf_op jit(solution)/shard_map/ppermute | solution.py:385
  46.0 2.8 %collective-permute-start.8 = (bf16[64,16,128]{2,1,0:T(8,128)(2,1)S(1)}, bf16[64,16,128]{2,1,0:T(8,128)(2,1)S(1)}, u32[]{:S(2)}, u32[]{:S(2)}) collective-permute-start(bf16[64,16,128]{2,1,0:T(8,128)(2,1)S(1)} %collective-permute-done.6), channel_id=1, source_target_pairs={{0,4},{1,5},{2,6},{3,7},{4,0},{5,1},{6,2},{7,3},{8,12},{9,13},{10,... | collective-permute-start | bytes 786440 | tf_op jit(solution)/shard_map/ppermute | solution.py:385
  46.0 3.0 %collective-permute-start.11 = (bf16[64,16,128]{2,1,0:T(8,128)(2,1)S(1)}, bf16[64,16,128]{2,1,0:T(8,128)(2,1)S(1)}, u32[]{:S(2)}, u32[]{:S(2)}) collective-permute-start(bf16[64,16,128]{2,1,0:T(8,128)(2,1)S(1)} %collective-permute-done.9), channel_id=1, source_target_pairs={{0,4},{1,5},{2,6},{3,7},{4,0},{5,1},{6,2},{7,3},{8,12},{9,13},{10,... | collective-permute-start | bytes 786440 | tf_op jit(solution)/shard_map/ppermute | solution.py:385
  47.9 1.5 %collective-permute-start.12 = (bf16[64,16,128]{2,1,0:T(8,128)(2,1)S(1)}, bf16[64,16,128]{2,1,0:T(8,128)(2,1)S(1)}, u32[]{:S(2)}, u32[]{:S(2)}) collective-permute-start(bf16[64,16,128]{2,1,0:T(8,128)(2,1)S(1)} %collective-permute-done.10), channel_id=1, source_target_pairs={{0,4},{1,5},{2,6},{3,7},{4,0},{5,1},{6,2},{7,3},{8,12},{9,13},{10,... | collective-permute-start | bytes 786440 | tf_op jit(solution)/shard_map/ppermute | solution.py:385
  48.2 1.6 %collective-permute-start.17 = (bf16[64,16,128]{2,1,0:T(8,128)(2,1)S(1)}, bf16[64,16,128]{2,1,0:T(8,128)(2,1)S(1)}, u32[]{:S(2)}, u32[]{:S(2)}) collective-permute-start(bf16[64,16,128]{2,1,0:T(8,128)(2,1)S(1)} %pad_maximum_fusion), channel_id=1, source_target_pairs={{0,4},{1,5},{2,6},{3,7},{4,0},{5,1},{6,2},{7,3},{8,12},{9,13},{10,... | collective-permute-start | bytes 786440 | tf_op jit(solution)/shard_map/ppermute | solution.py:385
  48.4 1.7 %collective-permute-start.18 = (bf16[64,16,128]{2,1,0:T(8,128)(2,1)S(1)}, bf16[64,16,128]{2,1,0:T(8,128)(2,1)S(1)}, u32[]{:S(2)}, u32[]{:S(2)}) collective-permute-start(bf16[64,16,128]{2,1,0:T(8,128)(2,1)S(1)} %pad_maximum_fusion.1), channel_id=1, source_target_pairs={{0,4},{1,5},{2,6},{3,7},{4,0},{5,1},{6,2},{7,3},{8,12},{9,13},{10,... | collective-permute-start | bytes 786440 | tf_op jit(solution)/shard_map/ppermute | solution.py:385
